TPU v7x, 512 devices: a 4x2x32 block of a 4x8x32 slice. The times are simulated.
512 devices in a mesh: grp: 2 (over y), tm: 32 (over z), chan: 4 (over x), sub: 2 (over core).
Axes of the slice: x: 4, y: 2, z: 32, core: 2. Of those that a mesh axis runs over, the one named last changes fastest.
The devices are a block of a 4x8x32 slice.
Arguments:
- signal: float32 [128, 1048576], P(('grp', 'chan', 'sub'), 'tm'), parts along dimension 0, may hold values from -24 to 24
- gap_mask: int32 [128, 64], P(('grp', 'chan', 'sub'), 'tm'), parts along dimension 0, may hold values from 0 to 1, as said below
- assignment: int32 [128], P(('grp', 'chan', 'sub')), parts along dimension 0, may hold values from 0 to 7, as said below
Outputs:
- peak_hold: float32 [128, 16384], P(('grp', 'chan', 'sub'), 'tm'), parts along dimension 0
- log_mean: float32 [128, 16384], P(('grp', 'chan', 'sub'), 'tm'), parts along dimension 0
- block_mean: float32 [16, 16384], P('grp', 'tm'), parts along dimension 0
There are 2 independent parts, one for each index of `grp`. A program takes and returns all parts, laid end to end along the dimension named above; each array names one. Nothing has to cross between parts.
Inputs may be any that keep to these rules, and one draw needn't show every extreme that they name: `gap_mask`: every channel keeps at least one of its 64 segments. `assignment`: every block holds at least one channel.
All inputs are finite; a program needn't handle non-finite values.
Results may differ from a plain program's by a relative error of at most 0.000086.
Values sent between devices are 32-bit elements; how exact they have to be, the bound alone decides.
No kernel may reach another device: no remote copies, remote signals or barrier semaphores. Data moves between devices by JAX's collectives and lax.ppermute only.
A program may use at most 128 MiB of HBM per device.

v0:
```python
import math

import jax
import jax.numpy as jnp
from jax import lax
from jax.sharding import PartitionSpec as P

LA = 256
LB = 128
BLOCKS = 8


def from_behind(x, axis, by):
    count = lax.axis_size(axis)
    pairs = [(i, i + by) for i in range(count) if 0 <= i + by < count]
    return lax.ppermute(x, axis, pairs)


def side_by_side(arrays, axis, split_dim, concat_dim, along):
    ends, at = ([], 0)
    for a in arrays[:-1]:
        at += a.shape[along]
        ends.append(at)
    both = jnp.concatenate(arrays, axis=along)
    return tuple(
        jnp.split(
            lax.all_to_all(both, axis, split_axis=split_dim, concat_axis=concat_dim, tiled=True),
            ends,
            axis=along,
        )
    )


def sent_to_all(x, axis):
    count = lax.axis_size(axis)
    return lax.all_to_all(jnp.broadcast_to(x[None], (count, *x.shape)), axis, 0, 0, tiled=True)


def taken_together(x, axis):
    return sent_to_all(x, axis).sum(axis=0)


def together(arrays, axis):
    ends = [0]
    for a in arrays:
        ends.append(ends[-1] + a.size)
    running = taken_together(jnp.concatenate([a.ravel() for a in arrays]), axis)
    return tuple((running[b:e].reshape(a.shape) for a, b, e in zip(arrays, ends, ends[1:])))


def rotations(height, columns, modulus):
    products = (
        jnp.arange(height, dtype=jnp.int32)[:, None]
        * jnp.arange(columns, dtype=jnp.int32)[None, :]
        % modulus
    )
    angles = products.astype(jnp.float32) * (2.0 * math.pi / modulus)
    return (jnp.cos(angles), -jnp.sin(angles))


def on_device(signal, gap_mask, assignment):
    channels, local_time = signal.shape
    seg_local = gap_mask.shape[1]
    half = local_time // seg_local
    seg_length = LA * LB
    highest = lax.Precision.HIGHEST
    borrowed = from_behind(signal[:, :half], "tm", -1)
    extended = jnp.concatenate([signal, borrowed], axis=1)
    hop_rows = extended.reshape(channels, seg_local + 1, half)
    section_one = rotations(LB, LB, LB)
    twiddle = rotations(LB, LA, seg_length)
    section_two = rotations(LA, LA // 2, LA)
    samples = jnp.arange(seg_length, dtype=jnp.float32)
    window = (0.5 - 0.5 * jnp.cos(samples * (2.0 * math.pi / seg_length))).reshape(LB, LA)
    norm_scale = 1.0 / (0.375 * seg_length)

    def one_channel(inputs):
        rows_here, keep_flags = inputs
        segments = jnp.concatenate([rows_here[:-1], rows_here[1:]], axis=-1)
        frames = segments.reshape(seg_local, LB, LA) * window
        real_one = jnp.einsum("kb,sba->ska", section_one[0], frames, precision=highest)
        imag_one = jnp.einsum("kb,sba->ska", section_one[1], frames, precision=highest)
        real_mid = real_one * twiddle[0] - imag_one * twiddle[1]
        imag_mid = real_one * twiddle[1] + imag_one * twiddle[0]
        real_two = jnp.einsum(
            "ska,aj->skj", real_mid, section_two[0], precision=highest
        ) - jnp.einsum("ska,aj->skj", imag_mid, section_two[1], precision=highest)
        imag_two = jnp.einsum(
            "ska,aj->skj", real_mid, section_two[1], precision=highest
        ) + jnp.einsum("ska,aj->skj", imag_mid, section_two[0], precision=highest)
        powers = (real_two * real_two + imag_two * imag_two) * norm_scale
        powers = jnp.swapaxes(powers, 1, 2).reshape(seg_local, -1)
        weights = keep_flags.astype(jnp.float32)
        peak_local = jnp.max(powers * weights[:, None], axis=0)
        log_terms = jnp.sum(weights[:, None] * jnp.log(0.25 + powers), axis=0)
        return (peak_local, log_terms)

    peak_local, log_terms = lax.map(one_channel, (hop_rows, gap_mask))
    kept_local = jnp.sum(gap_mask.astype(jnp.float32), axis=1)
    time_devices = lax.axis_size("tm")
    count_terms = jnp.broadcast_to(kept_local[:, None], (channels, time_devices))
    peak_parts, log_parts, count_parts = (
        *side_by_side((peak_local[:, None, :], log_terms[:, None, :]), "tm", 2, 1, 0),
        lax.all_to_all(count_terms[:, None, :], "tm", split_axis=2, concat_axis=1, tiled=True),
    )
    peak_hold = jnp.max(peak_parts, axis=1)
    log_sum = jnp.sum(log_parts, axis=1)
    kept_total = jnp.sum(count_parts, axis=1)
    log_mean = log_sum / kept_total
    onehot = (assignment[None, :] == jnp.arange(BLOCKS, dtype=jnp.int32)[:, None]).astype(
        jnp.float32
    )
    block_part = jnp.dot(onehot, log_mean, precision=highest)
    block_total, block_counts = together((block_part, jnp.sum(onehot, axis=1)), ("chan", "sub"))
    block_mean = block_total / block_counts[:, None]
    return (peak_hold, log_mean, block_mean)


def solution(mesh):
    in_specs = (
        P(("grp", "chan", "sub"), "tm"),
        P(("grp", "chan", "sub"), "tm"),
        P(("grp", "chan", "sub")),
    )
    out_specs = (P(("grp", "chan", "sub"), "tm"), P(("grp", "chan", "sub"), "tm"), P("grp", "tm"))
    return jax.shard_map(
        on_device, mesh=mesh, in_specs=in_specs, out_specs=out_specs, check_vma=False
    )
```

profile of v0, /device:TPU:33, one launch (start us, length us, event | category | flops | bytes accessed | tf_op | source)
XLA Modules:
  0.0 407.4 jit_solution(17776370923741288129)
XLA Ops:
  0.6 1.1 slice.20
  1.7 1.3 collective-permute-start
  4.3 46.8 %all-to-all-start.1 = ((f32[8,1,32]{0,1,2:T(1,128)}), f32[8,1,32]{0,1,2:T(1,128)S(1)}, u32[]{:S(2)}, u32[]{:S(2)}) async-start(f32[8,1,32]{0,1,2:T(1,128)} %broadcast_in_dim_broadcast_in_dim.2), calls=%async_computation.1 | async-start | bytes 32768 | tf_op jit(solution)/shard_map/all_to_all | solution.py:104
  52.0 1.3 pad_maximum_fusion
  53.3 2.5 reshape.65
  55.8 72.9 %while.14 = (s32[]{:T(128)}, f32[8,16384]{1,0:T(8,128)S(1)}, f32[8,16384]{1,0:T(8,128)S(1)}, f32[8,3,16384]{2,1,0:T(4,128)}, s32[8,2]{1,0:T(8,128)S(1)}, /*index=5*/s32[]{:T(128)}, s32[]{:T(128)}, s32[]{}) while((s32[]{:T(128)}, f32[8,16384]{1,0:T(8,128)S(1)}, f32[8,16384]{1,0:T(8,128)S(1)}, f32[8,3,16384]{2,1,0:T(4,128)}, ...), condition=%wide.region_3.4_spmd.clone.clone, body=%wide.region_0.3_spmd.clone.clone.sunk | while | flops 608321536 | bytes 8388765 | solution.py:98
  55.8 1.1 constant_dynamic-slice_fusion.4
  62.7 1.0 multiply_reduce_fusion.3
  64.9 1.2 constant_dynamic-slice_fusion.4
  71.8 1.0 multiply_reduce_fusion.3
  74.0 1.2 constant_dynamic-slice_fusion.4
  80.9 1.0 multiply_reduce_fusion.3
  83.2 1.2 constant_dynamic-slice_fusion.4
  90.1 1.0 multiply_reduce_fusion.3
  92.3 1.2 constant_dynamic-slice_fusion.4
  99.2 1.0 multiply_reduce_fusion.3
  101.4 1.2 constant_dynamic-slice_fusion.4
  108.3 1.0 multiply_reduce_fusion.3
  110.5 1.2 constant_dynamic-slice_fusion.4
  117.4 1.0 multiply_reduce_fusion.3
  119.6 1.2 constant_dynamic-slice_fusion.4
  128.8 12.2 %copy.79 = f32[16,1,16384]{0,1,2:T(1,128)} copy(f32[16,1,16384]{2,0,1:T(8,128)S(1)} %pad_maximum_fusion.1) | data formatting | bytes 2097152 | tf_op jit(solution)/shard_map/concatenate | solution.py:24
  141.5 74.6 %reduce.12 = f32[16384,16]{1,0:T(8,128)} reduce(f32[16384,1,16]{2,1,0:T(1,128)} %bitcast.82, f32[]{:T(128)} %broadcast.130), dimensions={1}, to_apply=%bitcast.41.reduce_sub_computation | reduce | bytes 2097156
  216.2 6.9 %reshape.72 = f32[32,1,8192]{2,1,0:T(1,128)} reshape(f32[16384,16]{1,0:T(8,128)} %reduce.12) | data formatting | bytes 2097152
  223.1 21.5 %all-to-all-start = ((f32[32,1,8192]{2,1,0:T(1,128)}), f32[32,1,8192]{2,1,0:T(1,128)S(1)}, u32[]{:S(2)}, u32[]{:S(2)}) async-start(f32[32,1,8192]{2,1,0:T(1,128)} %reshape.72), calls=%async_computation | async-start | bytes 2097152 | tf_op jit(solution)/shard_map/all_to_all | solution.py:27
  244.7 104.5 %all-to-all-done = f32[32,1,8192]{2,1,0:T(1,128)S(1)} async-done(((f32[32,1,8192]{2,1,0:T(1,128)}), f32[32,1,8192]{2,1,0:T(1,128)S(1)}, u32[]{:S(2)}, u32[]{:S(2)}) %all-to-all-start) | async-done | bytes 1048608 | tf_op jit(solution)/shard_map/all_to_all | solution.py:27
  349.2 3.2 reduce.13
  352.4 17.2 %reshape.73 = f32[16384,1,16]{2,1,0:T(1,128)} reshape(f32[32,8192]{1,0:T(8,128)S(1)} %reduce.13) | data formatting | bytes 2097152
  369.7 21.0 %fusion.84 = (f32[8,1,16384]{0,1,2:T(1,128)}, f32[8,1,16384]{0,1,2:T(1,128)}) fusion(f32[16,1,16384]{0,1,2:T(1,128)} %bitcast.81), kind=kLoop, calls=%fused_computation.106 | loop fusion | bytes 2097152 | tf_op jit(solution)/shard_map/split | solution.py:26
  390.7 4.0 reduce_sum.54
  395.8 5.3 %all-to-all-start.2 = ((f32[8,1,4104]{2,1,0:T(1,128)}), f32[8,1,4104]{2,1,0:T(1,128)S(1)}, u32[]{:S(2)}, u32[]{:S(2)}) async-start(f32[8,1,4104]{2,1,0:T(1,128)} %broadcast_in_dim.21), calls=%async_computation.2 | async-start | bytes 270336 | tf_op jit(solution)/shard_map/all_to_all | solution.py:36
  401.8 4.0 reduce_max.20
  (171 shorter events, 61.6 us)
Async XLA Ops:
  1.7 50.2 %collective-permute-start = (f32[8,16384]{1,0:T(8,128)S(1)}, f32[8,16384]{1,0:T(8,128)S(1)}, u32[]{:S(2)}, u32[]{:S(2)}) collective-permute-start(f32[8,16384]{1,0:T(8,128)S(1)} %slice.20), channel_id=1, source_target_pairs={{8,0},{16,8},{24,16},{32,24},{40,32},{48,40},{56,48},{64,56},{72,6... | collective-permute-start | bytes 1572872 | tf_op jit(solution)/shard_map/ppermute | solution.py:16
  4.3 218.7 %all-to-all-start.1 = ((f32[8,1,32]{0,1,2:T(1,128)}), f32[8,1,32]{0,1,2:T(1,128)S(1)}, u32[]{:S(2)}, u32[]{:S(2)}) async-start(f32[8,1,32]{0,1,2:T(1,128)} %broadcast_in_dim_broadcast_in_dim.2), calls=%async_computation.1 | async-start | bytes 32768 | tf_op jit(solution)/shard_map/all_to_all | solution.py:104
  216.2 28.4 %copy-start = (s32[8]{0:T(128)S(1)}, s32[8]{0:T(128)}, u32[]{:S(2)}) copy-start(s32[8]{0:T(128)} %param.7) | copy-start | bytes 100
  223.1 126.1 %all-to-all-start = ((f32[32,1,8192]{2,1,0:T(1,128)}), f32[32,1,8192]{2,1,0:T(1,128)S(1)}, u32[]{:S(2)}, u32[]{:S(2)}) async-start(f32[32,1,8192]{2,1,0:T(1,128)} %reshape.72), calls=%async_computation | async-start | bytes 2097152 | tf_op jit(solution)/shard_map/all_to_all | solution.py:27
  395.8 10.8 %all-to-all-start.2 = ((f32[8,1,4104]{2,1,0:T(1,128)}), f32[8,1,4104]{2,1,0:T(1,128)S(1)}, u32[]{:S(2)}, u32[]{:S(2)}) async-start(f32[8,1,4104]{2,1,0:T(1,128)} %broadcast_in_dim.21), calls=%async_computation.2 | async-start | bytes 270336 | tf_op jit(solution)/shard_map/all_to_all | solution.py:36
where the time goes:
time: 408 us; the launch traced here: 407 us
  waiting for transfers between devices  104 us (25%)
  other arithmetic  97.2 us (24%)
  local copies, waits for them, and re-layouts  86.7 us (21%)
  starting transfers between devices  74.9 us (18%)
  matrix products  42.2 us (10%)
    all_to_all x1, waiting for transfers between devices, side_by_side(): lax.all_to_all(both, axis, split_axis=split_dim, concat_axis=concat_dim,...  104 us
    unnamed x1, other arithmetic  74.6 us
    all_to_all x1, starting transfers between devices, on_device(): lax.all_to_all(count_terms[:, None, :], 'tm', split_axis=2, concat_axis=1...  46.8 us
    unnamed x9, local copies, waits for them, and re-layouts  26.9 us
    all_to_all x1, starting transfers between devices, side_by_side(): lax.all_to_all(both, axis, split_axis=split_dim, concat_axis=concat_dim,...  21.5 us
    split x1, local copies, waits for them, and re-layouts, side_by_side(): jnp.split(lax.all_to_all(both, axis, split_axis=split_dim, concat_axis=co...  21 us
    concatenate x1, local copies, waits for them, and re-layouts, side_by_side(): both = jnp.concatenate(arrays, axis=along)  12.2 us
    slice x8, local copies, waits for them, and re-layouts, one_channel(): segments = jnp.concatenate([rows_here[:-1], rows_here[1:]], axis=-1)  9.2 us
  transfers between devices with their start and end apart: 4, of which 1 were waited for; matrix products, arithmetic and copies ran while one was open for 44% of the time, Pallas kernels for 0%

commit v1 on v0

v1 whole, which is shorter than its diff:
```python
import functools
import math

import jax
import jax.numpy as jnp
import numpy as np
from jax import lax
from jax.experimental import pallas as pl
from jax.experimental.pallas import tpu as pltpu
from jax.sharding import PartitionSpec as P

LA = 256
LB = 128
BLOCKS = 8
SEG = LA * LB
GROUP = 4
ROWS = 144
LANES = 128


def split(x):
    high = x.astype(jnp.bfloat16)
    return high, (x - high.astype(jnp.float32)).astype(jnp.bfloat16)


def split_np(x):
    high = x.astype(np.float32).astype(jnp.bfloat16)
    low = (x - high.astype(np.float64)).astype(np.float32).astype(jnp.bfloat16)
    return high, low


@functools.lru_cache
def tables(shards):
    k1 = np.arange(ROWS)[:, None]
    angle = 2 * math.pi * ((k1 * np.arange(LA)[None, :]) % LA) / LA
    live = k1 <= LA // 2
    first = np.concatenate([np.cos(angle) * live, -np.sin(angle) * live], axis=0)
    high, low = split_np(first)
    first = np.concatenate([high, high, low], axis=1)
    angle = 2 * math.pi * (k1 * np.arange(LB)[None, :]) / SEG
    scale = math.sqrt(1.0 / (0.375 * SEG)) * live
    twiddle = np.stack([np.cos(angle) * scale, -np.sin(angle) * scale]).astype(np.float32)
    own = LB // 2 // shards
    d = np.arange(shards)
    k2 = [own * d + e for e in range(own)] + [LB - 1 - own * d - e for e in range(own)]
    k2 = np.concatenate(k2)[None, :]
    angle = 2 * math.pi * ((np.arange(LB)[:, None] * k2) % LB) / LB
    c, s = np.cos(angle), -np.sin(angle)
    second = np.concatenate([np.concatenate([c, s], 1), np.concatenate([-s, c], 1)], 0)
    high, low = split_np(second)
    second = np.concatenate([high, high, low], axis=0)
    n = np.arange(SEG)
    window = (0.5 - 0.5 * np.cos(2 * math.pi * n / SEG)).reshape(LA, LB).astype(np.float32)
    return first, second, twiddle, window


def pack_kernel(per, mask_ref, x_ref, o_ref, a_ref, b_ref, c_ref, h_ref, cnt_ref):
    me = lax.axis_index("tm")
    channels = GROUP * per
    rows = x_ref.shape[0] // channels
    half = rows // 2
    even = lax.rem(me, 2) == 0

    def masks(ref, at, first):
        ref[at : at + 8, :] = jnp.zeros((8, LANES), jnp.float32)
        for c in range(per):
            for s in range(2):
                value = mask_ref[first + c, s].astype(jnp.float32)
                ref[at + 2 * c + s : at + 2 * c + s + 1, :] = jnp.full((1, LANES), value)

    for ref, shift in ((a_ref, 1), (b_ref, GROUP - 1), (c_ref, 2), (o_ref, 0)):
        first = per * lax.rem(me + shift, GROUP)
        for c in range(per):
            ref[c * rows : (c + 1) * rows, :] = x_ref[pl.ds(first + c, rows, stride=channels), :]
        masks(ref, per * rows, first)
    first = per * lax.rem(me + jnp.where(even, GROUP - 1, 1), GROUP)
    start = jnp.where(even, half * channels, 0)
    for c in range(per):
        h_ref[c * half : (c + 1) * half, :] = x_ref[
            pl.ds(start + first + c, half, stride=channels), :
        ]
    masks(h_ref, per * half, first)
    lane = lax.broadcasted_iota(jnp.int32, (1, LANES), 1)
    kept = jnp.zeros((1, LANES), jnp.float32)
    for c in range(channels):
        total = (mask_ref[c, 0] + mask_ref[c, 1]).astype(jnp.float32)
        kept = jnp.where(lane == c, total, kept)
    for d in range(cnt_ref.shape[0]):
        cnt_ref[d] = kept


def spectra_kernel(
    per, shards, o_ref, a_ref, b_ref, c_ref, h_ref, f_ref, w_ref, tw_ref, win_ref, out_ref
):
    me = lax.axis_index("tm")
    even = lax.rem(me, 2) == 0
    rows = (o_ref.shape[0] - 8) // per
    half = rows // 2
    parts = 2 * (LB // 2 // shards)
    lines = 2 * parts * per
    c_index = lax.rem(me + jnp.where(even, 2, shards - 2), shards)
    after_o = jnp.where(me == shards - 1, 0.0, 1.0)
    before_o = jnp.where(me == 0, 0.0, 1.0)
    before_c = jnp.where(c_index == 0, 0.0, 1.0)
    y_index = lax.rem(me + jnp.where(even, 3, shards - 1), shards)
    before_y = jnp.where(y_index == 0, 0.0, 1.0)
    swap = (lax.broadcasted_iota(jnp.int32, (8, LANES), 0) == 0) & (
        lax.broadcasted_iota(jnp.int32, (8, LANES), 1) >= LB // 2
    )

    def one_channel(c, carry):
        base = pl.multiple_of(c * rows, rows)
        h_base = pl.multiple_of(c * half, half)

        def halves(ref):
            return ref[pl.ds(base, half), :], ref[pl.ds(base + half, half), :]

        def weight(ref, s, at):
            return ref[pl.ds(at + 2 * c + s, 1), :]

        mask_at, h_mask_at = per * rows, per * half
        o0, o1 = halves(o_ref)
        a0, a1 = halves(a_ref)
        b0, b1 = halves(b_ref)
        c0, c1 = halves(c_ref)
        h = h_ref[pl.ds(h_base, half), :]
        x1 = jnp.where(even, b1, h)
        y = jnp.where(even, h, a0)
        x_weight = jnp.where(even, weight(b_ref, 1, mask_at), weight(h_ref, 1, h_mask_at))
        pairs = (
            ((a0, a1, None, weight(a_ref, 0, mask_at)), (a1, o0, before_o, weight(a_ref, 1, mask_at))),
            ((o0, o1, None, weight(o_ref, 0, mask_at)), (o1, b0, after_o, weight(o_ref, 1, mask_at))),
            ((b0, b1, None, weight(b_ref, 0, mask_at)), (x1, c0, before_c, x_weight)),
            ((c0, c1, None, weight(c_ref, 0, mask_at)), (c1, y, before_y, weight(c_ref, 1, mask_at))),
        )
        peak = log_sum = None
        for pair in pairs:
            framed = []
            for head, tail, live, _ in pair:
                tail = tail * win_ref[half:, :]
                if live is not None:
                    tail = tail * live
                framed.append(jnp.concatenate([head * win_ref[:half, :], tail], axis=0))
            high, low = split(jnp.concatenate(framed, axis=1))
            mid = jnp.dot(
                f_ref[...],
                jnp.concatenate([high, low, high], axis=0),
                preferred_element_type=jnp.float32,
            )
            turned = []
            for s in range(2):
                re = mid[:ROWS, s * LB : (s + 1) * LB]
                im = mid[ROWS:, s * LB : (s + 1) * LB]
                turned.append(
                    jnp.concatenate(
                        [re * tw_ref[0] - im * tw_ref[1], re * tw_ref[1] + im * tw_ref[0]], axis=1
                    )
                )
            high, low = split(jnp.concatenate(turned, axis=0))
            out = jnp.dot(
                jnp.concatenate([high, low, high], axis=1),
                w_ref[...],
                preferred_element_type=jnp.float32,
            )
            powers = out[:, :LB] * out[:, :LB] + out[:, LB:] * out[:, LB:]
            for s in range(2):
                mine = powers[s * ROWS : (s + 1) * ROWS]
                first = jnp.where(swap, mine[LA // 2 : LA // 2 + 8], mine[:8])
                mine = jnp.concatenate([first, mine[8 : LA // 2]], axis=0)
                keep = pair[s][3]
                kept_power = keep * mine
                kept_log = keep * jnp.log(0.25 + mine)
                peak = kept_power if peak is None else jnp.maximum(peak, kept_power)
                log_sum = kept_log if log_sum is None else log_sum + kept_log
        for kind, value in enumerate((peak, log_sum)):
            turned = jnp.transpose(value)
            for i in range(parts):
                out_ref[pl.ds(kind * parts * per + i * per + c, shards, stride=lines), :] = turned[
                    i * shards : (i + 1) * shards
                ]
        return carry

    lax.fori_loop(0, per, one_channel, 0)


def finish_kernel(per, own, assign_ref, z_ref, cnt_ref, peak_ref, log_ref, part_ref):
    channels = GROUP * per
    parts = 2 * own
    lines = 2 * parts * per
    shards = z_ref.shape[0] // lines
    lane = lax.broadcasted_iota(jnp.int32, (channels, LANES), 1)
    line = lax.broadcasted_iota(jnp.int32, (channels, LANES), 0)
    kept_row = jnp.sum(cnt_ref[...].reshape(shards, LANES), axis=0, keepdims=True)
    kept = jnp.sum(jnp.where(lane == line, kept_row, 0.0), axis=1, keepdims=True)
    back = jnp.where(lane == 0, 0, LANES - lane)

    def joined(kind, op):
        size = parts * per
        sets = []
        for r in range(GROUP):
            total = None
            for q in range(shards // GROUP):
                at = (GROUP * q + r) * lines + kind * size
                term = z_ref[at : at + size, :]
                total = term if total is None else op(total, term)
            sets.append(total)
        pieces = []
        for e in range(own):
            for i, mirrored in ((e, False), (own + e, True)):
                piece = jnp.concatenate([t[i * per : (i + 1) * per] for t in sets], axis=0)
                if mirrored:
                    piece = jnp.take_along_axis(piece, back, axis=1)
                pieces.append(piece)
        return jnp.concatenate(pieces, axis=1)

    peak_ref[...] = joined(0, jnp.maximum)
    log_mean = joined(1, jnp.add) / kept
    log_ref[...] = log_mean
    bins = log_mean.shape[1]
    block = lax.broadcasted_iota(jnp.int32, (BLOCKS, bins), 0)
    block_small = lax.broadcasted_iota(jnp.int32, (BLOCKS, LANES), 0)
    sums = jnp.zeros((BLOCKS, bins), jnp.float32)
    counts = jnp.zeros((BLOCKS, LANES), jnp.float32)
    for c in range(channels):
        sums = sums + jnp.where(block == assign_ref[c], log_mean[c : c + 1], 0.0)
        counts = counts + jnp.where(block_small == assign_ref[c], 1.0, 0.0)
    both = jnp.concatenate([sums, counts], axis=1)
    for p in range(part_ref.shape[0]):
        part_ref[p] = both


def blocks_kernel(parts_ref, out_ref):
    total = parts_ref[0]
    for p in range(1, parts_ref.shape[0]):
        total = total + parts_ref[p]
    bins = out_ref.shape[1]
    out_ref[...] = total[:, :bins] / total[:, bins : bins + 1]


VMEM = pl.BlockSpec(memory_space=pltpu.VMEM)
SMEM = pl.BlockSpec(memory_space=pltpu.SMEM)
PARAMS = pltpu.CompilerParams(vmem_limit_bytes=48 * 1024 * 1024)


def f32(*shape):
    return jax.ShapeDtypeStruct(shape, jnp.float32)


def on_device(signal, gap_mask, assignment):
    channels, local_time = signal.shape
    shards = lax.axis_size("tm")
    per = channels // GROUP
    rows = local_time // LANES
    half_bins = SEG // 2
    bins = half_bins // shards
    own = LB // 2 // shards
    lines = 2 * 2 * own * per
    first, second, twiddle, window = tables(shards)

    lined = signal.reshape(channels, rows, LANES).transpose(1, 0, 2).reshape(-1, LANES)
    size, small = per * rows + 8, per * rows // 2 + 8
    o, a, b, c, h, cnt = pl.pallas_call(
        functools.partial(pack_kernel, per),
        out_shape=[f32(size, LANES)] * 4 + [f32(small, LANES), f32(shards, 1, LANES)],
        in_specs=[SMEM, VMEM],
        out_specs=[VMEM] * 6,
        compiler_params=PARAMS,
        name="pack",
    )(gap_mask, lined)

    def moved(x, by):
        return lax.ppermute(x, "tm", [(i, (i + by(i)) % shards) for i in range(shards)])

    a = moved(a, lambda i: 1)
    b = moved(b, lambda i: -1)
    c = moved(c, lambda i: 2 if i % 2 else -2)
    h = moved(h, lambda i: -3 if i % 2 else 3)
    cnt = lax.all_to_all(cnt, "tm", 0, 0, tiled=True)

    sums = pl.pallas_call(
        functools.partial(spectra_kernel, per, shards),
        out_shape=f32(shards * lines, LANES),
        in_specs=[VMEM] * 9,
        out_specs=VMEM,
        compiler_params=PARAMS,
        cost_estimate=pl.CostEstimate(
            flops=4_000_000_000, bytes_accessed=4_000_000, transcendentals=300_000
        ),
        name="spectra",
    )(o, a, b, c, h, jnp.asarray(first), jnp.asarray(second), twiddle, window)
    sums = lax.all_to_all(sums.reshape(shards, lines, LANES), "tm", 0, 0, tiled=True)
    peers = lax.axis_size(("chan", "sub"))
    peak_hold, log_mean, part = pl.pallas_call(
        functools.partial(finish_kernel, per, own),
        out_shape=[f32(channels, bins), f32(channels, bins), f32(peers, BLOCKS, bins + LANES)],
        in_specs=[SMEM, VMEM, VMEM],
        out_specs=[VMEM] * 3,
        compiler_params=PARAMS,
        name="finish",
    )(assignment, sums.reshape(shards * lines, LANES), cnt)
    part = lax.all_to_all(part, ("chan", "sub"), 0, 0, tiled=True)
    block_mean = pl.pallas_call(
        blocks_kernel,
        out_shape=f32(BLOCKS, bins),
        in_specs=[VMEM],
        out_specs=VMEM,
        compiler_params=PARAMS,
        name="blocks",
    )(part)
    return peak_hold, log_mean, block_mean


def solution(mesh):
    in_specs = (
        P(("grp", "chan", "sub"), "tm"),
        P(("grp", "chan", "sub"), "tm"),
        P(("grp", "chan", "sub")),
    )
    out_specs = (P(("grp", "chan", "sub"), "tm"), P(("grp", "chan", "sub"), "tm"), P("grp", "tm"))
    return jax.shard_map(
        on_device, mesh=mesh, in_specs=in_specs, out_specs=out_specs, check_vma=False
    )
```

time: 408 us -> 147 us (0.36)
  other arithmetic: 97.2 us -> 0 us
  waiting for transfers between devices: 104 us -> 16.5 us
  local copies, waits for them, and re-layouts: 86.7 us -> 3.54 us
  blocking collectives: 0 us -> 57.7 us
  matrix products: 42.2 us -> 0 us
  starting transfers between devices: 74.9 us -> 61.8 us
  Pallas kernels: 0 us -> 6.52 us
    all_to_all x3 -> x1, waiting for transfers between devices: 104 us -> 16.1 us  [on_device(): cnt = lax.all_to_all(cnt, 'tm', 0, 0, tiled=True)]
    unnamed x1 -> x0, other arithmetic: 74.6 us -> none
    all_to_all x3 -> x1, starting transfers between devices: 73.6 us -> 8.91 us  [on_device(): cnt = lax.all_to_all(cnt, 'tm', 0, 0, tiled=True)]
    all_to_all x0 -> x2, blocking collectives: none -> 57.7 us  [the longest x1 42 us: on_device(): lax.all_to_all(sums.reshape(shards, lines, LANES), 'tm', 0, 0, tiled=True)]
    ppermute x1 -> x4, starting transfers between devices: 1.31 us -> 52.9 us  [moved(): lax.ppermute(x, 'tm', [(i, (i + by(i)) % shards) for i in range(shards)])]
    dot_general x49 -> x0, matrix products: 42.2 us -> none  [the longest x8 8.04 us: one_channel(): jnp.einsum('ska,aj->skj', imag_mid, section_two[0], precision=highest)]
    unnamed x9 -> x13, local copies, waits for them, and re-layouts: 26.9 us -> 3.54 us
    split x1 -> x0, local copies, waits for them, and re-layouts: 21 us -> none  [side_by_side(): jnp.split(lax.all_to_all(both, axis, split_axis=split_dim, concat_axis=co...]
  transfers between devices with their start and end apart: 4 -> 5, of which waited for: 1 -> 2; matrix products, arithmetic and copies ran while one was open for 44% -> 0% of each run, Pallas kernels for 0% -> 2%
where the time goes in v1:
time: 147 us
  starting transfers between devices  61.8 us (42%)
  blocking collectives  57.7 us (39%)
  waiting for transfers between devices  16.5 us (11%)
  Pallas kernels  6.52 us (4%)
  local copies, waits for them, and re-layouts  3.54 us (2%)
    ppermute x4, starting transfers between devices, moved(): lax.ppermute(x, 'tm', [(i, (i + by(i)) % shards) for i in range(shards)])  52.9 us
    all_to_all x1, blocking collectives, on_device(): lax.all_to_all(sums.reshape(shards, lines, LANES), 'tm', 0, 0, tiled=True)  42 us
    all_to_all x1, waiting for transfers between devices, on_device(): cnt = lax.all_to_all(cnt, 'tm', 0, 0, tiled=True)  16.1 us
    all_to_all x1, blocking collectives, on_device(): part = lax.all_to_all(part, ('chan', 'sub'), 0, 0, tiled=True)  15.8 us
    all_to_all x1, starting transfers between devices, on_device(): cnt = lax.all_to_all(cnt, 'tm', 0, 0, tiled=True)  8.91 us
    unnamed x13, local copies, waits for them, and re-layouts  3.54 us
    pallas_call x1, Pallas kernels, on_device(): pl.pallas_call(functools.partial(spectra_kernel, per, shards), out_shape=...  3.11 us
  transfers between devices with their start and end apart: 5, of which 2 were waited for; matrix products, arithmetic and copies ran while one was open for 0% of the time, Pallas kernels for 2%

profile of v1, /device:TPU:33, one launch (start us, length us, event | category | flops | bytes accessed | tf_op | source)
XLA Modules:
  0.0 146.8 jit_solution(10944471294504087256)
XLA Ops:
  0.6 0.8 copy.10.mask_ref
  1.4 0.0 copy-start
  1.4 1.2 copy-done
  2.6 0.0 copy-start.2
  2.6 0.0 copy-start.3
  2.6 0.0 copy-start.4
  2.6 1.5 pack.1
  4.1 5.2 %collective-permute-start = (f32[520,128]{1,0:T(8,128)S(1)}, f32[520,128]{1,0:T(8,128)S(1)}, u32[]{:S(2)}, u32[]{:S(2)}) collective-permute-start(f32[520,128]{1,0:T(8,128)S(1)} %get-tuple-element.13), channel_id=1, source_target_pairs={{0,8},{8,16},{16,24},{24,32},{32,40},{40,48},{48,56},{56,64},{64,7... | collective-permute-start | bytes 798728 | tf_op jit(solution)/shard_map/ppermute | solution.py:272
  9.3 42.6 %collective-permute-start.1 = (f32[520,128]{1,0:T(8,128)S(1)}, f32[520,128]{1,0:T(8,128)S(1)}, u32[]{:S(2)}, u32[]{:S(2)}) collective-permute-start(f32[520,128]{1,0:T(8,128)S(1)} %get-tuple-element.14), channel_id=1, source_target_pairs={{0,248},{8,0},{16,8},{24,16},{32,24},{40,32},{48,40},{56,48},{64,5... | collective-permute-start | bytes 798728 | tf_op jit(solution)/shard_map/ppermute | solution.py:272
  51.9 3.1 %collective-permute-start.2 = (f32[520,128]{1,0:T(8,128)S(1)}, f32[520,128]{1,0:T(8,128)S(1)}, u32[]{:S(2)}, u32[]{:S(2)}) collective-permute-start(f32[520,128]{1,0:T(8,128)S(1)} %get-tuple-element.15), channel_id=1, source_target_pairs={{0,240},{8,24},{16,0},{24,40},{32,16},{40,56},{48,32},{56,72},{64,... | collective-permute-start | bytes 798728 | tf_op jit(solution)/shard_map/ppermute | solution.py:272
  55.0 2.0 %collective-permute-start.3 = (f32[264,128]{1,0:T(8,128)S(1)}, f32[264,128]{1,0:T(8,128)S(1)}, u32[]{:S(2)}, u32[]{:S(2)}) collective-permute-start(f32[264,128]{1,0:T(8,128)S(1)} %get-tuple-element.16), channel_id=1, source_target_pairs={{0,24},{8,240},{16,40},{24,0},{32,56},{40,16},{48,72},{56,32},{64,... | collective-permute-start | bytes 405512 | tf_op jit(solution)/shard_map/ppermute | solution.py:272
  57.0 8.9 %all-to-all-start.1 = ((f32[32,1,128]{2,1,0:T(1,128)}), f32[32,1,128]{2,1,0:T(1,128)S(1)}, u32[]{:S(2)}, u32[]{:S(2)}) async-start(f32[32,1,128]{2,1,0:T(1,128)} %get-tuple-element.17), calls=%async_computation.1 | async-start | bytes 32768 | tf_op jit(solution)/shard_map/all_to_all | solution.py:278
  65.9 0.4 collective-permute-done.3.h_ref
  66.3 0.0 collective-permute-done.a_ref
  66.3 0.0 collective-permute-done.1.b_ref
  66.3 0.0 collective-permute-done.2.c_ref
  66.3 0.0 copy-done.2
  66.3 0.0 copy-done.3
  66.3 0.0 copy-done.4
  66.3 0.0 copy-start.5
  66.4 0.9 copy-done.5
  67.3 3.1 %spectra.1 = f32[512,128]{1,0:T(8,128)S(1)} custom-call(f32[520,128]{1,0:T(8,128)S(1)} %get-tuple-element.12.o_ref, f32[520,128]{1,0:T(8,128)S(1)} %collective-permute-done.a_ref, f32[520,128]{1,0:T(8,128)S(1)} %collective-permute-done.1.b_ref, f32[520,128]{1,0:T(8,128)S(1)} %collective-permute-done.2.c_ref, f32[264,128]{1,0:T(8,128)S(1)} %collective-permute-done.3.h_ref, ...), custom_call_target="tpu_custom_call" | custom-call | flops 4000000000 | bytes 4000000 | tf_op jit(solution)/shard_map/spectra/pallas_call | solution.py:280
  70.4 16.1 %all-to-all-done.1.cnt_ref = f32[32,1,128]{2,1,0:T(1,128)S(1)} async-done(((f32[32,1,128]{2,1,0:T(1,128)}), f32[32,1,128]{2,1,0:T(1,128)S(1)}, u32[]{:S(2)}, u32[]{:S(2)}) %all-to-all-start.1) | async-done | bytes 16416 | tf_op jit(solution)/shard_map/all_to_all | solution.py:278
  86.5 42.0 %all_to_all.15 = f32[32,16,128]{2,1,0:T(8,128)S(1)} all-to-all(f32[32,16,128]{2,1,0:T(8,128)S(1)} %bitcast.9), channel_id=1, replica_groups=mesh['grp'=2,'tm'=32,'chan'=4,'sub'=2] {'tm'}, dimensions={0} | all-to-all | bytes 524288 | tf_op jit(solution)/shard_map/all_to_all | solution.py:291
  128.4 0.0 copy-start.1
  128.4 0.7 copy-done.1
  129.1 1.3 finish.1
  130.3 15.8 %all_to_all.16.parts_ref = f32[8,8,640]{2,1,0:T(8,128)S(1)} all-to-all(f32[8,8,640]{2,1,0:T(8,128)S(1)} %get-tuple-element.20), channel_id=1, replica_groups=mesh['grp'=2,'tm'=32,'chan'=4,'sub'=2] {'chan','sub'}, dimensions={0} | all-to-all | bytes 327680 | tf_op jit(solution)/shard_map/all_to_all | solution.py:301
  146.1 0.7 blocks.1
Async XLA Ops:
  1.4 1.2 copy-start
  2.6 63.7 %copy-start.2 = (bf16[288,768]{1,0:T(8,128)(2,1)S(1)}, bf16[288,768]{1,0:T(8,128)(2,1)}, u32[]{:S(2)}) copy-start(bf16[288,768]{1,0:T(8,128)(2,1)} %constant.8.clone.f_ref) | copy-start | bytes 1327108
  2.6 63.7 %copy-start.3 = (bf16[768,256]{1,0:T(8,128)(2,1)S(1)}, bf16[768,256]{1,0:T(8,128)(2,1)}, u32[]{:S(2)}) copy-start(bf16[768,256]{1,0:T(8,128)(2,1)} %constant.9.clone.w_ref) | copy-start | bytes 1179652
  2.6 63.7 %copy-start.4 = (f32[2,144,128]{2,1,0:T(8,128)S(1)}, f32[2,144,128]{2,1,0:T(8,128)}, u32[]{:S(2)}) copy-start(f32[2,144,128]{2,1,0:T(8,128)} %constant.10.clone.tw_ref) | copy-start | bytes 442372
  4.1 62.2 %collective-permute-start = (f32[520,128]{1,0:T(8,128)S(1)}, f32[520,128]{1,0:T(8,128)S(1)}, u32[]{:S(2)}, u32[]{:S(2)}) collective-permute-start(f32[520,128]{1,0:T(8,128)S(1)} %get-tuple-element.13), channel_id=1, source_target_pairs={{0,8},{8,16},{16,24},{24,32},{32,40},{40,48},{48,56},{56,64},{64,7... | collective-permute-start | bytes 798728 | tf_op jit(solution)/shard_map/ppermute | solution.py:272
  9.3 57.0 %collective-permute-start.1 = (f32[520,128]{1,0:T(8,128)S(1)}, f32[520,128]{1,0:T(8,128)S(1)}, u32[]{:S(2)}, u32[]{:S(2)}) collective-permute-start(f32[520,128]{1,0:T(8,128)S(1)} %get-tuple-element.14), channel_id=1, source_target_pairs={{0,248},{8,0},{16,8},{24,16},{32,24},{40,32},{48,40},{56,48},{64,5... | collective-permute-start | bytes 798728 | tf_op jit(solution)/shard_map/ppermute | solution.py:272
  51.9 14.4 %collective-permute-start.2 = (f32[520,128]{1,0:T(8,128)S(1)}, f32[520,128]{1,0:T(8,128)S(1)}, u32[]{:S(2)}, u32[]{:S(2)}) collective-permute-start(f32[520,128]{1,0:T(8,128)S(1)} %get-tuple-element.15), channel_id=1, source_target_pairs={{0,240},{8,24},{16,0},{24,40},{32,16},{40,56},{48,32},{56,72},{64,... | collective-permute-start | bytes 798728 | tf_op jit(solution)/shard_map/ppermute | solution.py:272
  55.0 11.3 %collective-permute-start.3 = (f32[264,128]{1,0:T(8,128)S(1)}, f32[264,128]{1,0:T(8,128)S(1)}, u32[]{:S(2)}, u32[]{:S(2)}) collective-permute-start(f32[264,128]{1,0:T(8,128)S(1)} %get-tuple-element.16), channel_id=1, source_target_pairs={{0,24},{8,240},{16,40},{24,0},{32,56},{40,16},{48,72},{56,32},{64,... | collective-permute-start | bytes 405512 | tf_op jit(solution)/shard_map/ppermute | solution.py:272
  57.0 29.5 %all-to-all-start.1 = ((f32[32,1,128]{2,1,0:T(1,128)}), f32[32,1,128]{2,1,0:T(1,128)S(1)}, u32[]{:S(2)}, u32[]{:S(2)}) async-start(f32[32,1,128]{2,1,0:T(1,128)} %get-tuple-element.17), calls=%async_computation.1 | async-start | bytes 32768 | tf_op jit(solution)/shard_map/all_to_all | solution.py:278
  66.3 0.9 copy-start.5
  128.4 0.7 copy-start.1

commit v2 on v1

--- a/solution.py
+++ b/solution.py
@@ -54,7 +54,7 @@
     return first, second, twiddle, window
 
 
-def pack_kernel(per, mask_ref, x_ref, o_ref, a_ref, b_ref, c_ref, h_ref, cnt_ref):
+def pack_kernel(per, mask_ref, x_ref, o_ref, a_ref, b_ref, c_ref, h_ref):
     me = lax.axis_index("tm")
     channels = GROUP * per
     rows = x_ref.shape[0] // channels
@@ -80,13 +80,6 @@
             pl.ds(start + first + c, half, stride=channels), :
         ]
     masks(h_ref, per * half, first)
-    lane = lax.broadcasted_iota(jnp.int32, (1, LANES), 1)
-    kept = jnp.zeros((1, LANES), jnp.float32)
-    for c in range(channels):
-        total = (mask_ref[c, 0] + mask_ref[c, 1]).astype(jnp.float32)
-        kept = jnp.where(lane == c, total, kept)
-    for d in range(cnt_ref.shape[0]):
-        cnt_ref[d] = kept
 
 
 def spectra_kernel(
@@ -107,6 +100,8 @@
     swap = (lax.broadcasted_iota(jnp.int32, (8, LANES), 0) == 0) & (
         lax.broadcasted_iota(jnp.int32, (8, LANES), 1) >= LB // 2
     )
+
+    lane = lax.broadcasted_iota(jnp.int32, (1, LANES), 1)
 
     def one_channel(c, carry):
         base = pl.multiple_of(c * rows, rows)
@@ -175,46 +170,58 @@
         for kind, value in enumerate((peak, log_sum)):
             turned = jnp.transpose(value)
             for i in range(parts):
-                out_ref[pl.ds(kind * parts * per + i * per + c, shards, stride=lines), :] = turned[
+                out_ref[pl.ds((kind * parts + i) * per + c, shards, stride=lines + 1), :] = turned[
                     i * shards : (i + 1) * shards
                 ]
-        return carry
-
-    lax.fori_loop(0, per, one_channel, 0)
-
-
-def finish_kernel(per, own, assign_ref, z_ref, cnt_ref, peak_ref, log_ref, part_ref):
+        kept = sum(w for pair in pairs for _, _, _, w in pair)
+        return jnp.where(lane == c, kept, carry)
+
+    kept = lax.fori_loop(0, per, one_channel, jnp.zeros((1, LANES), jnp.float32))
+    out_ref[pl.ds(lines, shards, stride=lines + 1), :] = jnp.broadcast_to(kept, (shards, LANES))
+
+
+def joined(ref, per, own, kind, op):
+    parts = 2 * own
+    size = parts * per
+    step = 2 * size + 1
+    shards = ref.shape[0] // step
+    lane = lax.broadcasted_iota(jnp.int32, (GROUP * per, LANES), 1)
+    back = jnp.where(lane == 0, 0, LANES - lane)
+    sets = []
+    for r in range(GROUP):
+        total = None
+        for q in range(shards // GROUP):
+            at = (GROUP * q + r) * step + kind * size
+            term = ref[at : at + size, :]
+            total = term if total is None else op(total, term)
+        sets.append(total)
+    pieces = []
+    for e in range(own):
+        for i, mirrored in ((e, False), (own + e, True)):
+            piece = jnp.concatenate([t[i * per : (i + 1) * per] for t in sets], axis=0)
+            if mirrored:
+                piece = jnp.take_along_axis(piece, back, axis=1)
+            pieces.append(piece)
+    return jnp.concatenate(pieces, axis=1)
+
+
+def finish_kernel(per, own, assign_ref, z_ref, peak_ref, log_ref, part_ref):
     channels = GROUP * per
-    parts = 2 * own
-    lines = 2 * parts * per
-    shards = z_ref.shape[0] // lines
+    lines = 4 * own * per
+    step = lines + 1
+    shards = z_ref.shape[0] // step
     lane = lax.broadcasted_iota(jnp.int32, (channels, LANES), 1)
     line = lax.broadcasted_iota(jnp.int32, (channels, LANES), 0)
-    kept_row = jnp.sum(cnt_ref[...].reshape(shards, LANES), axis=0, keepdims=True)
-    kept = jnp.sum(jnp.where(lane == line, kept_row, 0.0), axis=1, keepdims=True)
-    back = jnp.where(lane == 0, 0, LANES - lane)
-
-    def joined(kind, op):
-        size = parts * per
-        sets = []
-        for r in range(GROUP):
-            total = None
-            for q in range(shards // GROUP):
-                at = (GROUP * q + r) * lines + kind * size
-                term = z_ref[at : at + size, :]
-                total = term if total is None else op(total, term)
-            sets.append(total)
-        pieces = []
-        for e in range(own):
-            for i, mirrored in ((e, False), (own + e, True)):
-                piece = jnp.concatenate([t[i * per : (i + 1) * per] for t in sets], axis=0)
-                if mirrored:
-                    piece = jnp.take_along_axis(piece, back, axis=1)
-                pieces.append(piece)
-        return jnp.concatenate(pieces, axis=1)
-
-    peak_ref[...] = joined(0, jnp.maximum)
-    log_mean = joined(1, jnp.add) / kept
+    kept = jnp.zeros((channels, LANES), jnp.float32)
+    for r in range(GROUP):
+        row = jnp.zeros((1, LANES), jnp.float32)
+        for q in range(shards // GROUP):
+            at = (GROUP * q + r) * step + lines
+            row = row + z_ref[at : at + 1, :]
+        kept = jnp.where((line - per * r == lane) & (lane < per), row, kept)
+    kept = jnp.sum(kept, axis=1, keepdims=True)
+    log_mean = joined(z_ref, per, own, 1, jnp.add) / kept
+    peak_ref[...] = joined(z_ref, per, own, 0, jnp.maximum)
     log_ref[...] = log_mean
     bins = log_mean.shape[1]
     block = lax.broadcasted_iota(jnp.int32, (BLOCKS, bins), 0)
@@ -254,16 +261,16 @@
     half_bins = SEG // 2
     bins = half_bins // shards
     own = LB // 2 // shards
-    lines = 2 * 2 * own * per
+    lines = 4 * own * per
     first, second, twiddle, window = tables(shards)
 
     lined = signal.reshape(channels, rows, LANES).transpose(1, 0, 2).reshape(-1, LANES)
     size, small = per * rows + 8, per * rows // 2 + 8
-    o, a, b, c, h, cnt = pl.pallas_call(
+    o, a, b, c, h = pl.pallas_call(
         functools.partial(pack_kernel, per),
-        out_shape=[f32(size, LANES)] * 4 + [f32(small, LANES), f32(shards, 1, LANES)],
+        out_shape=[f32(size, LANES)] * 4 + [f32(small, LANES)],
         in_specs=[SMEM, VMEM],
-        out_specs=[VMEM] * 6,
+        out_specs=[VMEM] * 5,
         compiler_params=PARAMS,
         name="pack",
     )(gap_mask, lined)
@@ -275,11 +282,10 @@
     b = moved(b, lambda i: -1)
     c = moved(c, lambda i: 2 if i % 2 else -2)
     h = moved(h, lambda i: -3 if i % 2 else 3)
-    cnt = lax.all_to_all(cnt, "tm", 0, 0, tiled=True)
 
     sums = pl.pallas_call(
         functools.partial(spectra_kernel, per, shards),
-        out_shape=f32(shards * lines, LANES),
+        out_shape=f32(shards * (lines + 1), LANES),
         in_specs=[VMEM] * 9,
         out_specs=VMEM,
         compiler_params=PARAMS,
@@ -288,16 +294,16 @@
         ),
         name="spectra",
     )(o, a, b, c, h, jnp.asarray(first), jnp.asarray(second), twiddle, window)
-    sums = lax.all_to_all(sums.reshape(shards, lines, LANES), "tm", 0, 0, tiled=True)
+    sums = lax.all_to_all(sums.reshape(shards, 1, -1), "tm", 0, 0, tiled=True)
     peers = lax.axis_size(("chan", "sub"))
     peak_hold, log_mean, part = pl.pallas_call(
         functools.partial(finish_kernel, per, own),
         out_shape=[f32(channels, bins), f32(channels, bins), f32(peers, BLOCKS, bins + LANES)],
-        in_specs=[SMEM, VMEM, VMEM],
+        in_specs=[SMEM, VMEM],
         out_specs=[VMEM] * 3,
         compiler_params=PARAMS,
         name="finish",
-    )(assignment, sums.reshape(shards * lines, LANES), cnt)
+    )(assignment, sums.reshape(-1, LANES))
     part = lax.all_to_all(part, ("chan", "sub"), 0, 0, tiled=True)
     block_mean = pl.pallas_call(
         blocks_kernel,

time: 147 us -> 137 us (0.932)
  starting transfers between devices: 61.8 us -> 52.9 us
  waiting for transfers between devices: 16.5 us -> 9.31 us
  blocking collectives: 57.7 us -> 63.6 us
    all_to_all x1 -> x0, waiting for transfers between devices: 16.1 us -> none  [on_device(): cnt = lax.all_to_all(cnt, 'tm', 0, 0, tiled=True)]
    ppermute x4, waiting for transfers between devices: 0.4 us -> 9.31 us  [moved(): lax.ppermute(x, 'tm', [(i, (i + by(i)) % shards) for i in range(shards)])]
    all_to_all x1 -> x0, starting transfers between devices: 8.91 us -> none  [on_device(): cnt = lax.all_to_all(cnt, 'tm', 0, 0, tiled=True)]
    all_to_all x1, blocking collectives: 42 us -> 50.5 us  [on_device(): sums = lax.all_to_all(sums.reshape(shards, 1, -1), 'tm', 0, 0, tiled=True)]
    all_to_all x1, blocking collectives: 15.8 us -> 13.1 us  [on_device(): part = lax.all_to_all(part, ('chan', 'sub'), 0, 0, tiled=True)]
  transfers between devices with their start and end apart: 5 -> 4, of which waited for: 2 -> 1; matrix products, arithmetic and copies ran while one was open for 0% -> 0% of each run, Pallas kernels for 2% -> 0%
where the time goes in v2:
time: 137 us; the launch traced here: 136 us
  blocking collectives  63.6 us (46%)
  starting transfers between devices  52.9 us (39%)
  waiting for transfers between devices  9.31 us (7%)
  Pallas kernels  6.09 us (4%)
  local copies, waits for them, and re-layouts  3.54 us (3%)
    ppermute x4, starting transfers between devices, moved(): lax.ppermute(x, 'tm', [(i, (i + by(i)) % shards) for i in range(shards)])  52.9 us
    all_to_all x1, blocking collectives, on_device(): sums = lax.all_to_all(sums.reshape(shards, 1, -1), 'tm', 0, 0, tiled=True)  50.5 us
    all_to_all x1, blocking collectives, on_device(): part = lax.all_to_all(part, ('chan', 'sub'), 0, 0, tiled=True)  13.1 us
    ppermute x4, waiting for transfers between devices, moved(): lax.ppermute(x, 'tm', [(i, (i + by(i)) % shards) for i in range(shards)])  9.31 us
    unnamed x13, local copies, waits for them, and re-layouts  3.54 us
    pallas_call x1, Pallas kernels, on_device(): pl.pallas_call(functools.partial(spectra_kernel, per, shards), out_shape=...  3.3 us
  transfers between devices with their start and end apart: 4, of which 1 were waited for; matrix products, arithmetic and copies ran while one was open for 0% of the time, Pallas kernels for 0%

profile of v2, /device:TPU:33, one launch (start us, length us, event | category | flops | bytes accessed | tf_op | source)
XLA Modules:
  0.0 136.2 jit_solution(6338286584319753312)
XLA Ops:
  0.6 0.8 copy.11.mask_ref
  1.4 0.0 copy-start
  1.4 1.2 copy-done
  2.6 0.0 copy-start.2
  2.6 0.0 copy-start.3
  2.6 0.0 copy-start.4
  2.6 0.9 pack.1
  3.5 5.3 %collective-permute-start = (f32[520,128]{1,0:T(8,128)S(1)}, f32[520,128]{1,0:T(8,128)S(1)}, u32[]{:S(2)}, u32[]{:S(2)}) collective-permute-start(f32[520,128]{1,0:T(8,128)S(1)} %get-tuple-element.12), channel_id=1, source_target_pairs={{0,8},{8,16},{16,24},{24,32},{32,40},{40,48},{48,56},{56,64},{64,7... | collective-permute-start | bytes 798728 | tf_op jit(solution)/shard_map/ppermute | solution.py:279
  8.7 42.6 %collective-permute-start.1 = (f32[520,128]{1,0:T(8,128)S(1)}, f32[520,128]{1,0:T(8,128)S(1)}, u32[]{:S(2)}, u32[]{:S(2)}) collective-permute-start(f32[520,128]{1,0:T(8,128)S(1)} %get-tuple-element.13), channel_id=1, source_target_pairs={{0,248},{8,0},{16,8},{24,16},{32,24},{40,32},{48,40},{56,48},{64,5... | collective-permute-start | bytes 798728 | tf_op jit(solution)/shard_map/ppermute | solution.py:279
  51.3 3.1 %collective-permute-start.2 = (f32[520,128]{1,0:T(8,128)S(1)}, f32[520,128]{1,0:T(8,128)S(1)}, u32[]{:S(2)}, u32[]{:S(2)}) collective-permute-start(f32[520,128]{1,0:T(8,128)S(1)} %get-tuple-element.14), channel_id=1, source_target_pairs={{0,240},{8,24},{16,0},{24,40},{32,16},{40,56},{48,32},{56,72},{64,... | collective-permute-start | bytes 798728 | tf_op jit(solution)/shard_map/ppermute | solution.py:279
  54.4 2.0 %collective-permute-start.3 = (f32[264,128]{1,0:T(8,128)S(1)}, f32[264,128]{1,0:T(8,128)S(1)}, u32[]{:S(2)}, u32[]{:S(2)}) collective-permute-start(f32[264,128]{1,0:T(8,128)S(1)} %get-tuple-element.15), channel_id=1, source_target_pairs={{0,24},{8,240},{16,40},{24,0},{32,56},{40,16},{48,72},{56,32},{64,... | collective-permute-start | bytes 405512 | tf_op jit(solution)/shard_map/ppermute | solution.py:279
  56.4 9.3 %collective-permute-done.3.h_ref = f32[264,128]{1,0:T(8,128)S(1)} collective-permute-done((f32[264,128]{1,0:T(8,128)S(1)}, f32[264,128]{1,0:T(8,128)S(1)}, u32[]{:S(2)}, u32[]{:S(2)}) %collective-permute-start.3) | collective-permute-done | bytes 135200 | tf_op jit(solution)/shard_map/ppermute | solution.py:279
  65.7 0.0 collective-permute-done.a_ref
  65.7 0.0 collective-permute-done.1.b_ref
  65.7 0.0 collective-permute-done.2.c_ref
  65.7 0.0 copy-done.2
  65.7 0.0 copy-done.3
  65.7 0.0 copy-done.4
  65.8 0.0 copy-start.5
  65.8 0.9 copy-done.5
  66.7 3.3 %spectra.1 = f32[544,128]{1,0:T(8,128)S(1)} custom-call(f32[520,128]{1,0:T(8,128)S(1)} %get-tuple-element.11.o_ref, f32[520,128]{1,0:T(8,128)S(1)} %collective-permute-done.a_ref, f32[520,128]{1,0:T(8,128)S(1)} %collective-permute-done.1.b_ref, f32[520,128]{1,0:T(8,128)S(1)} %collective-permute-done.2.c_ref, f32[264,128]{1,0:T(8,128)S(1)} %collective-permute-done.3.h_ref, ...), custom_call_target="tpu_custom_call" | custom-call | flops 4000000000 | bytes 4000000 | tf_op jit(solution)/shard_map/spectra/pallas_call | solution.py:286
  70.0 50.5 %all_to_all.10 = f32[32,1,2176]{2,1,0:T(1,128)S(1)} all-to-all(f32[32,1,2176]{2,1,0:T(1,128)S(1)} %bitcast.9), channel_id=1, replica_groups=mesh['grp'=2,'tm'=32,'chan'=4,'sub'=2] {'tm'}, dimensions={0} | all-to-all | bytes 557056 | tf_op jit(solution)/shard_map/all_to_all | solution.py:297
  120.5 0.0 copy-start.1
  120.5 0.7 copy-done.1
  121.1 1.3 finish.1
  122.4 13.1 %all_to_all.11.parts_ref = f32[8,8,640]{2,1,0:T(8,128)S(1)} all-to-all(f32[8,8,640]{2,1,0:T(8,128)S(1)} %get-tuple-element.18), channel_id=1, replica_groups=mesh['grp'=2,'tm'=32,'chan'=4,'sub'=2] {'chan','sub'}, dimensions={0} | all-to-all | bytes 327680 | tf_op jit(solution)/shard_map/all_to_all | solution.py:307
  135.5 0.7 blocks.1
Async XLA Ops:
  1.4 1.2 copy-start
  2.6 63.1 %copy-start.2 = (bf16[288,768]{1,0:T(8,128)(2,1)S(1)}, bf16[288,768]{1,0:T(8,128)(2,1)}, u32[]{:S(2)}) copy-start(bf16[288,768]{1,0:T(8,128)(2,1)} %constant.8.clone.f_ref) | copy-start | bytes 1327108
  2.6 63.1 %copy-start.3 = (bf16[768,256]{1,0:T(8,128)(2,1)S(1)}, bf16[768,256]{1,0:T(8,128)(2,1)}, u32[]{:S(2)}) copy-start(bf16[768,256]{1,0:T(8,128)(2,1)} %constant.9.clone.w_ref) | copy-start | bytes 1179652
  2.6 63.1 %copy-start.4 = (f32[2,144,128]{2,1,0:T(8,128)S(1)}, f32[2,144,128]{2,1,0:T(8,128)}, u32[]{:S(2)}) copy-start(f32[2,144,128]{2,1,0:T(8,128)} %constant.10.clone.tw_ref) | copy-start | bytes 442372
  3.5 62.2 %collective-permute-start = (f32[520,128]{1,0:T(8,128)S(1)}, f32[520,128]{1,0:T(8,128)S(1)}, u32[]{:S(2)}, u32[]{:S(2)}) collective-permute-start(f32[520,128]{1,0:T(8,128)S(1)} %get-tuple-element.12), channel_id=1, source_target_pairs={{0,8},{8,16},{16,24},{24,32},{32,40},{40,48},{48,56},{56,64},{64,7... | collective-permute-start | bytes 798728 | tf_op jit(solution)/shard_map/ppermute | solution.py:279
  8.7 57.0 %collective-permute-start.1 = (f32[520,128]{1,0:T(8,128)S(1)}, f32[520,128]{1,0:T(8,128)S(1)}, u32[]{:S(2)}, u32[]{:S(2)}) collective-permute-start(f32[520,128]{1,0:T(8,128)S(1)} %get-tuple-element.13), channel_id=1, source_target_pairs={{0,248},{8,0},{16,8},{24,16},{32,24},{40,32},{48,40},{56,48},{64,5... | collective-permute-start | bytes 798728 | tf_op jit(solution)/shard_map/ppermute | solution.py:279
  51.3 14.4 %collective-permute-start.2 = (f32[520,128]{1,0:T(8,128)S(1)}, f32[520,128]{1,0:T(8,128)S(1)}, u32[]{:S(2)}, u32[]{:S(2)}) collective-permute-start(f32[520,128]{1,0:T(8,128)S(1)} %get-tuple-element.14), channel_id=1, source_target_pairs={{0,240},{8,24},{16,0},{24,40},{32,16},{40,56},{48,32},{56,72},{64,... | collective-permute-start | bytes 798728 | tf_op jit(solution)/shard_map/ppermute | solution.py:279
  54.4 11.3 %collective-permute-start.3 = (f32[264,128]{1,0:T(8,128)S(1)}, f32[264,128]{1,0:T(8,128)S(1)}, u32[]{:S(2)}, u32[]{:S(2)}) collective-permute-start(f32[264,128]{1,0:T(8,128)S(1)} %get-tuple-element.15), channel_id=1, source_target_pairs={{0,24},{8,240},{16,40},{24,0},{32,56},{40,16},{48,72},{56,32},{64,... | collective-permute-start | bytes 405512 | tf_op jit(solution)/shard_map/ppermute | solution.py:279
  65.8 0.9 copy-start.5
  120.5 0.7 copy-start.1

commit v3 on v2

v3 whole, which is shorter than its diff:
```python
import functools
import math

import jax
import jax.numpy as jnp
import numpy as np
from jax import lax
from jax.experimental import pallas as pl
from jax.experimental.pallas import tpu as pltpu
from jax.sharding import PartitionSpec as P

LA = 256
LB = 128
BLOCKS = 8
SEG = LA * LB
GROUP = 4
ROWS = 144
LANES = 128


def split(x):
    high = x.astype(jnp.bfloat16)
    return high, (x - high.astype(jnp.float32)).astype(jnp.bfloat16)


def split_np(x):
    high = x.astype(np.float32).astype(jnp.bfloat16)
    low = (x - high.astype(np.float64)).astype(np.float32).astype(jnp.bfloat16)
    return high, low


@functools.lru_cache
def tables(shards):
    k1 = np.arange(ROWS)[:, None]
    angle = 2 * math.pi * ((k1 * np.arange(LA)[None, :]) % LA) / LA
    live = k1 <= LA // 2
    first = np.concatenate([np.cos(angle) * live, -np.sin(angle) * live], axis=0)
    high, low = split_np(first)
    first = np.concatenate([high, high, low], axis=1)
    angle = 2 * math.pi * (k1 * np.arange(LB)[None, :]) / SEG
    scale = math.sqrt(1.0 / (0.375 * SEG)) * live
    twiddle = np.stack([np.cos(angle) * scale, -np.sin(angle) * scale]).astype(np.float32)
    own = LB // 2 // shards
    d = np.arange(shards).reshape(-1, GROUP).T
    k2 = [own * d + e for e in range(own)] + [LB - 1 - own * d - e for e in range(own)]
    k2 = np.stack(k2, axis=1).reshape(1, -1)
    angle = 2 * math.pi * ((np.arange(LB)[:, None] * k2) % LB) / LB
    c, s = np.cos(angle), -np.sin(angle)
    second = np.concatenate([np.concatenate([c, s], 1), np.concatenate([-s, c], 1)], 0)
    high, low = split_np(second)
    second = np.concatenate([high, high, low], axis=0)
    n = np.arange(SEG)
    window = (0.5 - 0.5 * np.cos(2 * math.pi * n / SEG)).reshape(LA, LB).astype(np.float32)
    return first, second, np.concatenate([*twiddle, window], axis=0)


def pack_kernel(per, mask_ref, x_ref, o_ref, a_ref, b_ref, c_ref, h_ref):
    me = lax.axis_index("tm")
    channels = GROUP * per
    rows = x_ref.shape[0] // channels
    half = rows // 2
    even = lax.rem(me, 2) == 0

    def masks(ref, at, first):
        ref[at : at + 8, :] = jnp.zeros((8, LANES), jnp.float32)
        for c in range(per):
            for s in range(2):
                value = mask_ref[s, first + c].astype(jnp.float32)
                ref[at + 2 * c + s : at + 2 * c + s + 1, :] = jnp.full((1, LANES), value)

    for ref, shift in ((c_ref, 2), (a_ref, 1), (b_ref, GROUP - 1), (o_ref, 0)):
        first = per * lax.rem(me + shift, GROUP)
        for c in range(per):
            ref[c * rows : (c + 1) * rows, :] = x_ref[pl.ds(first + c, rows, stride=channels), :]
        masks(ref, per * rows, first)
    first = per * lax.rem(me + 2, GROUP)
    start = jnp.where(even, half * channels, 0)
    for c in range(per):
        h_ref[c * half : (c + 1) * half, :] = x_ref[
            pl.ds(start + first + c, half, stride=channels), :
        ]
    masks(h_ref, per * half, first)


def spectra_kernel(per, shards, o_ref, a_ref, b_ref, c_ref, h_ref, f_ref, w_ref, t_ref, out_ref):
    me = lax.axis_index("tm")
    even = lax.rem(me, 2) == 0
    rows = (o_ref.shape[0] - 8) // per
    half = rows // 2
    sets = shards // GROUP
    parts = LB // sets
    lines = 2 * parts * per
    starts_a = jnp.where(me == 1, 0.0, 1.0)
    starts_o = jnp.where(me == 0, 0.0, 1.0)
    starts_b = jnp.where(me == shards - 1, 0.0, 1.0)
    starts_y = jnp.where(me == shards - 2, 0.0, 1.0)
    lane = lax.broadcasted_iota(jnp.int32, (1, LANES), 1)
    swap = (lax.broadcasted_iota(jnp.int32, (8, LANES), 0) == 0) & (
        lax.rem(lax.broadcasted_iota(jnp.int32, (8, LANES), 1), parts // GROUP * sets)
        >= parts // GROUP // 2 * sets
    )

    def one_channel(c, carry):
        base = pl.multiple_of(c * rows, rows)

        def halves(ref):
            return ref[pl.ds(base, half), :], ref[pl.ds(base + half, half), :]

        def weight(ref, s, at=per * rows):
            return ref[pl.ds(at + 2 * c + s, 1), :]

        o0, o1 = halves(o_ref)
        a0, a1 = halves(a_ref)
        b0, b1 = halves(b_ref)
        c0, c1 = halves(c_ref)
        h = h_ref[pl.ds(pl.multiple_of(c * half, half), half), :]
        x = jnp.where(even, h, c1)
        y = jnp.where(even, c0, h)
        x_weight = jnp.where(even, weight(h_ref, 1, per * half), weight(c_ref, 1))
        pairs = (
            ((o0, o1, None, weight(o_ref, 0)), (o1, b0, starts_b, weight(o_ref, 1))),
            ((a0, a1, None, weight(a_ref, 0)), (a1, o0, starts_o, weight(a_ref, 1))),
            ((b0, b1, None, weight(b_ref, 0)), (b1, y, starts_y, weight(b_ref, 1))),
            ((c0, c1, None, weight(c_ref, 0)), (x, a0, starts_a, x_weight)),
        )
        window = t_ref[2 * ROWS :, :]
        peak = log_sum = None
        for pair in pairs:
            framed = []
            for head, tail, live, _ in pair:
                tail = tail * window[half:]
                if live is not None:
                    tail = tail * live
                framed.append(jnp.concatenate([head * window[:half], tail], axis=0))
            high, low = split(jnp.concatenate(framed, axis=1))
            mid = jnp.dot(
                f_ref[...],
                jnp.concatenate([high, low, high], axis=0),
                preferred_element_type=jnp.float32,
            )
            cosine, sine = t_ref[:ROWS, :], t_ref[ROWS : 2 * ROWS, :]
            turned = []
            for s in range(2):
                re = mid[:ROWS, s * LB : (s + 1) * LB]
                im = mid[ROWS:, s * LB : (s + 1) * LB]
                turned.append(
                    jnp.concatenate([re * cosine - im * sine, re * sine + im * cosine], axis=1)
                )
            high, low = split(jnp.concatenate(turned, axis=0))
            out = jnp.dot(
                jnp.concatenate([high, low, high], axis=1),
                w_ref[...],
                preferred_element_type=jnp.float32,
            )
            powers = out[:, :LB] * out[:, :LB] + out[:, LB:] * out[:, LB:]
            for s in range(2):
                mine = powers[s * ROWS : (s + 1) * ROWS]
                first = jnp.where(swap, mine[LA // 2 : LA // 2 + 8], mine[:8])
                mine = jnp.concatenate([first, mine[8 : LA // 2]], axis=0)
                keep = pair[s][3]
                kept_power = keep * mine
                kept_log = keep * jnp.log(0.25 + mine)
                peak = kept_power if peak is None else jnp.maximum(peak, kept_power)
                log_sum = kept_log if log_sum is None else log_sum + kept_log
        for kind, value in enumerate((peak, log_sum)):
            turned = jnp.transpose(value)
            for i in range(parts):
                out_ref[pl.ds((kind * parts + i) * per + c, sets, stride=lines + 1), :] = turned[
                    i * sets : (i + 1) * sets
                ]
        kept = sum(w for pair in pairs for _, _, _, w in pair)
        return jnp.where(lane == c, kept, carry)

    kept = lax.fori_loop(0, per, one_channel, jnp.zeros((1, LANES), jnp.float32))
    out_ref[pl.ds(lines, sets, stride=lines + 1), :] = jnp.broadcast_to(kept, (sets, LANES))


def join_kernel(per, sets, peers, assign_ref, z_ref, out_ref):
    lines = z_ref.shape[0] // sets
    size = (lines - 1) // 2 // GROUP
    first = per * lax.rem(lax.axis_index("tm"), GROUP)
    lane = lax.broadcasted_iota(jnp.int32, (size, LANES), 1)
    line = lax.broadcasted_iota(jnp.int32, (size, LANES), 0)

    def joined(at, count, op):
        total = z_ref[at : at + count, :]
        for q in range(1, sets):
            total = op(total, z_ref[q * lines + at : q * lines + at + count, :])
        return total

    kept = joined(lines - 1, 1, jnp.add)
    kept = jnp.sum(jnp.where(lane == lax.rem(line, per), kept, 0.0), axis=1, keepdims=True)
    ids = [jnp.full((1, LANES), assign_ref[first + c].astype(jnp.float32)) for c in range(per)]
    ids = jnp.concatenate(ids, axis=0)
    step = 2 * size + per
    for r in range(GROUP):
        peak = joined(r * size, size, jnp.maximum)
        log_mean = joined((GROUP + r) * size, size, jnp.add) / kept
        for p in range(peers):
            at = (r * peers + p) * step
            out_ref[at : at + size, :] = peak
            out_ref[at + size : at + 2 * size, :] = log_mean
            out_ref[at + 2 * size : at + step, :] = ids


def finish_kernel(per, peers, z_ref, peak_ref, log_ref, block_ref):
    me = lax.axis_index(("chan", "sub"))
    step = z_ref.shape[0] // (GROUP * peers)
    size = (step - per) // 2
    parts = size // per
    own = parts // 2
    lane = lax.broadcasted_iota(jnp.int32, (GROUP * per, LANES), 1)
    back = jnp.where(lane == 0, 0, LANES - lane)

    def in_order(pieces):
        out = []
        for e in range(own):
            out.append(pieces[e])
            out.append(jnp.take_along_axis(pieces[own + e], back, axis=1))
        return jnp.concatenate(out, axis=1)

    for kind, ref in enumerate((peak_ref, log_ref)):
        mine = []
        for r in range(GROUP):
            value = None
            for p in range(peers):
                at = (r * peers + p) * step + kind * size
                term = z_ref[at : at + size, :]
                value = term if value is None else jnp.where(me == p, term, value)
            mine.append(value)
        ref[...] = in_order(
            [
                jnp.concatenate([m[i * per : (i + 1) * per] for m in mine], axis=0)
                for i in range(parts)
            ]
        )
    block = lax.broadcasted_iota(jnp.int32, (BLOCKS, LANES), 0).astype(jnp.float32)
    sums = [jnp.zeros((BLOCKS, LANES), jnp.float32)] * parts
    counts = jnp.zeros((BLOCKS, LANES), jnp.float32)
    for s in range(GROUP * peers):
        at = s * step
        for c in range(per):
            inside = block == z_ref[at + 2 * size + c : at + 2 * size + c + 1, :]
            counts = counts + jnp.where(inside, 1.0, 0.0)
            for i in range(parts):
                row = at + size + i * per + c
                sums[i] = sums[i] + jnp.where(inside, z_ref[row : row + 1, :], 0.0)
    block_ref[...] = in_order([total / counts for total in sums])


VMEM = pl.BlockSpec(memory_space=pltpu.VMEM)
SMEM = pl.BlockSpec(memory_space=pltpu.SMEM)
PARAMS = pltpu.CompilerParams(vmem_limit_bytes=48 * 1024 * 1024)


def f32(*shape):
    return jax.ShapeDtypeStruct(shape, jnp.float32)


def on_device(signal, gap_mask, assignment):
    channels, local_time = signal.shape
    shards = lax.axis_size("tm")
    peers = lax.axis_size(("chan", "sub"))
    sets = shards // GROUP
    per = channels // GROUP
    rows = local_time // LANES
    bins = SEG // 2 // shards
    size = bins // LANES * per
    first, second, tables_f32 = tables(shards)

    lined = signal.reshape(channels, rows, LANES).transpose(1, 0, 2).reshape(-1, LANES)
    whole, small = per * rows + 8, per * rows // 2 + 8
    o, a, b, c, h = pl.pallas_call(
        functools.partial(pack_kernel, per),
        out_shape=[f32(whole, LANES)] * 4 + [f32(small, LANES)],
        in_specs=[SMEM, VMEM],
        out_specs=[VMEM] * 5,
        compiler_params=PARAMS,
        name="pack",
    )(gap_mask.T, lined)

    def moved(x, by):
        return lax.ppermute(x, "tm", [(i, (i + by(i)) % shards) for i in range(shards)])

    c = moved(c, lambda i: 2 if i % 2 else -2)
    h = moved(h, lambda i: -2 if i % 2 else 2)
    a = moved(a, lambda i: 1)
    b = moved(b, lambda i: -1)

    lines = 2 * GROUP * size + 1
    sums = pl.pallas_call(
        functools.partial(spectra_kernel, per, shards),
        out_shape=f32(sets * lines, LANES),
        in_specs=[VMEM] * 8,
        out_specs=VMEM,
        compiler_params=PARAMS,
        cost_estimate=pl.CostEstimate(
            flops=4_000_000_000, bytes_accessed=4_000_000, transcendentals=300_000
        ),
        name="spectra",
    )(o, a, b, c, h, jnp.asarray(first), jnp.asarray(second), tables_f32)
    sums = lax.all_to_all(
        sums.reshape(sets, 1, -1),
        "tm",
        0,
        0,
        tiled=True,
        axis_index_groups=[[GROUP * q + r for q in range(sets)] for r in range(GROUP)],
    )
    step = 2 * size + per
    near = GROUP * peers
    joined = pl.pallas_call(
        functools.partial(join_kernel, per, sets, peers),
        out_shape=f32(near * step, LANES),
        in_specs=[SMEM, VMEM],
        out_specs=VMEM,
        compiler_params=PARAMS,
        name="join",
    )(assignment, sums.reshape(-1, LANES))
    joined = lax.all_to_all(
        joined.reshape(near, 1, -1),
        ("tm", "chan", "sub"),
        0,
        0,
        tiled=True,
        axis_index_groups=[[near * q + s for s in range(near)] for q in range(sets)],
    )
    return pl.pallas_call(
        functools.partial(finish_kernel, per, peers),
        out_shape=[f32(channels, bins), f32(channels, bins), f32(BLOCKS, bins)],
        in_specs=[VMEM],
        out_specs=[VMEM] * 3,
        compiler_params=PARAMS,
        name="finish",
    )(joined.reshape(-1, LANES))


def solution(mesh):
    in_specs = (
        P(("grp", "chan", "sub"), "tm"),
        P(("grp", "chan", "sub"), "tm"),
        P(("grp", "chan", "sub")),
    )
    out_specs = (P(("grp", "chan", "sub"), "tm"), P(("grp", "chan", "sub"), "tm"), P("grp", "tm"))
    return jax.shard_map(
        on_device, mesh=mesh, in_specs=in_specs, out_specs=out_specs, check_vma=False
    )
```

time: 137 us -> 135 us (0.985)
    unnamed x13 -> x12, local copies, waits for them, and re-layouts: 3.54 us -> 3.51 us
where the time goes in v3:
time: 135 us
  blocking collectives  63 us (47%)
  starting transfers between devices  54.1 us (40%)
  waiting for transfers between devices  7.96 us (6%)
  Pallas kernels  5.46 us (4%)
  local copies, waits for them, and re-layouts  3.51 us (3%)
    ppermute x4, starting transfers between devices, moved(): lax.ppermute(x, 'tm', [(i, (i + by(i)) % shards) for i in range(shards)])  54.1 us
    all_to_all x1, blocking collectives, on_device(): lax.all_to_all(sums.reshape(sets, 1, -1), 'tm', 0, 0, tiled=True, axis_in...  32.2 us
    all_to_all x1, blocking collectives, on_device(): lax.all_to_all(joined.reshape(near, 1, -1), ('tm', 'chan', 'sub'), 0, 0,...  30.8 us
    ppermute x4, waiting for transfers between devices, moved(): lax.ppermute(x, 'tm', [(i, (i + by(i)) % shards) for i in range(shards)])  7.96 us
    unnamed x12, local copies, waits for them, and re-layouts  3.51 us
    pallas_call x1, Pallas kernels, on_device(): pl.pallas_call(functools.partial(spectra_kernel, per, shards), out_shape=...  3.21 us
  transfers between devices with their start and end apart: 4, of which 1 were waited for; matrix products, arithmetic and copies ran while one was open for 0% of the time, Pallas kernels for 0%

profile of v3, /device:TPU:33, one launch (start us, length us, event | category | flops | bytes accessed | tf_op | source)
XLA Modules:
  0.0 134.8 jit_solution(1108489343381359499)
XLA Ops:
  0.6 0.0 copy-start.1
  0.6 0.7 copy-done.1
  1.3 0.0 copy-start
  1.3 1.2 copy-done
  2.5 0.0 copy-start.3
  2.5 0.0 copy-start.4
  2.5 0.8 pack.1
  3.4 5.3 %collective-permute-start = (f32[520,128]{1,0:T(8,128)S(1)}, f32[520,128]{1,0:T(8,128)S(1)}, u32[]{:S(2)}, u32[]{:S(2)}) collective-permute-start(f32[520,128]{1,0:T(8,128)S(1)} %get-tuple-element.9), channel_id=1, source_target_pairs={{0,8},{8,16},{16,24},{24,32},{32,40},{40,48},{48,56},{56,64},{64,7... | collective-permute-start | bytes 798728 | tf_op jit(solution)/shard_map/ppermute | solution.py:283
  8.6 42.6 %collective-permute-start.1 = (f32[520,128]{1,0:T(8,128)S(1)}, f32[520,128]{1,0:T(8,128)S(1)}, u32[]{:S(2)}, u32[]{:S(2)}) collective-permute-start(f32[520,128]{1,0:T(8,128)S(1)} %get-tuple-element.10), channel_id=1, source_target_pairs={{0,248},{8,0},{16,8},{24,16},{32,24},{40,32},{48,40},{56,48},{64,5... | collective-permute-start | bytes 798728 | tf_op jit(solution)/shard_map/ppermute | solution.py:283
  51.2 3.1 %collective-permute-start.2 = (f32[520,128]{1,0:T(8,128)S(1)}, f32[520,128]{1,0:T(8,128)S(1)}, u32[]{:S(2)}, u32[]{:S(2)}) collective-permute-start(f32[520,128]{1,0:T(8,128)S(1)} %get-tuple-element.11), channel_id=1, source_target_pairs={{0,240},{8,24},{16,0},{24,40},{32,16},{40,56},{48,32},{56,72},{64,... | collective-permute-start | bytes 798728 | tf_op jit(solution)/shard_map/ppermute | solution.py:283
  54.3 3.1 %collective-permute-start.3 = (f32[264,128]{1,0:T(8,128)S(1)}, f32[264,128]{1,0:T(8,128)S(1)}, u32[]{:S(2)}, u32[]{:S(2)}) collective-permute-start(f32[264,128]{1,0:T(8,128)S(1)} %get-tuple-element.12), channel_id=1, source_target_pairs={{0,16},{8,248},{16,32},{24,8},{32,48},{40,24},{48,64},{56,40},{64,... | collective-permute-start | bytes 405512 | tf_op jit(solution)/shard_map/ppermute | solution.py:283
  57.5 8.0 %collective-permute-done.3.h_ref = f32[264,128]{1,0:T(8,128)S(1)} collective-permute-done((f32[264,128]{1,0:T(8,128)S(1)}, f32[264,128]{1,0:T(8,128)S(1)}, u32[]{:S(2)}, u32[]{:S(2)}) %collective-permute-start.3) | collective-permute-done | bytes 135200 | tf_op jit(solution)/shard_map/ppermute | solution.py:283
  65.4 0.0 collective-permute-done.a_ref
  65.4 0.0 collective-permute-done.1.b_ref
  65.4 0.0 collective-permute-done.2.c_ref
  65.4 0.0 copy-done.3
  65.4 0.0 copy-done.4
  65.4 0.0 copy-start.5
  65.5 0.9 copy-done.5
  66.4 3.2 %spectra.1 = f32[520,128]{1,0:T(8,128)S(1)} custom-call(f32[520,128]{1,0:T(8,128)S(1)} %get-tuple-element.8.o_ref, f32[520,128]{1,0:T(8,128)S(1)} %collective-permute-done.a_ref, f32[520,128]{1,0:T(8,128)S(1)} %collective-permute-done.1.b_ref, f32[520,128]{1,0:T(8,128)S(1)} %collective-permute-done.2.c_ref, f32[264,128]{1,0:T(8,128)S(1)} %collective-permute-done.3.h_ref, ...), custom_call_target="tpu_custom_call" | custom-call | flops 4000000000 | bytes 4000000 | tf_op jit(solution)/shard_map/spectra/pallas_call | solution.py:291
  69.6 32.2 %all_to_all.10 = f32[8,1,8320]{2,1,0:T(1,128)S(1)} all-to-all(f32[8,1,8320]{2,1,0:T(1,128)S(1)} %bitcast.14), channel_id=1, replica_groups={{0,32,64,96,128,160,192,224},{8,40,72,104,136,168,200,232},{16,48,80,11..., dimensions={0} | all-to-all | bytes 532480 | tf_op jit(solution)/shard_map/all_to_all | solution.py:302
  101.8 0.0 copy-start.2
  101.8 0.7 copy-done.2
  102.5 0.6 join.1
  103.1 30.8 %all_to_all.11 = f32[32,1,2304]{2,1,0:T(1,128)S(1)} all-to-all(f32[32,1,2304]{2,1,0:T(1,128)S(1)} %bitcast.10), channel_id=1, replica_groups={{0,1,2,3,4,5,6,7,8,9,10,11,12,13,14,15,16,17,18,19,20,21,22,23,24,25,26..., dimensions={0} | all-to-all | bytes 589824 | tf_op jit(solution)/shard_map/all_to_all | solution.py:320
  133.9 0.8 finish.1
Async XLA Ops:
  0.6 0.7 copy-start.1
  1.3 1.2 copy-start
  2.5 62.9 %copy-start.3 = (bf16[288,768]{1,0:T(8,128)(2,1)S(1)}, bf16[288,768]{1,0:T(8,128)(2,1)}, u32[]{:S(2)}) copy-start(bf16[288,768]{1,0:T(8,128)(2,1)} %constant.6.clone.f_ref) | copy-start | bytes 1327108
  2.5 62.9 %copy-start.4 = (bf16[768,256]{1,0:T(8,128)(2,1)S(1)}, bf16[768,256]{1,0:T(8,128)(2,1)}, u32[]{:S(2)}) copy-start(bf16[768,256]{1,0:T(8,128)(2,1)} %constant.7.clone.w_ref) | copy-start | bytes 1179652
  3.4 62.1 %collective-permute-start = (f32[520,128]{1,0:T(8,128)S(1)}, f32[520,128]{1,0:T(8,128)S(1)}, u32[]{:S(2)}, u32[]{:S(2)}) collective-permute-start(f32[520,128]{1,0:T(8,128)S(1)} %get-tuple-element.9), channel_id=1, source_target_pairs={{0,8},{8,16},{16,24},{24,32},{32,40},{40,48},{48,56},{56,64},{64,7... | collective-permute-start | bytes 798728 | tf_op jit(solution)/shard_map/ppermute | solution.py:283
  8.6 56.8 %collective-permute-start.1 = (f32[520,128]{1,0:T(8,128)S(1)}, f32[520,128]{1,0:T(8,128)S(1)}, u32[]{:S(2)}, u32[]{:S(2)}) collective-permute-start(f32[520,128]{1,0:T(8,128)S(1)} %get-tuple-element.10), channel_id=1, source_target_pairs={{0,248},{8,0},{16,8},{24,16},{32,24},{40,32},{48,40},{56,48},{64,5... | collective-permute-start | bytes 798728 | tf_op jit(solution)/shard_map/ppermute | solution.py:283
  51.2 14.2 %collective-permute-start.2 = (f32[520,128]{1,0:T(8,128)S(1)}, f32[520,128]{1,0:T(8,128)S(1)}, u32[]{:S(2)}, u32[]{:S(2)}) collective-permute-start(f32[520,128]{1,0:T(8,128)S(1)} %get-tuple-element.11), channel_id=1, source_target_pairs={{0,240},{8,24},{16,0},{24,40},{32,16},{40,56},{48,32},{56,72},{64,... | collective-permute-start | bytes 798728 | tf_op jit(solution)/shard_map/ppermute | solution.py:283
  54.3 11.1 %collective-permute-start.3 = (f32[264,128]{1,0:T(8,128)S(1)}, f32[264,128]{1,0:T(8,128)S(1)}, u32[]{:S(2)}, u32[]{:S(2)}) collective-permute-start(f32[264,128]{1,0:T(8,128)S(1)} %get-tuple-element.12), channel_id=1, source_target_pairs={{0,16},{8,248},{16,32},{24,8},{32,48},{40,24},{48,64},{56,40},{64,... | collective-permute-start | bytes 405512 | tf_op jit(solution)/shard_map/ppermute | solution.py:283
  65.4 1.0 copy-start.5
  101.8 0.7 copy-start.2

commit v4 on v1

v4 whole, which is shorter than its diff:
```python
import functools
import math

import jax
import jax.numpy as jnp
import numpy as np
from jax import lax
from jax.experimental import pallas as pl
from jax.experimental.pallas import tpu as pltpu
from jax.sharding import PartitionSpec as P

LA = 256
LB = 128
BLOCKS = 8
SEG = LA * LB
GROUP = 4
ROWS = 144
LANES = 128


def split(x):
    high = x.astype(jnp.bfloat16)
    return high, (x - high.astype(jnp.float32)).astype(jnp.bfloat16)


def owners(shards, role):
    return [
        GROUP * (2 * m + (role + r) % 2) + r
        for m in range(shards // GROUP // 2)
        for r in range(GROUP)
    ]


@functools.lru_cache
def tables(shards):
    k1 = np.arange(ROWS)[:, None]
    angle = 2 * math.pi * ((k1 * np.arange(LA)[None, :]) % LA) / LA
    live = k1 <= LA // 2
    first = np.concatenate([np.cos(angle) * live, -np.sin(angle) * live], axis=0)
    angle = 2 * math.pi * (k1 * np.arange(LB)[None, :]) / SEG
    scale = math.sqrt(1.0 / (0.375 * SEG)) * live
    twiddle = np.cos(angle) * scale, -np.sin(angle) * scale
    own = LB // 2 // shards
    roles = [owners(shards, role) for role in range(2)]
    k2 = [
        k
        for d in map(np.array, roles)
        for k in [own * d + e for e in range(own)] + [LB - 1 - own * d - e for e in range(own)]
    ]
    k2 = np.concatenate(k2)[None, :]
    angle = 2 * math.pi * ((np.arange(LB)[:, None] * k2) % LB) / LB
    c, s = np.cos(angle), -np.sin(angle)
    second = np.concatenate([np.concatenate([c, s], 1), np.concatenate([-s, c], 1)], 0)
    n = np.arange(SEG)
    window = (0.5 - 0.5 * np.cos(2 * math.pi * n / SEG)).reshape(LA, LB)
    halves = [x[:, at : at + LANES] for x in (first, second) for at in (0, LANES)]
    return np.concatenate([*twiddle, window, *halves], axis=0).astype(np.float32)


def pack_kernel(per, mask_ref, assign_ref, x_ref, *refs):
    o_ref, a_ref, b_ref, c_ref, h_ref, ids_ref = refs
    me = lax.axis_index("tm")
    channels = GROUP * per
    rows = x_ref.shape[0] // channels
    half = rows // 2
    even = lax.rem(me, 2) == 0
    for c in range(channels):
        ids_ref[c : c + 1, :] = jnp.full((1, LANES), assign_ref[c].astype(jnp.float32))

    def masks(ref, at, first):
        ref[at : at + 8, :] = jnp.zeros((8, LANES), jnp.float32)
        for c in range(per):
            for s in range(2):
                value = mask_ref[s, first + c].astype(jnp.float32)
                ref[at + 2 * c + s : at + 2 * c + s + 1, :] = jnp.full((1, LANES), value)

    for ref, shift in ((c_ref, 2), (a_ref, 1), (b_ref, GROUP - 1), (o_ref, 0)):
        first = per * lax.rem(me + shift, GROUP)
        for c in range(per):
            ref[c * rows : (c + 1) * rows, :] = x_ref[pl.ds(first + c, rows, stride=channels), :]
        masks(ref, per * rows, first)
    first = per * lax.rem(me + 2, GROUP)
    start = jnp.where(even, half * channels, 0)
    for c in range(per):
        h_ref[c * half : (c + 1) * half, :] = x_ref[
            pl.ds(start + first + c, half, stride=channels), :
        ]
    masks(h_ref, per * half, first)


def spectra_kernel(per, shards, *refs):
    o_ref, a_ref, b_ref, c_ref, h_ref, t_ref, keep_ref, send_ref, f_ref, w_ref = refs
    at = 2 * ROWS + LA
    side = t_ref[at : at + 2 * ROWS, :], t_ref[at + 2 * ROWS : at + 4 * ROWS, :]
    high, low = split(jnp.concatenate(side, axis=1))
    f_ref[...] = jnp.concatenate([high, high, low], axis=1)
    at += 4 * ROWS
    side = t_ref[at : at + 2 * LB, :], t_ref[at + 2 * LB :, :]
    high, low = split(jnp.concatenate(side, axis=1))
    w_ref[...] = jnp.concatenate([high, high, low], axis=0)
    me = lax.axis_index("tm")
    even = lax.rem(me, 2) == 0
    role = lax.rem(me // GROUP + lax.rem(me, GROUP), 2)
    rows = (o_ref.shape[0] - 8) // per
    half = rows // 2
    dests = shards // 2
    parts = LB // shards
    lines = 2 * parts * per
    starts_a = jnp.where(me == 1, 0.0, 1.0)
    starts_o = jnp.where(me == 0, 0.0, 1.0)
    starts_b = jnp.where(me == shards - 1, 0.0, 1.0)
    starts_y = jnp.where(me == shards - 2, 0.0, 1.0)
    lane = lax.broadcasted_iota(jnp.int32, (1, LANES), 1)
    swap = (lax.broadcasted_iota(jnp.int32, (8, LANES), 0) == 0) & (
        lax.rem(lax.broadcasted_iota(jnp.int32, (8, LANES), 1), LB // 2) >= LB // 4
    )

    def one_channel(c, carry):
        base = pl.multiple_of(c * rows, rows)

        def halves(ref):
            return ref[pl.ds(base, half), :], ref[pl.ds(base + half, half), :]

        def weight(ref, s, at=per * rows):
            return ref[pl.ds(at + 2 * c + s, 1), :]

        o0, o1 = halves(o_ref)
        a0, a1 = halves(a_ref)
        b0, b1 = halves(b_ref)
        c0, c1 = halves(c_ref)
        h = h_ref[pl.ds(pl.multiple_of(c * half, half), half), :]
        x = jnp.where(even, h, c1)
        y = jnp.where(even, c0, h)
        x_weight = jnp.where(even, weight(h_ref, 1, per * half), weight(c_ref, 1))
        pairs = (
            ((o0, o1, None, weight(o_ref, 0)), (o1, b0, starts_b, weight(o_ref, 1))),
            ((a0, a1, None, weight(a_ref, 0)), (a1, o0, starts_o, weight(a_ref, 1))),
            ((b0, b1, None, weight(b_ref, 0)), (b1, y, starts_y, weight(b_ref, 1))),
            ((c0, c1, None, weight(c_ref, 0)), (x, a0, starts_a, x_weight)),
        )
        window = t_ref[2 * ROWS : 2 * ROWS + LA, :]
        peak = log_sum = None
        for pair in pairs:
            framed = []
            for head, tail, live, _ in pair:
                tail = tail * window[half:]
                if live is not None:
                    tail = tail * live
                framed.append(jnp.concatenate([head * window[:half], tail], axis=0))
            high, low = split(jnp.concatenate(framed, axis=1))
            mid = jnp.dot(
                f_ref[...],
                jnp.concatenate([high, low, high], axis=0),
                preferred_element_type=jnp.float32,
            )
            cosine, sine = t_ref[:ROWS, :], t_ref[ROWS : 2 * ROWS, :]
            turned = []
            for s in range(2):
                re = mid[:ROWS, s * LB : (s + 1) * LB]
                im = mid[ROWS:, s * LB : (s + 1) * LB]
                turned.append(
                    jnp.concatenate([re * cosine - im * sine, re * sine + im * cosine], axis=1)
                )
            high, low = split(jnp.concatenate(turned, axis=0))
            out = jnp.dot(
                jnp.concatenate([high, low, high], axis=1),
                w_ref[...],
                preferred_element_type=jnp.float32,
            )
            powers = out[:, :LB] * out[:, :LB] + out[:, LB:] * out[:, LB:]
            for s in range(2):
                mine = powers[s * ROWS : (s + 1) * ROWS]
                first = jnp.where(swap, mine[LA // 2 : LA // 2 + 8], mine[:8])
                mine = jnp.concatenate([first, mine[8 : LA // 2]], axis=0)
                keep = pair[s][3]
                kept_power = keep * mine
                kept_log = keep * jnp.log(0.25 + mine)
                peak = kept_power if peak is None else jnp.maximum(peak, kept_power)
                log_sum = kept_log if log_sum is None else log_sum + kept_log
        for kind, value in enumerate((peak, log_sum)):
            turned = jnp.transpose(value)
            for ref, mine in ((keep_ref, 0), (send_ref, 1)):
                chosen = jnp.where(role == mine, turned[: LB // 2], turned[LB // 2 :])
                for i in range(parts):
                    at = (kind * parts + i) * per + c
                    ref[pl.ds(at, dests, stride=lines + 1), :] = chosen[
                        i * dests : (i + 1) * dests
                    ]
        kept = sum(w for pair in pairs for _, _, _, w in pair)
        return jnp.where(lane == c, kept, carry)

    kept = lax.fori_loop(0, per, one_channel, jnp.zeros((1, LANES), jnp.float32))
    for ref in (keep_ref, send_ref):
        ref[pl.ds(lines, dests, stride=lines + 1), :] = jnp.broadcast_to(kept, (dests, LANES))


def join_kernel(lines, mine_ref, other_ref, out_ref):
    mine, other = mine_ref[...], other_ref[...]
    line = lax.rem(lax.broadcasted_iota(jnp.int32, mine.shape, 0), lines)
    out_ref[...] = jnp.where(line < lines // 2, jnp.maximum(mine, other), mine + other)


def finish_kernel(per, ids_ref, z_ref, peak_ref, log_ref, part_ref):
    channels, bins = log_ref.shape
    parts = bins // LANES
    own = parts // 2
    size = parts * per
    step = 2 * size + 1
    sources = z_ref.shape[0] // step
    lane = lax.broadcasted_iota(jnp.int32, (channels, LANES), 1)
    line = lax.broadcasted_iota(jnp.int32, (channels, LANES), 0)
    back = jnp.where(lane == 0, 0, LANES - lane)

    def joined(r, at, count, op):
        total = None
        for s in range(r, sources, GROUP):
            term = z_ref[s * step + at : s * step + at + count, :]
            total = term if total is None else op(total, term)
        return total

    def in_order(kind, op):
        sets = [joined(r, kind * size, size, op) for r in range(GROUP)]
        pieces = []
        for e in range(own):
            for i, mirrored in ((e, False), (own + e, True)):
                piece = jnp.concatenate([t[i * per : (i + 1) * per] for t in sets], axis=0)
                if mirrored:
                    piece = jnp.take_along_axis(piece, back, axis=1)
                pieces.append(piece)
        return jnp.concatenate(pieces, axis=1)

    kept = jnp.zeros((channels, LANES), jnp.float32)
    for r in range(GROUP):
        row = joined(r, 2 * size, 1, jnp.add)
        kept = jnp.where((line - per * r == lane) & (lane < per), row, kept)
    log_mean = in_order(1, jnp.add) / jnp.sum(kept, axis=1, keepdims=True)
    log_ref[...] = log_mean
    peak_ref[...] = in_order(0, jnp.maximum)
    block = lax.broadcasted_iota(jnp.int32, (BLOCKS, LANES), 0).astype(jnp.float32)
    inside = [block == ids_ref[c : c + 1, :] for c in range(channels)]
    for i in range(parts + 1):
        total = jnp.zeros((BLOCKS, LANES), jnp.float32)
        for c in range(channels):
            term = log_mean[c : c + 1, i * LANES : (i + 1) * LANES] if i < parts else 1.0
            total = total + jnp.where(inside[c], term, 0.0)
        for p in range(part_ref.shape[0]):
            part_ref[p, i * BLOCKS : (i + 1) * BLOCKS, :] = total


def blocks_kernel(parts_ref, out_ref):
    total = parts_ref[0]
    for p in range(1, parts_ref.shape[0]):
        total = total + parts_ref[p]
    counts = total[-BLOCKS:]
    for i in range(out_ref.shape[1] // LANES):
        out_ref[:, i * LANES : (i + 1) * LANES] = total[i * BLOCKS : (i + 1) * BLOCKS] / counts


VMEM = pl.BlockSpec(memory_space=pltpu.VMEM)
SMEM = pl.BlockSpec(memory_space=pltpu.SMEM)
PARAMS = pltpu.CompilerParams(vmem_limit_bytes=48 * 1024 * 1024)


def f32(*shape):
    return jax.ShapeDtypeStruct(shape, jnp.float32)


def on_device(signal, gap_mask, assignment):
    channels, local_time = signal.shape
    shards = lax.axis_size("tm")
    per = channels // GROUP
    rows = local_time // LANES
    bins = SEG // 2 // shards

    lined = signal.reshape(channels, rows, LANES).transpose(1, 0, 2).reshape(-1, LANES)
    whole, small = per * rows + 8, per * rows // 2 + 8
    o, a, b, c, h, ids = pl.pallas_call(
        functools.partial(pack_kernel, per),
        out_shape=[f32(whole, LANES)] * 4 + [f32(small, LANES), f32(channels, LANES)],
        in_specs=[SMEM, SMEM, VMEM],
        out_specs=[VMEM] * 6,
        compiler_params=PARAMS,
        name="pack",
    )(gap_mask.T, assignment, lined)

    def moved(x, by):
        return lax.ppermute(x, "tm", [(i, (i + by(i)) % shards) for i in range(shards)])

    a = moved(a, lambda i: 1)
    b = moved(b, lambda i: -1)
    c = moved(c, lambda i: 2 if i % 2 else -2)
    h = moved(h, lambda i: -2 if i % 2 else 2)

    dests = shards // 2
    lines = 2 * (bins // LANES) * per + 1
    keep, send = pl.pallas_call(
        functools.partial(spectra_kernel, per, shards),
        out_shape=[f32(dests * lines, LANES)] * 2,
        in_specs=[VMEM] * 6,
        out_specs=[VMEM] * 2,
        scratch_shapes=[
            pltpu.VMEM((2 * ROWS, 3 * LA), jnp.bfloat16),
            pltpu.VMEM((6 * LB, 2 * LB), jnp.bfloat16),
        ],
        compiler_params=PARAMS,
        cost_estimate=pl.CostEstimate(
            flops=4_000_000_000, bytes_accessed=4_000_000, transcendentals=300_000
        ),
        name="spectra",
    )(o, a, b, c, h, tables(shards))
    roles = [owners(shards, role) for role in range(2)]
    other = moved(send, lambda i: GROUP if i in roles[0] else -GROUP)
    sums = pl.pallas_call(
        functools.partial(join_kernel, lines),
        out_shape=f32(dests * lines, LANES),
        in_specs=[VMEM] * 2,
        out_specs=VMEM,
        compiler_params=PARAMS,
        name="join",
    )(keep, other)
    sums = lax.all_to_all(
        sums.reshape(dests, 1, -1), "tm", 0, 0, tiled=True, axis_index_groups=roles
    )
    peers = lax.axis_size(("chan", "sub"))
    peak_hold, log_mean, part = pl.pallas_call(
        functools.partial(finish_kernel, per),
        out_shape=[
            f32(channels, bins),
            f32(channels, bins),
            f32(peers, (bins // LANES + 1) * BLOCKS, LANES),
        ],
        in_specs=[VMEM] * 2,
        out_specs=[VMEM] * 3,
        compiler_params=PARAMS,
        name="finish",
    )(ids, sums.reshape(-1, LANES))
    part = lax.all_to_all(part, ("chan", "sub"), 0, 0, tiled=True)
    block_mean = pl.pallas_call(
        blocks_kernel,
        out_shape=f32(BLOCKS, bins),
        in_specs=[VMEM],
        out_specs=VMEM,
        compiler_params=PARAMS,
        name="blocks",
    )(part)
    return peak_hold, log_mean, block_mean


def solution(mesh):
    in_specs = (
        P(("grp", "chan", "sub"), "tm"),
        P(("grp", "chan", "sub"), "tm"),
        P(("grp", "chan", "sub")),
    )
    out_specs = (P(("grp", "chan", "sub"), "tm"), P(("grp", "chan", "sub"), "tm"), P("grp", "tm"))
    return jax.shard_map(
        on_device, mesh=mesh, in_specs=in_specs, out_specs=out_specs, check_vma=False
    )
```

time: 147 us -> 130 us (0.88)
  blocking collectives: 57.7 us -> 45.7 us
  starting transfers between devices: 61.8 us -> 56 us
  waiting for transfers between devices: 16.5 us -> 19.4 us
  local copies, waits for them, and re-layouts: 3.54 us -> 1.89 us
    ppermute x4 -> x5, waiting for transfers between devices: 0.4 us -> 19.4 us  [moved(): lax.ppermute(x, 'tm', [(i, (i + by(i)) % shards) for i in range(shards)])]
    all_to_all x1 -> x0, waiting for transfers between devices: 16.1 us -> none  [on_device(): cnt = lax.all_to_all(cnt, 'tm', 0, 0, tiled=True)]
    all_to_all x1, blocking collectives: 42 us -> 30.5 us  [on_device(): lax.all_to_all(sums.reshape(dests, 1, -1), 'tm', 0, 0, tiled=True, axis_i...]
    all_to_all x1 -> x0, starting transfers between devices: 8.91 us -> none  [on_device(): cnt = lax.all_to_all(cnt, 'tm', 0, 0, tiled=True)]
    ppermute x4 -> x5, starting transfers between devices: 52.9 us -> 56 us  [moved(): lax.ppermute(x, 'tm', [(i, (i + by(i)) % shards) for i in range(shards)])]
    unnamed x13 -> x8, local copies, waits for them, and re-layouts: 3.54 us -> 1.89 us
  transfers between devices with their start and end apart: 5 -> 5, of which waited for: 2 -> 2; matrix products, arithmetic and copies ran while one was open for 0% -> 0% of each run, Pallas kernels for 2% -> 0%
where the time goes in v4:
time: 130 us; the launch traced here: 129 us
  starting transfers between devices  56 us (43%)
  blocking collectives  45.7 us (35%)
  waiting for transfers between devices  19.4 us (15%)
  Pallas kernels  5.4 us (4%)
  local copies, waits for them, and re-layouts  1.89 us (1%)
    ppermute x5, starting transfers between devices, moved(): lax.ppermute(x, 'tm', [(i, (i + by(i)) % shards) for i in range(shards)])  56 us
    all_to_all x1, blocking collectives, on_device(): lax.all_to_all(sums.reshape(dests, 1, -1), 'tm', 0, 0, tiled=True, axis_i...  30.5 us
    ppermute x5, waiting for transfers between devices, moved(): lax.ppermute(x, 'tm', [(i, (i + by(i)) % shards) for i in range(shards)])  19.4 us
    all_to_all x1, blocking collectives, on_device(): part = lax.all_to_all(part, ('chan', 'sub'), 0, 0, tiled=True)  15.3 us
    pallas_call x1, Pallas kernels, on_device(): pl.pallas_call(functools.partial(spectra_kernel, per, shards), out_shape=...  3.21 us
  transfers between devices with their start and end apart: 5, of which 2 were waited for; matrix products, arithmetic and copies ran while one was open for 0% of the time, Pallas kernels for 0%

profile of v4, /device:TPU:33, one launch (start us, length us, event | category | flops | bytes accessed | tf_op | source)
XLA Modules:
  0.0 129.2 jit_solution(12238111793270041928)
XLA Ops:
  0.6 0.0 copy-start.1
  0.6 0.0 copy-start.2
  0.7 0.7 copy-done.1
  1.3 0.0 copy-done.2
  1.3 0.0 copy-start
  1.3 1.2 copy-done
  2.5 0.0 copy-start.3
  2.5 0.8 pack.1
  3.4 5.3 %collective-permute-start = (f32[520,128]{1,0:T(8,128)S(1)}, f32[520,128]{1,0:T(8,128)S(1)}, u32[]{:S(2)}, u32[]{:S(2)}) collective-permute-start(f32[520,128]{1,0:T(8,128)S(1)} %get-tuple-element.16), channel_id=1, source_target_pairs={{0,8},{8,16},{16,24},{24,32},{32,40},{40,48},{48,56},{56,64},{64,7... | collective-permute-start | bytes 798728 | tf_op jit(solution)/shard_map/ppermute | solution.py:287
  8.6 42.6 %collective-permute-start.1 = (f32[520,128]{1,0:T(8,128)S(1)}, f32[520,128]{1,0:T(8,128)S(1)}, u32[]{:S(2)}, u32[]{:S(2)}) collective-permute-start(f32[520,128]{1,0:T(8,128)S(1)} %get-tuple-element.17), channel_id=1, source_target_pairs={{0,248},{8,0},{16,8},{24,16},{32,24},{40,32},{48,40},{56,48},{64,5... | collective-permute-start | bytes 798728 | tf_op jit(solution)/shard_map/ppermute | solution.py:287
  51.2 3.1 %collective-permute-start.2 = (f32[520,128]{1,0:T(8,128)S(1)}, f32[520,128]{1,0:T(8,128)S(1)}, u32[]{:S(2)}, u32[]{:S(2)}) collective-permute-start(f32[520,128]{1,0:T(8,128)S(1)} %get-tuple-element.18), channel_id=1, source_target_pairs={{0,240},{8,24},{16,0},{24,40},{32,16},{40,56},{48,32},{56,72},{64,... | collective-permute-start | bytes 798728 | tf_op jit(solution)/shard_map/ppermute | solution.py:287
  54.3 3.1 %collective-permute-start.3 = (f32[264,128]{1,0:T(8,128)S(1)}, f32[264,128]{1,0:T(8,128)S(1)}, u32[]{:S(2)}, u32[]{:S(2)}) collective-permute-start(f32[264,128]{1,0:T(8,128)S(1)} %get-tuple-element.19), channel_id=1, source_target_pairs={{0,16},{8,248},{16,32},{24,8},{32,48},{40,24},{48,64},{56,40},{64,... | collective-permute-start | bytes 405512 | tf_op jit(solution)/shard_map/ppermute | solution.py:287
  57.5 7.9 %collective-permute-done.3.refs_4_ = f32[264,128]{1,0:T(8,128)S(1)} collective-permute-done((f32[264,128]{1,0:T(8,128)S(1)}, f32[264,128]{1,0:T(8,128)S(1)}, u32[]{:S(2)}, u32[]{:S(2)}) %collective-permute-start.3) | collective-permute-done | bytes 135200 | tf_op jit(solution)/shard_map/ppermute | solution.py:287
  65.4 0.0 collective-permute-done.refs_1_
  65.4 0.0 collective-permute-done.1.refs_2_
  65.4 0.0 collective-permute-done.2.refs_3_
  65.4 0.0 copy-done.3
  65.4 3.2 %spectra.1 = (f32[272,128]{1,0:T(8,128)S(1)}, f32[272,128]{1,0:T(8,128)S(1)}) custom-call(f32[520,128]{1,0:T(8,128)S(1)} %get-tuple-element.15.refs_0_, f32[520,128]{1,0:T(8,128)S(1)} %collective-permute-done.refs_1_, f32[520,128]{1,0:T(8,128)S(1)} %collective-permute-done.1.refs_2_, f32[520,128]{1,0:T(8,128)S(1)} %collective-permute-done.2.refs_3_, ...), custom_call_target="tpu_custom_call" | custom-call | flops 4000000000 | bytes 4000000 | tf_op jit(solution)/shard_map/spectra/pallas_call | solution.py:296
  68.6 2.0 %collective-permute-start.4 = (f32[272,128]{1,0:T(8,128)S(1)}, f32[272,128]{1,0:T(8,128)S(1)}, u32[]{:S(2)}, u32[]{:S(2)}) collective-permute-start(f32[272,128]{1,0:T(8,128)S(1)} %get-tuple-element.21), channel_id=1, source_target_pairs={{0,32},{8,232},{16,48},{24,248},{32,0},{40,72},{48,16},{56,88},{64... | collective-permute-start | bytes 417800 | tf_op jit(solution)/shard_map/ppermute | solution.py:287
  70.6 11.4 %collective-permute-done.4.other_ref = f32[272,128]{1,0:T(8,128)S(1)} collective-permute-done((f32[272,128]{1,0:T(8,128)S(1)}, f32[272,128]{1,0:T(8,128)S(1)}, u32[]{:S(2)}, u32[]{:S(2)}) %collective-permute-start.4) | collective-permute-done | bytes 139296 | tf_op jit(solution)/shard_map/ppermute | solution.py:287
  82.0 0.1 join.1
  82.1 30.5 %all_to_all.10 = f32[16,1,2176]{2,1,0:T(1,128)S(1)} all-to-all(f32[16,1,2176]{2,1,0:T(1,128)S(1)} %bitcast.10), channel_id=1, replica_groups={{0,40,16,56,64,104,80,120,128,168,144,184,192,232,208,248},{32,8,48,24,..., dimensions={0} | all-to-all | bytes 278528 | tf_op jit(solution)/shard_map/all_to_all | solution.py:321
  112.6 0.7 finish.1
  113.3 15.3 %all_to_all.11.parts_ref = f32[8,40,128]{2,1,0:T(8,128)S(1)} all-to-all(f32[8,40,128]{2,1,0:T(8,128)S(1)} %get-tuple-element.24), channel_id=1, replica_groups=mesh['grp'=2,'tm'=32,'chan'=4,'sub'=2] {'chan','sub'}, dimensions={0} | all-to-all | bytes 327680 | tf_op jit(solution)/shard_map/all_to_all | solution.py:337
  128.5 0.6 blocks.1
Async XLA Ops:
  0.6 0.7 copy-start.1
  0.6 0.7 copy-start.2
  1.3 1.2 copy-start
  2.5 62.9 %copy-start.3 = (f32[1632,128]{1,0:T(8,128)S(1)}, f32[1632,128]{1,0:T(8,128)}, u32[]{:S(2)}) copy-start(f32[1632,128]{1,0:T(8,128)} %constant.2.clone.refs_5_) | copy-start | bytes 2506756
  3.4 62.1 %collective-permute-start = (f32[520,128]{1,0:T(8,128)S(1)}, f32[520,128]{1,0:T(8,128)S(1)}, u32[]{:S(2)}, u32[]{:S(2)}) collective-permute-start(f32[520,128]{1,0:T(8,128)S(1)} %get-tuple-element.16), channel_id=1, source_target_pairs={{0,8},{8,16},{16,24},{24,32},{32,40},{40,48},{48,56},{56,64},{64,7... | collective-permute-start | bytes 798728 | tf_op jit(solution)/shard_map/ppermute | solution.py:287
  8.6 56.8 %collective-permute-start.1 = (f32[520,128]{1,0:T(8,128)S(1)}, f32[520,128]{1,0:T(8,128)S(1)}, u32[]{:S(2)}, u32[]{:S(2)}) collective-permute-start(f32[520,128]{1,0:T(8,128)S(1)} %get-tuple-element.17), channel_id=1, source_target_pairs={{0,248},{8,0},{16,8},{24,16},{32,24},{40,32},{48,40},{56,48},{64,5... | collective-permute-start | bytes 798728 | tf_op jit(solution)/shard_map/ppermute | solution.py:287
  51.2 14.2 %collective-permute-start.2 = (f32[520,128]{1,0:T(8,128)S(1)}, f32[520,128]{1,0:T(8,128)S(1)}, u32[]{:S(2)}, u32[]{:S(2)}) collective-permute-start(f32[520,128]{1,0:T(8,128)S(1)} %get-tuple-element.18), channel_id=1, source_target_pairs={{0,240},{8,24},{16,0},{24,40},{32,16},{40,56},{48,32},{56,72},{64,... | collective-permute-start | bytes 798728 | tf_op jit(solution)/shard_map/ppermute | solution.py:287
  54.3 11.1 %collective-permute-start.3 = (f32[264,128]{1,0:T(8,128)S(1)}, f32[264,128]{1,0:T(8,128)S(1)}, u32[]{:S(2)}, u32[]{:S(2)}) collective-permute-start(f32[264,128]{1,0:T(8,128)S(1)} %get-tuple-element.19), channel_id=1, source_target_pairs={{0,16},{8,248},{16,32},{24,8},{32,48},{40,24},{48,64},{56,40},{64,... | collective-permute-start | bytes 405512 | tf_op jit(solution)/shard_map/ppermute | solution.py:287
  68.6 13.4 %collective-permute-start.4 = (f32[272,128]{1,0:T(8,128)S(1)}, f32[272,128]{1,0:T(8,128)S(1)}, u32[]{:S(2)}, u32[]{:S(2)}) collective-permute-start(f32[272,128]{1,0:T(8,128)S(1)} %get-tuple-element.21), channel_id=1, source_target_pairs={{0,32},{8,232},{16,48},{24,248},{32,0},{40,72},{48,16},{56,88},{64... | collective-permute-start | bytes 417800 | tf_op jit(solution)/shard_map/ppermute | solution.py:287

commit v5 on v4

--- a/solution.py
+++ b/solution.py
@@ -8,6 +8,7 @@
 from jax.experimental import pallas as pl
 from jax.experimental.pallas import tpu as pltpu
 from jax.sharding import PartitionSpec as P
+
 
 LA = 256
 LB = 128
@@ -88,8 +89,51 @@
     masks(h_ref, per * half, first)
 
 
+def powers_of(frames, t_ref, f_ref, w_ref):
+    swap = (lax.broadcasted_iota(jnp.int32, (8, LANES), 0) == 0) & (
+        lax.rem(lax.broadcasted_iota(jnp.int32, (8, LANES), 1), LB // 2) >= LB // 4
+    )
+    window = t_ref[2 * ROWS : 2 * ROWS + LA, :]
+    framed = []
+    for head, tail, live in frames:
+        half = head.shape[0]
+        tail = tail * window[half:]
+        if live is not None:
+            tail = tail * live
+        framed.append(jnp.concatenate([head * window[:half], tail], axis=0))
+    high, low = split(jnp.concatenate(framed, axis=1))
+    mid = jnp.dot(
+        f_ref[...],
+        jnp.concatenate([high, low, high], axis=0),
+        preferred_element_type=jnp.float32,
+    )
+    cosine, sine = t_ref[:ROWS, :], t_ref[ROWS : 2 * ROWS, :]
+    turned = []
+    for s in range(2):
+        re = mid[:ROWS, s * LB : (s + 1) * LB]
+        im = mid[ROWS:, s * LB : (s + 1) * LB]
+        turned.append(jnp.concatenate([re * cosine - im * sine, re * sine + im * cosine], axis=1))
+    high, low = split(jnp.concatenate(turned, axis=0))
+    out = jnp.dot(
+        jnp.concatenate([high, low, high], axis=1),
+        w_ref[...],
+        preferred_element_type=jnp.float32,
+    )
+    powers = out[:, :LB] * out[:, :LB] + out[:, LB:] * out[:, LB:]
+    both = []
+    for s in range(2):
+        mine = powers[s * ROWS : (s + 1) * ROWS]
+        first = jnp.where(swap, mine[LA // 2 : LA // 2 + 8], mine[:8])
+        both.append(jnp.concatenate([first, mine[8 : LA // 2]], axis=0))
+    return both
+
+
+def live(me, ahead, shards):
+    return jnp.where(lax.rem(me + ahead + shards, shards) == 0, 0.0, 1.0)
+
+
 def spectra_kernel(per, shards, *refs):
-    o_ref, a_ref, b_ref, c_ref, h_ref, t_ref, keep_ref, send_ref, f_ref, w_ref = refs
+    o_ref, a_ref, b_ref, c_ref, t_ref, peak_ref, log_ref, kept_ref, f_ref, w_ref = refs
     at = 2 * ROWS + LA
     side = t_ref[at : at + 2 * ROWS, :], t_ref[at + 2 * ROWS : at + 4 * ROWS, :]
     high, low = split(jnp.concatenate(side, axis=1))
@@ -100,96 +144,98 @@
     w_ref[...] = jnp.concatenate([high, high, low], axis=0)
     me = lax.axis_index("tm")
     even = lax.rem(me, 2) == 0
+    rows = (o_ref.shape[0] - 8) // per
+    half = rows // 2
+
+    def weight(ref, c, s):
+        return ref[pl.ds(per * rows + 2 * c + s, 1), :]
+
+    def one_channel(c, carry):
+        base = pl.multiple_of(c * rows, rows)
+
+        def halves(ref):
+            return ref[pl.ds(base, half), :], ref[pl.ds(base + half, half), :]
+
+        o0, o1 = halves(o_ref)
+        a0, a1 = halves(a_ref)
+        b0, b1 = halves(b_ref)
+        c0, c1 = halves(c_ref)
+        pairs = (
+            ((c0, c1, None, weight(c_ref, c, 0)), (o0, o1, None, weight(o_ref, c, 0))),
+            ((a0, a1, None, weight(a_ref, c, 0)), (a1, o0, live(me, 0, shards), weight(a_ref, c, 1))),
+            ((o1, b0, live(me, 1, shards), weight(o_ref, c, 1)), (b0, b1, None, weight(b_ref, c, 0))),
+        )
+        peak = log_sum = None
+        for pair in pairs:
+            powers = powers_of([segment[:3] for segment in pair], t_ref, f_ref, w_ref)
+            for power, (_, _, _, keep) in zip(powers, pair):
+                kept_log = keep * jnp.log(0.25 + power)
+                peak = keep * power if peak is None else jnp.maximum(peak, keep * power)
+                log_sum = kept_log if log_sum is None else log_sum + kept_log
+        at = pl.multiple_of(c * LANES, LANES)
+        peak_ref[pl.ds(at, LANES), :] = peak
+        log_ref[pl.ds(at, LANES), :] = log_sum
+        kept_ref[pl.ds(c, 1), :] = sum(w for pair in pairs for _, _, _, w in pair)
+        return carry
+
+    kept_ref[...] = jnp.zeros_like(kept_ref)
+    lax.fori_loop(0, per, one_channel, 0)
+    crosses = jnp.where(even, live(me, 2, shards), live(me, -1, shards))
+    for first in range(0, per, 2):
+        frames, keeps = [], []
+        for c in range(first, first + 2):
+            at = c * rows
+            head = jnp.where(even, b_ref[at + half : at + rows, :], c_ref[at + half : at + rows, :])
+            tail = jnp.where(even, c_ref[at : at + half, :], a_ref[at : at + half, :])
+            frames.append((head, tail, crosses))
+            keeps.append(jnp.where(even, weight(b_ref, c, 1), weight(c_ref, c, 1)))
+        for i, power in enumerate(powers_of(frames, t_ref, f_ref, w_ref)):
+            c, keep = first + i, keeps[i]
+            at = slice(c * LANES, (c + 1) * LANES)
+            peak_ref[at, :] = jnp.maximum(peak_ref[at, :], keep * power)
+            log_ref[at, :] = log_ref[at, :] + keep * jnp.log(0.25 + power)
+            kept_ref[c : c + 1, :] = kept_ref[c : c + 1, :] + keep
+
+
+def chunks_kernel(per, shards, *refs):
+    a_ref, b_ref, h_ref, t_ref, peak_ref, log_ref, kept_ref, f_ref, w_ref, keep_ref, send_ref = refs
+    me = lax.axis_index("tm")
+    even = lax.rem(me, 2) == 0
     role = lax.rem(me // GROUP + lax.rem(me, GROUP), 2)
-    rows = (o_ref.shape[0] - 8) // per
+    rows = (a_ref.shape[0] - 8) // per
     half = rows // 2
     dests = shards // 2
     parts = LB // shards
     lines = 2 * parts * per
-    starts_a = jnp.where(me == 1, 0.0, 1.0)
-    starts_o = jnp.where(me == 0, 0.0, 1.0)
-    starts_b = jnp.where(me == shards - 1, 0.0, 1.0)
-    starts_y = jnp.where(me == shards - 2, 0.0, 1.0)
+    crosses = jnp.where(even, live(me, -1, shards), live(me, 2, shards))
     lane = lax.broadcasted_iota(jnp.int32, (1, LANES), 1)
-    swap = (lax.broadcasted_iota(jnp.int32, (8, LANES), 0) == 0) & (
-        lax.rem(lax.broadcasted_iota(jnp.int32, (8, LANES), 1), LB // 2) >= LB // 4
-    )
-
-    def one_channel(c, carry):
-        base = pl.multiple_of(c * rows, rows)
-
-        def halves(ref):
-            return ref[pl.ds(base, half), :], ref[pl.ds(base + half, half), :]
-
-        def weight(ref, s, at=per * rows):
-            return ref[pl.ds(at + 2 * c + s, 1), :]
-
-        o0, o1 = halves(o_ref)
-        a0, a1 = halves(a_ref)
-        b0, b1 = halves(b_ref)
-        c0, c1 = halves(c_ref)
-        h = h_ref[pl.ds(pl.multiple_of(c * half, half), half), :]
-        x = jnp.where(even, h, c1)
-        y = jnp.where(even, c0, h)
-        x_weight = jnp.where(even, weight(h_ref, 1, per * half), weight(c_ref, 1))
-        pairs = (
-            ((o0, o1, None, weight(o_ref, 0)), (o1, b0, starts_b, weight(o_ref, 1))),
-            ((a0, a1, None, weight(a_ref, 0)), (a1, o0, starts_o, weight(a_ref, 1))),
-            ((b0, b1, None, weight(b_ref, 0)), (b1, y, starts_y, weight(b_ref, 1))),
-            ((c0, c1, None, weight(c_ref, 0)), (x, a0, starts_a, x_weight)),
-        )
-        window = t_ref[2 * ROWS : 2 * ROWS + LA, :]
-        peak = log_sum = None
-        for pair in pairs:
-            framed = []
-            for head, tail, live, _ in pair:
-                tail = tail * window[half:]
-                if live is not None:
-                    tail = tail * live
-                framed.append(jnp.concatenate([head * window[:half], tail], axis=0))
-            high, low = split(jnp.concatenate(framed, axis=1))
-            mid = jnp.dot(
-                f_ref[...],
-                jnp.concatenate([high, low, high], axis=0),
-                preferred_element_type=jnp.float32,
-            )
-            cosine, sine = t_ref[:ROWS, :], t_ref[ROWS : 2 * ROWS, :]
-            turned = []
-            for s in range(2):
-                re = mid[:ROWS, s * LB : (s + 1) * LB]
-                im = mid[ROWS:, s * LB : (s + 1) * LB]
-                turned.append(
-                    jnp.concatenate([re * cosine - im * sine, re * sine + im * cosine], axis=1)
-                )
-            high, low = split(jnp.concatenate(turned, axis=0))
-            out = jnp.dot(
-                jnp.concatenate([high, low, high], axis=1),
-                w_ref[...],
-                preferred_element_type=jnp.float32,
-            )
-            powers = out[:, :LB] * out[:, :LB] + out[:, LB:] * out[:, LB:]
-            for s in range(2):
-                mine = powers[s * ROWS : (s + 1) * ROWS]
-                first = jnp.where(swap, mine[LA // 2 : LA // 2 + 8], mine[:8])
-                mine = jnp.concatenate([first, mine[8 : LA // 2]], axis=0)
-                keep = pair[s][3]
-                kept_power = keep * mine
-                kept_log = keep * jnp.log(0.25 + mine)
-                peak = kept_power if peak is None else jnp.maximum(peak, kept_power)
-                log_sum = kept_log if log_sum is None else log_sum + kept_log
-        for kind, value in enumerate((peak, log_sum)):
-            turned = jnp.transpose(value)
-            for ref, mine in ((keep_ref, 0), (send_ref, 1)):
-                chosen = jnp.where(role == mine, turned[: LB // 2], turned[LB // 2 :])
-                for i in range(parts):
-                    at = (kind * parts + i) * per + c
-                    ref[pl.ds(at, dests, stride=lines + 1), :] = chosen[
-                        i * dests : (i + 1) * dests
-                    ]
-        kept = sum(w for pair in pairs for _, _, _, w in pair)
-        return jnp.where(lane == c, kept, carry)
-
-    kept = lax.fori_loop(0, per, one_channel, jnp.zeros((1, LANES), jnp.float32))
+    kept = jnp.zeros((1, LANES), jnp.float32)
+    for first in range(0, per, 2):
+        frames, keeps = [], []
+        for c in range(first, first + 2):
+            at = c * rows
+            lent = h_ref[c * half : (c + 1) * half, :]
+            head = jnp.where(even, lent, b_ref[at + half : at + rows, :])
+            tail = jnp.where(even, a_ref[at : at + half, :], lent)
+            frames.append((head, tail, crosses))
+            at = per * half + 2 * c + 1
+            own = per * rows + 2 * c + 1
+            keeps.append(jnp.where(even, h_ref[at : at + 1, :], b_ref[own : own + 1, :]))
+        for i, power in enumerate(powers_of(frames, t_ref, f_ref, w_ref)):
+            c, keep = first + i, keeps[i]
+            at = slice(c * LANES, (c + 1) * LANES)
+            peak = jnp.maximum(peak_ref[at, :], keep * power)
+            log_sum = log_ref[at, :] + keep * jnp.log(0.25 + power)
+            kept = jnp.where(lane == c, kept_ref[c : c + 1, :] + keep, kept)
+            for kind, value in enumerate((peak, log_sum)):
+                turned = jnp.transpose(value)
+                for ref, mine in ((keep_ref, 0), (send_ref, 1)):
+                    chosen = jnp.where(role == mine, turned[: LB // 2], turned[LB // 2 :])
+                    for part in range(parts):
+                        line = (kind * parts + part) * per + c
+                        ref[pl.ds(line, dests, stride=lines + 1), :] = chosen[
+                            part * dests : (part + 1) * dests
+                        ]
     for ref in (keep_ref, send_ref):
         ref[pl.ds(lines, dests, stride=lines + 1), :] = jnp.broadcast_to(kept, (dests, LANES))
 
@@ -293,21 +339,32 @@
 
     dests = shards // 2
     lines = 2 * (bins // LANES) * per + 1
-    keep, send = pl.pallas_call(
+    table = tables(shards)
+    sums = pl.pallas_call(
         functools.partial(spectra_kernel, per, shards),
-        out_shape=[f32(dests * lines, LANES)] * 2,
-        in_specs=[VMEM] * 6,
-        out_specs=[VMEM] * 2,
-        scratch_shapes=[
-            pltpu.VMEM((2 * ROWS, 3 * LA), jnp.bfloat16),
-            pltpu.VMEM((6 * LB, 2 * LB), jnp.bfloat16),
+        out_shape=[
+            f32(per * LANES, LANES),
+            f32(per * LANES, LANES),
+            f32(8, LANES),
+            jax.ShapeDtypeStruct((2 * ROWS, 3 * LA), jnp.bfloat16),
+            jax.ShapeDtypeStruct((6 * LB, 2 * LB), jnp.bfloat16),
         ],
+        in_specs=[VMEM] * 5,
+        out_specs=[VMEM] * 5,
         compiler_params=PARAMS,
         cost_estimate=pl.CostEstimate(
             flops=4_000_000_000, bytes_accessed=4_000_000, transcendentals=300_000
         ),
         name="spectra",
-    )(o, a, b, c, h, tables(shards))
+    )(o, a, b, c, table)
+    keep, send = pl.pallas_call(
+        functools.partial(chunks_kernel, per, shards),
+        out_shape=[f32(dests * lines, LANES)] * 2,
+        in_specs=[VMEM] * 9,
+        out_specs=[VMEM] * 2,
+        compiler_params=PARAMS,
+        name="chunks",
+    )(a, b, h, table, *sums)
     roles = [owners(shards, role) for role in range(2)]
     other = moved(send, lambda i: GROUP if i in roles[0] else -GROUP)
     sums = pl.pallas_call(

time: 130 us -> 129 us (level)
  waiting for transfers between devices: 19.4 us -> 17 us
    ppermute x5, waiting for transfers between devices: 19.4 us -> 17 us  [moved(): lax.ppermute(x, 'tm', [(i, (i + by(i)) % shards) for i in range(shards)])]
  transfers between devices with their start and end apart: 5 -> 5, of which waited for: 2 -> 2; matrix products, arithmetic and copies ran while one was open for 0% -> 0% of each run, Pallas kernels for 0% -> 3%
where the time goes in v5:
time: 129 us; the launch traced here: 127 us
  starting transfers between devices  56 us (43%)
  blocking collectives  45.5 us (35%)
  waiting for transfers between devices  17 us (13%)
  Pallas kernels  6.29 us (5%)
  local copies, waits for them, and re-layouts  1.89 us (1%)
    ppermute x5, starting transfers between devices, moved(): lax.ppermute(x, 'tm', [(i, (i + by(i)) % shards) for i in range(shards)])  56 us
    all_to_all x1, blocking collectives, on_device(): lax.all_to_all(sums.reshape(dests, 1, -1), 'tm', 0, 0, tiled=True, axis_i...  30 us
    ppermute x5, waiting for transfers between devices, moved(): lax.ppermute(x, 'tm', [(i, (i + by(i)) % shards) for i in range(shards)])  17 us
    all_to_all x1, blocking collectives, on_device(): part = lax.all_to_all(part, ('chan', 'sub'), 0, 0, tiled=True)  15.5 us
    pallas_call x1, Pallas kernels, on_device(): pl.pallas_call(functools.partial(spectra_kernel, per, shards), out_shape=...  3.27 us
  transfers between devices with their start and end apart: 5, of which 2 were waited for; matrix products, arithmetic and copies ran while one was open for 0% of the time, Pallas kernels for 3%

profile of v5, /device:TPU:33, one launch (start us, length us, event | category | flops | bytes accessed | tf_op | source)
XLA Modules:
  0.0 127.4 jit_solution(4897506816031703389)
XLA Ops:
  0.6 0.0 copy-start.2
  0.6 0.0 copy-start.3
  0.7 0.7 copy-done.2
  1.3 0.0 copy-done.3
  1.3 0.0 copy-start
  1.3 1.2 copy-done
  2.5 0.0 copy-start.1
  2.5 0.8 pack.1
  3.4 5.3 %collective-permute-start = (f32[520,128]{1,0:T(8,128)S(1)}, f32[520,128]{1,0:T(8,128)S(1)}, u32[]{:S(2)}, u32[]{:S(2)}) collective-permute-start(f32[520,128]{1,0:T(8,128)S(1)} %get-tuple-element.20), channel_id=1, source_target_pairs={{0,8},{8,16},{16,24},{24,32},{32,40},{40,48},{48,56},{56,64},{64,7... | collective-permute-start | bytes 798728 | tf_op jit(solution)/shard_map/ppermute | solution.py:333
  8.6 42.6 %collective-permute-start.1 = (f32[520,128]{1,0:T(8,128)S(1)}, f32[520,128]{1,0:T(8,128)S(1)}, u32[]{:S(2)}, u32[]{:S(2)}) collective-permute-start(f32[520,128]{1,0:T(8,128)S(1)} %get-tuple-element.21), channel_id=1, source_target_pairs={{0,248},{8,0},{16,8},{24,16},{32,24},{40,32},{48,40},{56,48},{64,5... | collective-permute-start | bytes 798728 | tf_op jit(solution)/shard_map/ppermute | solution.py:333
  51.2 3.1 %collective-permute-start.3 = (f32[520,128]{1,0:T(8,128)S(1)}, f32[520,128]{1,0:T(8,128)S(1)}, u32[]{:S(2)}, u32[]{:S(2)}) collective-permute-start(f32[520,128]{1,0:T(8,128)S(1)} %get-tuple-element.24), channel_id=1, source_target_pairs={{0,240},{8,24},{16,0},{24,40},{32,16},{40,56},{48,32},{56,72},{64,... | collective-permute-start | bytes 798728 | tf_op jit(solution)/shard_map/ppermute | solution.py:333
  54.3 3.1 %collective-permute-start.2 = (f32[264,128]{1,0:T(8,128)S(1)}, f32[264,128]{1,0:T(8,128)S(1)}, u32[]{:S(2)}, u32[]{:S(2)}) collective-permute-start(f32[264,128]{1,0:T(8,128)S(1)} %get-tuple-element.22), channel_id=1, source_target_pairs={{0,16},{8,248},{16,32},{24,8},{32,48},{40,24},{48,64},{56,40},{64,... | collective-permute-start | bytes 405512 | tf_op jit(solution)/shard_map/ppermute | solution.py:333
  57.5 0.0 collective-permute-done.refs_1_.refs_0_
  57.5 0.0 collective-permute-done.1.refs_2_.refs_1_
  57.5 5.4 %collective-permute-done.3.refs_3_ = f32[520,128]{1,0:T(8,128)S(1)} collective-permute-done((f32[520,128]{1,0:T(8,128)S(1)}, f32[520,128]{1,0:T(8,128)S(1)}, u32[]{:S(2)}, u32[]{:S(2)}) %collective-permute-start.3) | collective-permute-done | bytes 266272 | tf_op jit(solution)/shard_map/ppermute | solution.py:333
  62.9 0.0 copy-done.1
  62.9 3.3 %spectra.1 = (f32[256,128]{1,0:T(8,128)S(1)}, f32[256,128]{1,0:T(8,128)S(1)}, f32[8,128]{1,0:T(8,128)S(1)}, bf16[288,768]{1,0:T(8,128)(2,1)S(1)}, bf16[768,256]{1,0:T(8,128)(2,1)S(1)}) custom-call(f32[520,128]{1,0:T(8,128)S(1)} %get-tuple-element.23.refs_0_, f32[520,128]{1,0:T(8,128)S(1)} %collective-permute-done.refs_1_.refs_0_, ...), custom_call_target="tpu_custom_call" | custom-call | flops 4000000000 | bytes 4000000 | tf_op jit(solution)/shard_map/spectra/pallas_call | solution.py:343
  66.1 0.0 collective-permute-done.2.refs_2_
  66.2 0.8 chunks.1
  67.0 2.0 %collective-permute-start.4 = (f32[272,128]{1,0:T(8,128)S(1)}, f32[272,128]{1,0:T(8,128)S(1)}, u32[]{:S(2)}, u32[]{:S(2)}) collective-permute-start(f32[272,128]{1,0:T(8,128)S(1)} %get-tuple-element.31), channel_id=1, source_target_pairs={{0,32},{8,232},{16,48},{24,248},{32,0},{40,72},{48,16},{56,88},{64... | collective-permute-start | bytes 417800 | tf_op jit(solution)/shard_map/ppermute | solution.py:333
  68.9 11.6 %collective-permute-done.4.other_ref = f32[272,128]{1,0:T(8,128)S(1)} collective-permute-done((f32[272,128]{1,0:T(8,128)S(1)}, f32[272,128]{1,0:T(8,128)S(1)}, u32[]{:S(2)}, u32[]{:S(2)}) %collective-permute-start.4) | collective-permute-done | bytes 139296 | tf_op jit(solution)/shard_map/ppermute | solution.py:333
  80.5 0.1 join.1
  80.6 30.0 %all_to_all.10 = f32[16,1,2176]{2,1,0:T(1,128)S(1)} all-to-all(f32[16,1,2176]{2,1,0:T(1,128)S(1)} %bitcast.10), channel_id=1, replica_groups={{0,40,16,56,64,104,80,120,128,168,144,184,192,232,208,248},{32,8,48,24,..., dimensions={0} | all-to-all | bytes 278528 | tf_op jit(solution)/shard_map/all_to_all | solution.py:378
  110.6 0.7 finish.1
  111.3 15.5 %all_to_all.11.parts_ref = f32[8,40,128]{2,1,0:T(8,128)S(1)} all-to-all(f32[8,40,128]{2,1,0:T(8,128)S(1)} %get-tuple-element.34), channel_id=1, replica_groups=mesh['grp'=2,'tm'=32,'chan'=4,'sub'=2] {'chan','sub'}, dimensions={0} | all-to-all | bytes 327680 | tf_op jit(solution)/shard_map/all_to_all | solution.py:394
  126.8 0.6 blocks.1
Async XLA Ops:
  0.6 0.7 copy-start.2
  0.6 0.7 copy-start.3
  1.3 1.2 copy-start
  2.5 60.3 %copy-start.1 = (f32[1632,128]{1,0:T(8,128)S(1)}, f32[1632,128]{1,0:T(8,128)}, u32[]{:S(2)}) copy-start(f32[1632,128]{1,0:T(8,128)} %constant.2.clone.refs_4_.refs_3_) | copy-start | bytes 2506756
  3.4 54.1 %collective-permute-start = (f32[520,128]{1,0:T(8,128)S(1)}, f32[520,128]{1,0:T(8,128)S(1)}, u32[]{:S(2)}, u32[]{:S(2)}) collective-permute-start(f32[520,128]{1,0:T(8,128)S(1)} %get-tuple-element.20), channel_id=1, source_target_pairs={{0,8},{8,16},{16,24},{24,32},{32,40},{40,48},{48,56},{56,64},{64,7... | collective-permute-start | bytes 798728 | tf_op jit(solution)/shard_map/ppermute | solution.py:333
  8.6 48.9 %collective-permute-start.1 = (f32[520,128]{1,0:T(8,128)S(1)}, f32[520,128]{1,0:T(8,128)S(1)}, u32[]{:S(2)}, u32[]{:S(2)}) collective-permute-start(f32[520,128]{1,0:T(8,128)S(1)} %get-tuple-element.21), channel_id=1, source_target_pairs={{0,248},{8,0},{16,8},{24,16},{32,24},{40,32},{48,40},{56,48},{64,5... | collective-permute-start | bytes 798728 | tf_op jit(solution)/shard_map/ppermute | solution.py:333
  51.2 11.7 %collective-permute-start.3 = (f32[520,128]{1,0:T(8,128)S(1)}, f32[520,128]{1,0:T(8,128)S(1)}, u32[]{:S(2)}, u32[]{:S(2)}) collective-permute-start(f32[520,128]{1,0:T(8,128)S(1)} %get-tuple-element.24), channel_id=1, source_target_pairs={{0,240},{8,24},{16,0},{24,40},{32,16},{40,56},{48,32},{56,72},{64,... | collective-permute-start | bytes 798728 | tf_op jit(solution)/shard_map/ppermute | solution.py:333
  54.3 11.8 %collective-permute-start.2 = (f32[264,128]{1,0:T(8,128)S(1)}, f32[264,128]{1,0:T(8,128)S(1)}, u32[]{:S(2)}, u32[]{:S(2)}) collective-permute-start(f32[264,128]{1,0:T(8,128)S(1)} %get-tuple-element.22), channel_id=1, source_target_pairs={{0,16},{8,248},{16,32},{24,8},{32,48},{40,24},{48,64},{56,40},{64,... | collective-permute-start | bytes 405512 | tf_op jit(solution)/shard_map/ppermute | solution.py:333
  67.0 13.5 %collective-permute-start.4 = (f32[272,128]{1,0:T(8,128)S(1)}, f32[272,128]{1,0:T(8,128)S(1)}, u32[]{:S(2)}, u32[]{:S(2)}) collective-permute-start(f32[272,128]{1,0:T(8,128)S(1)} %get-tuple-element.31), channel_id=1, source_target_pairs={{0,32},{8,232},{16,48},{24,248},{32,0},{40,72},{48,16},{56,88},{64... | collective-permute-start | bytes 417800 | tf_op jit(solution)/shard_map/ppermute | solution.py:333

commit v6 on v5

--- a/solution.py
+++ b/solution.py
@@ -132,8 +132,29 @@
     return jnp.where(lax.rem(me + ahead + shards, shards) == 0, 0.0, 1.0)
 
 
+def add_segments(c, pairs, tabled, sums_refs, fresh=False):
+    peak_ref, log_ref, kept_ref = sums_refs
+    at = pl.ds(pl.multiple_of(c * LANES, LANES), LANES)
+    row = pl.ds(c, 1)
+    peak, log_sum, kept = None, None, None
+    if not fresh:
+        peak, log_sum, kept = peak_ref[at, :], log_ref[at, :], kept_ref[row, :]
+    for pair in pairs:
+        powers = powers_of([segment[:3] for segment in pair], *tabled)
+        for power, (_, _, _, keep) in zip(powers, pair):
+            kept_log = keep * jnp.log(0.25 + power)
+            peak = keep * power if peak is None else jnp.maximum(peak, keep * power)
+            log_sum = kept_log if log_sum is None else log_sum + kept_log
+            kept = keep if kept is None else kept + keep
+    peak_ref[at, :], log_ref[at, :], kept_ref[row, :] = peak, log_sum, kept
+
+
+def weight(ref, c, s):
+    return ref[pl.ds(ref.shape[0] - 8 + 2 * c + s, 1), :]
+
+
 def spectra_kernel(per, shards, *refs):
-    o_ref, a_ref, b_ref, c_ref, t_ref, peak_ref, log_ref, kept_ref, f_ref, w_ref = refs
+    o_ref, a_ref, c_ref, t_ref, peak_ref, log_ref, kept_ref, f_ref, w_ref = refs
     at = 2 * ROWS + LA
     side = t_ref[at : at + 2 * ROWS, :], t_ref[at + 2 * ROWS : at + 4 * ROWS, :]
     high, low = split(jnp.concatenate(side, axis=1))
@@ -143,42 +164,52 @@
     high, low = split(jnp.concatenate(side, axis=1))
     w_ref[...] = jnp.concatenate([high, high, low], axis=0)
     me = lax.axis_index("tm")
+    rows = (o_ref.shape[0] - 8) // per
+    half = rows // 2
+
+    def one_channel(c, carry):
+        base = pl.multiple_of(c * rows, rows)
+        (o0, o1), (a0, a1), (c0, c1) = (
+            (ref[pl.ds(base, half), :], ref[pl.ds(base + half, half), :])
+            for ref in (o_ref, a_ref, c_ref)
+        )
+        pairs = (
+            ((c0, c1, None, weight(c_ref, c, 0)), (o0, o1, None, weight(o_ref, c, 0))),
+            (
+                (a0, a1, None, weight(a_ref, c, 0)),
+                (a1, o0, live(me, 0, shards), weight(a_ref, c, 1)),
+            ),
+        )
+        add_segments(c, pairs, (t_ref, f_ref, w_ref), (peak_ref, log_ref, kept_ref), fresh=True)
+        return carry
+
+    kept_ref[...] = jnp.zeros_like(kept_ref)
+    lax.fori_loop(0, per, one_channel, 0)
+
+
+def more_kernel(per, shards, *refs):
+    o_ref, a_ref, b_ref, c_ref, t_ref, *old_refs, f_ref, w_ref, peak_ref, log_ref, kept_ref = refs
+    sums_refs = peak_ref, log_ref, kept_ref
+    for old, new in zip(old_refs, sums_refs):
+        new[...] = old[...]
+    me = lax.axis_index("tm")
     even = lax.rem(me, 2) == 0
     rows = (o_ref.shape[0] - 8) // per
     half = rows // 2
 
-    def weight(ref, c, s):
-        return ref[pl.ds(per * rows + 2 * c + s, 1), :]
-
     def one_channel(c, carry):
         base = pl.multiple_of(c * rows, rows)
-
-        def halves(ref):
-            return ref[pl.ds(base, half), :], ref[pl.ds(base + half, half), :]
-
-        o0, o1 = halves(o_ref)
-        a0, a1 = halves(a_ref)
-        b0, b1 = halves(b_ref)
-        c0, c1 = halves(c_ref)
+        o1 = o_ref[pl.ds(base + half, half), :]
+        b0, b1 = b_ref[pl.ds(base, half), :], b_ref[pl.ds(base + half, half), :]
         pairs = (
-            ((c0, c1, None, weight(c_ref, c, 0)), (o0, o1, None, weight(o_ref, c, 0))),
-            ((a0, a1, None, weight(a_ref, c, 0)), (a1, o0, live(me, 0, shards), weight(a_ref, c, 1))),
-            ((o1, b0, live(me, 1, shards), weight(o_ref, c, 1)), (b0, b1, None, weight(b_ref, c, 0))),
+            (
+                (o1, b0, live(me, 1, shards), weight(o_ref, c, 1)),
+                (b0, b1, None, weight(b_ref, c, 0)),
+            ),
         )
-        peak = log_sum = None
-        for pair in pairs:
-            powers = powers_of([segment[:3] for segment in pair], t_ref, f_ref, w_ref)
-            for power, (_, _, _, keep) in zip(powers, pair):
-                kept_log = keep * jnp.log(0.25 + power)
-                peak = keep * power if peak is None else jnp.maximum(peak, keep * power)
-                log_sum = kept_log if log_sum is None else log_sum + kept_log
-        at = pl.multiple_of(c * LANES, LANES)
-        peak_ref[pl.ds(at, LANES), :] = peak
-        log_ref[pl.ds(at, LANES), :] = log_sum
-        kept_ref[pl.ds(c, 1), :] = sum(w for pair in pairs for _, _, _, w in pair)
+        add_segments(c, pairs, (t_ref, f_ref, w_ref), sums_refs)
         return carry
 
-    kept_ref[...] = jnp.zeros_like(kept_ref)
     lax.fori_loop(0, per, one_channel, 0)
     crosses = jnp.where(even, live(me, 2, shards), live(me, -1, shards))
     for first in range(0, per, 2):
@@ -340,23 +371,30 @@
     dests = shards // 2
     lines = 2 * (bins // LANES) * per + 1
     table = tables(shards)
-    sums = pl.pallas_call(
+    cost = pl.CostEstimate(flops=2_000_000_000, bytes_accessed=2_000_000, transcendentals=150_000)
+    sums_shape = [f32(per * LANES, LANES), f32(per * LANES, LANES), f32(8, LANES)]
+    *sums, left, right = pl.pallas_call(
         functools.partial(spectra_kernel, per, shards),
         out_shape=[
-            f32(per * LANES, LANES),
-            f32(per * LANES, LANES),
-            f32(8, LANES),
+            *sums_shape,
             jax.ShapeDtypeStruct((2 * ROWS, 3 * LA), jnp.bfloat16),
             jax.ShapeDtypeStruct((6 * LB, 2 * LB), jnp.bfloat16),
         ],
-        in_specs=[VMEM] * 5,
+        in_specs=[VMEM] * 4,
         out_specs=[VMEM] * 5,
         compiler_params=PARAMS,
-        cost_estimate=pl.CostEstimate(
-            flops=4_000_000_000, bytes_accessed=4_000_000, transcendentals=300_000
-        ),
+        cost_estimate=cost,
         name="spectra",
-    )(o, a, b, c, table)
+    )(o, a, c, table)
+    sums = pl.pallas_call(
+        functools.partial(more_kernel, per, shards),
+        out_shape=sums_shape,
+        in_specs=[VMEM] * 10,
+        out_specs=[VMEM] * 3,
+        compiler_params=PARAMS,
+        cost_estimate=cost,
+        name="more",
+    )(o, a, b, c, table, *sums, left, right)
     keep, send = pl.pallas_call(
         functools.partial(chunks_kernel, per, shards),
         out_shape=[f32(dests * lines, LANES)] * 2,
@@ -364,7 +402,7 @@
         out_specs=[VMEM] * 2,
         compiler_params=PARAMS,
         name="chunks",
-    )(a, b, h, table, *sums)
+    )(a, b, h, table, *sums, left, right)
     roles = [owners(shards, role) for role in range(2)]
     other = moved(send, lambda i: GROUP if i in roles[0] else -GROUP)
     sums = pl.pallas_call(

time: 129 us -> 129 us (level)
    pallas_call x0 -> x1, Pallas kernels: none -> 2.17 us  [on_device(): pl.pallas_call(functools.partial(more_kernel, per, shards), out_shape=sum...]
    all_to_all x1, blocking collectives: 30 us -> 31.5 us  [on_device(): lax.all_to_all(sums.reshape(dests, 1, -1), 'tm', 0, 0, tiled=True, axis_i...]
  transfers between devices with their start and end apart: 5 -> 5, of which waited for: 2 -> 3; matrix products, arithmetic and copies ran while one was open for 0% -> 0% of each run, Pallas kernels for 3% -> 3%
where the time goes in v6:
time: 129 us; the launch traced here: 128 us
  starting transfers between devices  54.8 us (42%)
  blocking collectives  45.8 us (36%)
  waiting for transfers between devices  17.7 us (14%)
  Pallas kernels  7.23 us (6%)
  local copies, waits for them, and re-layouts  1.89 us (1%)
    ppermute x5, starting transfers between devices, moved(): lax.ppermute(x, 'tm', [(i, (i + by(i)) % shards) for i in range(shards)])  54.8 us
    all_to_all x1, blocking collectives, on_device(): lax.all_to_all(sums.reshape(dests, 1, -1), 'tm', 0, 0, tiled=True, axis_i...  31.5 us
    ppermute x5, waiting for transfers between devices, moved(): lax.ppermute(x, 'tm', [(i, (i + by(i)) % shards) for i in range(shards)])  17.7 us
    all_to_all x1, blocking collectives, on_device(): part = lax.all_to_all(part, ('chan', 'sub'), 0, 0, tiled=True)  14.3 us
  transfers between devices with their start and end apart: 5, of which 3 were waited for; matrix products, arithmetic and copies ran while one was open for 0% of the time, Pallas kernels for 3%

profile of v6, /device:TPU:33, one launch (start us, length us, event | category | flops | bytes accessed | tf_op | source)
XLA Modules:
  0.0 128.2 jit_solution(11374997207902449985)
XLA Ops:
  0.6 0.0 copy-start.2
  0.6 0.0 copy-start.3
  0.7 0.7 copy-done.2
  1.3 0.0 copy-done.3
  1.3 0.0 copy-start
  1.3 1.2 copy-done
  2.5 0.0 copy-start.1
  2.5 0.8 pack.1
  3.4 5.3 %collective-permute-start = (f32[520,128]{1,0:T(8,128)S(1)}, f32[520,128]{1,0:T(8,128)S(1)}, u32[]{:S(2)}, u32[]{:S(2)}) collective-permute-start(f32[520,128]{1,0:T(8,128)S(1)} %get-tuple-element.23), channel_id=1, source_target_pairs={{0,8},{8,16},{16,24},{24,32},{32,40},{40,48},{48,56},{56,64},{64,7... | collective-permute-start | bytes 798728 | tf_op jit(solution)/shard_map/ppermute | solution.py:364
  8.6 43.7 %collective-permute-start.3 = (f32[520,128]{1,0:T(8,128)S(1)}, f32[520,128]{1,0:T(8,128)S(1)}, u32[]{:S(2)}, u32[]{:S(2)}) collective-permute-start(f32[520,128]{1,0:T(8,128)S(1)} %get-tuple-element.27), channel_id=1, source_target_pairs={{0,240},{8,24},{16,0},{24,40},{32,16},{40,56},{48,32},{56,72},{64,... | collective-permute-start | bytes 798728 | tf_op jit(solution)/shard_map/ppermute | solution.py:364
  52.4 2.0 %collective-permute-start.1 = (f32[520,128]{1,0:T(8,128)S(1)}, f32[520,128]{1,0:T(8,128)S(1)}, u32[]{:S(2)}, u32[]{:S(2)}) collective-permute-start(f32[520,128]{1,0:T(8,128)S(1)} %get-tuple-element.24), channel_id=1, source_target_pairs={{0,248},{8,0},{16,8},{24,16},{32,24},{40,32},{48,40},{56,48},{64,5... | collective-permute-start | bytes 798728 | tf_op jit(solution)/shard_map/ppermute | solution.py:364
  54.3 2.0 %collective-permute-start.2 = (f32[264,128]{1,0:T(8,128)S(1)}, f32[264,128]{1,0:T(8,128)S(1)}, u32[]{:S(2)}, u32[]{:S(2)}) collective-permute-start(f32[264,128]{1,0:T(8,128)S(1)} %get-tuple-element.25), channel_id=1, source_target_pairs={{0,16},{8,248},{16,32},{24,8},{32,48},{40,24},{48,64},{56,40},{64,... | collective-permute-start | bytes 405512 | tf_op jit(solution)/shard_map/ppermute | solution.py:364
  56.3 0.0 collective-permute-done.refs_1_.refs_0_
  56.3 1.0 collective-permute-done.3.refs_2_.refs_3_
  57.3 0.0 copy-done.1
  57.3 2.0 %spectra.1 = (f32[256,128]{1,0:T(8,128)S(1)}, f32[256,128]{1,0:T(8,128)S(1)}, f32[8,128]{1,0:T(8,128)S(1)}, bf16[288,768]{1,0:T(8,128)(2,1)S(1)}, bf16[768,256]{1,0:T(8,128)(2,1)S(1)}) custom-call(f32[520,128]{1,0:T(8,128)S(1)} %get-tuple-element.26.refs_0_, f32[520,128]{1,0:T(8,128)S(1)} %collective-permute-done.refs_1_.refs_0_, ...), custom_call_target="tpu_custom_call" | custom-call | flops 2000000000 | bytes 2000000 | tf_op jit(solution)/shard_map/spectra/pallas_call | solution.py:376
  59.3 6.4 %collective-permute-done.1.refs_2_.refs_1_ = f32[520,128]{1,0:T(8,128)S(1)} collective-permute-done((f32[520,128]{1,0:T(8,128)S(1)}, f32[520,128]{1,0:T(8,128)S(1)}, u32[]{:S(2)}, u32[]{:S(2)}) %collective-permute-start.1) | collective-permute-done | bytes 266272 | tf_op jit(solution)/shard_map/ppermute | solution.py:364
  65.7 2.2 %more.1 = (f32[256,128]{1,0:T(8,128)S(1)}, f32[256,128]{1,0:T(8,128)S(1)}, f32[8,128]{1,0:T(8,128)S(1)}) custom-call(f32[520,128]{1,0:T(8,128)S(1)} %get-tuple-element.26.refs_0_, f32[520,128]{1,0:T(8,128)S(1)} %collective-permute-done.refs_1_.refs_0_, f32[520,128]{1,0:T(8,128)S(1)} %collective-permute-done.1.refs_2_.refs_1_, ...), custom_call_target="tpu_custom_call" | custom-call | flops 2000000000 | bytes 2000000 | tf_op jit(solution)/shard_map/more/pallas_call | solution.py:389
  67.9 0.0 collective-permute-done.2.refs_2_
  67.9 0.8 chunks.1
  68.7 2.0 %collective-permute-start.4 = (f32[272,128]{1,0:T(8,128)S(1)}, f32[272,128]{1,0:T(8,128)S(1)}, u32[]{:S(2)}, u32[]{:S(2)}) collective-permute-start(f32[272,128]{1,0:T(8,128)S(1)} %get-tuple-element.37), channel_id=1, source_target_pairs={{0,32},{8,232},{16,48},{24,248},{32,0},{40,72},{48,16},{56,88},{64... | collective-permute-start | bytes 417800 | tf_op jit(solution)/shard_map/ppermute | solution.py:364
  70.7 10.3 %collective-permute-done.4.other_ref = f32[272,128]{1,0:T(8,128)S(1)} collective-permute-done((f32[272,128]{1,0:T(8,128)S(1)}, f32[272,128]{1,0:T(8,128)S(1)}, u32[]{:S(2)}, u32[]{:S(2)}) %collective-permute-start.4) | collective-permute-done | bytes 139296 | tf_op jit(solution)/shard_map/ppermute | solution.py:364
  81.0 0.1 join.1
  81.1 31.5 %all_to_all.10 = f32[16,1,2176]{2,1,0:T(1,128)S(1)} all-to-all(f32[16,1,2176]{2,1,0:T(1,128)S(1)} %bitcast.10), channel_id=1, replica_groups={{0,40,16,56,64,104,80,120,128,168,144,184,192,232,208,248},{32,8,48,24,..., dimensions={0} | all-to-all | bytes 278528 | tf_op jit(solution)/shard_map/all_to_all | solution.py:416
  112.6 0.7 finish.1
  113.3 14.3 %all_to_all.11.parts_ref = f32[8,40,128]{2,1,0:T(8,128)S(1)} all-to-all(f32[8,40,128]{2,1,0:T(8,128)S(1)} %get-tuple-element.40), channel_id=1, replica_groups=mesh['grp'=2,'tm'=32,'chan'=4,'sub'=2] {'chan','sub'}, dimensions={0} | all-to-all | bytes 327680 | tf_op jit(solution)/shard_map/all_to_all | solution.py:432
  127.6 0.6 blocks.1
Async XLA Ops:
  0.6 0.7 copy-start.2
  0.6 0.7 copy-start.3
  1.3 1.2 copy-start
  2.5 54.7 %copy-start.1 = (f32[1632,128]{1,0:T(8,128)S(1)}, f32[1632,128]{1,0:T(8,128)}, u32[]{:S(2)}) copy-start(f32[1632,128]{1,0:T(8,128)} %constant.2.clone.refs_3_.refs_4_) | copy-start | bytes 2506756
  3.4 52.9 %collective-permute-start = (f32[520,128]{1,0:T(8,128)S(1)}, f32[520,128]{1,0:T(8,128)S(1)}, u32[]{:S(2)}, u32[]{:S(2)}) collective-permute-start(f32[520,128]{1,0:T(8,128)S(1)} %get-tuple-element.23), channel_id=1, source_target_pairs={{0,8},{8,16},{16,24},{24,32},{32,40},{40,48},{48,56},{56,64},{64,7... | collective-permute-start | bytes 798728 | tf_op jit(solution)/shard_map/ppermute | solution.py:364
  8.6 48.6 %collective-permute-start.3 = (f32[520,128]{1,0:T(8,128)S(1)}, f32[520,128]{1,0:T(8,128)S(1)}, u32[]{:S(2)}, u32[]{:S(2)}) collective-permute-start(f32[520,128]{1,0:T(8,128)S(1)} %get-tuple-element.27), channel_id=1, source_target_pairs={{0,240},{8,24},{16,0},{24,40},{32,16},{40,56},{48,32},{56,72},{64,... | collective-permute-start | bytes 798728 | tf_op jit(solution)/shard_map/ppermute | solution.py:364
  52.4 13.3 %collective-permute-start.1 = (f32[520,128]{1,0:T(8,128)S(1)}, f32[520,128]{1,0:T(8,128)S(1)}, u32[]{:S(2)}, u32[]{:S(2)}) collective-permute-start(f32[520,128]{1,0:T(8,128)S(1)} %get-tuple-element.24), channel_id=1, source_target_pairs={{0,248},{8,0},{16,8},{24,16},{32,24},{40,32},{48,40},{56,48},{64,5... | collective-permute-start | bytes 798728 | tf_op jit(solution)/shard_map/ppermute | solution.py:364
  54.3 13.6 %collective-permute-start.2 = (f32[264,128]{1,0:T(8,128)S(1)}, f32[264,128]{1,0:T(8,128)S(1)}, u32[]{:S(2)}, u32[]{:S(2)}) collective-permute-start(f32[264,128]{1,0:T(8,128)S(1)} %get-tuple-element.25), channel_id=1, source_target_pairs={{0,16},{8,248},{16,32},{24,8},{32,48},{40,24},{48,64},{56,40},{64,... | collective-permute-start | bytes 405512 | tf_op jit(solution)/shard_map/ppermute | solution.py:364
  68.7 12.3 %collective-permute-start.4 = (f32[272,128]{1,0:T(8,128)S(1)}, f32[272,128]{1,0:T(8,128)S(1)}, u32[]{:S(2)}, u32[]{:S(2)}) collective-permute-start(f32[272,128]{1,0:T(8,128)S(1)} %get-tuple-element.37), channel_id=1, source_target_pairs={{0,32},{8,232},{16,48},{24,248},{32,0},{40,72},{48,16},{56,88},{64... | collective-permute-start | bytes 417800 | tf_op jit(solution)/shard_map/ppermute | solution.py:364

commit v7 on v5

--- a/solution.py
+++ b/solution.py
@@ -284,22 +284,40 @@
     peak_ref[...] = in_order(0, jnp.maximum)
     block = lax.broadcasted_iota(jnp.int32, (BLOCKS, LANES), 0).astype(jnp.float32)
     inside = [block == ids_ref[c : c + 1, :] for c in range(channels)]
-    for i in range(parts + 1):
+    step = parts * BLOCKS + 1
+    peers = part_ref.shape[0] // step
+    for i in range(parts):
         total = jnp.zeros((BLOCKS, LANES), jnp.float32)
         for c in range(channels):
-            term = log_mean[c : c + 1, i * LANES : (i + 1) * LANES] if i < parts else 1.0
+            term = log_mean[c : c + 1, i * LANES : (i + 1) * LANES]
             total = total + jnp.where(inside[c], term, 0.0)
-        for p in range(part_ref.shape[0]):
-            part_ref[p, i * BLOCKS : (i + 1) * BLOCKS, :] = total
+        for p in range(peers):
+            at = p * step + i * BLOCKS
+            part_ref[at : at + BLOCKS, :] = total
+    matches = jnp.where(ids_ref[...] == lane.astype(jnp.float32), 1.0, 0.0)
+    counts = jnp.sum(matches, axis=0, keepdims=True)
+    for p in range(peers):
+        at = p * step + parts * BLOCKS
+        part_ref[at : at + 1, :] = counts
 
 
 def blocks_kernel(parts_ref, out_ref):
-    total = parts_ref[0]
-    for p in range(1, parts_ref.shape[0]):
-        total = total + parts_ref[p]
-    counts = total[-BLOCKS:]
-    for i in range(out_ref.shape[1] // LANES):
-        out_ref[:, i * LANES : (i + 1) * LANES] = total[i * BLOCKS : (i + 1) * BLOCKS] / counts
+    parts = out_ref.shape[1] // LANES
+    step = parts * BLOCKS + 1
+    peers = parts_ref.shape[0] // step
+
+    def total(at, count):
+        value = parts_ref[at : at + count, :]
+        for p in range(1, peers):
+            value = value + parts_ref[p * step + at : p * step + at + count, :]
+        return value
+
+    lane = lax.broadcasted_iota(jnp.int32, (BLOCKS, LANES), 1)
+    block = lax.broadcasted_iota(jnp.int32, (BLOCKS, LANES), 0)
+    row = total(parts * BLOCKS, 1)
+    counts = jnp.sum(jnp.where(lane == block, row, 0.0), axis=1, keepdims=True)
+    for i in range(parts):
+        out_ref[:, i * LANES : (i + 1) * LANES] = total(i * BLOCKS, BLOCKS) / counts
 
 
 VMEM = pl.BlockSpec(memory_space=pltpu.VMEM)
@@ -384,14 +402,14 @@
         out_shape=[
             f32(channels, bins),
             f32(channels, bins),
-            f32(peers, (bins // LANES + 1) * BLOCKS, LANES),
+            f32(peers * (bins // LANES * BLOCKS + 1), LANES),
         ],
         in_specs=[VMEM] * 2,
         out_specs=[VMEM] * 3,
         compiler_params=PARAMS,
         name="finish",
     )(ids, sums.reshape(-1, LANES))
-    part = lax.all_to_all(part, ("chan", "sub"), 0, 0, tiled=True)
+    part = lax.all_to_all(part.reshape(peers, 1, -1), ("chan", "sub"), 0, 0, tiled=True)
     block_mean = pl.pallas_call(
         blocks_kernel,
         out_shape=f32(BLOCKS, bins),
@@ -399,7 +417,7 @@
         out_specs=VMEM,
         compiler_params=PARAMS,
         name="blocks",
-    )(part)
+    )(part.reshape(-1, LANES))
     return peak_hold, log_mean, block_mean
 
 

time: 129 us -> 129 us (level)
  no operation moved by 1% of the time
where the time goes in v7:
time: 129 us; the launch traced here: 127 us
  starting transfers between devices  56 us (43%)
  blocking collectives  45.3 us (35%)
  waiting for transfers between devices  17 us (13%)
  Pallas kernels  6.36 us (5%)
  local copies, waits for them, and re-layouts  1.89 us (1%)
    ppermute x5, starting transfers between devices, moved(): lax.ppermute(x, 'tm', [(i, (i + by(i)) % shards) for i in range(shards)])  56 us
    all_to_all x1, blocking collectives, on_device(): lax.all_to_all(sums.reshape(dests, 1, -1), 'tm', 0, 0, tiled=True, axis_i...  30 us
    ppermute x5, waiting for transfers between devices, moved(): lax.ppermute(x, 'tm', [(i, (i + by(i)) % shards) for i in range(shards)])  17 us
    all_to_all x1, blocking collectives, on_device(): lax.all_to_all(part.reshape(peers, 1, -1), ('chan', 'sub'), 0, 0, tiled=T...  15.3 us
    pallas_call x1, Pallas kernels, on_device(): pl.pallas_call(functools.partial(spectra_kernel, per, shards), out_shape=...  3.27 us
  transfers between devices with their start and end apart: 5, of which 2 were waited for; matrix products, arithmetic and copies ran while one was open for 0% of the time, Pallas kernels for 3%

profile of v7, /device:TPU:33, one launch (start us, length us, event | category | flops | bytes accessed | tf_op | source)
XLA Modules:
  0.0 127.3 jit_solution(4042151016085747313)
XLA Ops:
  0.6 0.0 copy-start.2
  0.6 0.0 copy-start.3
  0.7 0.7 copy-done.2
  1.3 0.0 copy-done.3
  1.3 0.0 copy-start
  1.3 1.2 copy-done
  2.5 0.0 copy-start.1
  2.5 0.8 pack.1
  3.4 5.3 %collective-permute-start = (f32[520,128]{1,0:T(8,128)S(1)}, f32[520,128]{1,0:T(8,128)S(1)}, u32[]{:S(2)}, u32[]{:S(2)}) collective-permute-start(f32[520,128]{1,0:T(8,128)S(1)} %get-tuple-element.20), channel_id=1, source_target_pairs={{0,8},{8,16},{16,24},{24,32},{32,40},{40,48},{48,56},{56,64},{64,7... | collective-permute-start | bytes 798728 | tf_op jit(solution)/shard_map/ppermute | solution.py:351
  8.6 42.6 %collective-permute-start.1 = (f32[520,128]{1,0:T(8,128)S(1)}, f32[520,128]{1,0:T(8,128)S(1)}, u32[]{:S(2)}, u32[]{:S(2)}) collective-permute-start(f32[520,128]{1,0:T(8,128)S(1)} %get-tuple-element.21), channel_id=1, source_target_pairs={{0,248},{8,0},{16,8},{24,16},{32,24},{40,32},{48,40},{56,48},{64,5... | collective-permute-start | bytes 798728 | tf_op jit(solution)/shard_map/ppermute | solution.py:351
  51.2 3.1 %collective-permute-start.3 = (f32[520,128]{1,0:T(8,128)S(1)}, f32[520,128]{1,0:T(8,128)S(1)}, u32[]{:S(2)}, u32[]{:S(2)}) collective-permute-start(f32[520,128]{1,0:T(8,128)S(1)} %get-tuple-element.24), channel_id=1, source_target_pairs={{0,240},{8,24},{16,0},{24,40},{32,16},{40,56},{48,32},{56,72},{64,... | collective-permute-start | bytes 798728 | tf_op jit(solution)/shard_map/ppermute | solution.py:351
  54.3 3.1 %collective-permute-start.2 = (f32[264,128]{1,0:T(8,128)S(1)}, f32[264,128]{1,0:T(8,128)S(1)}, u32[]{:S(2)}, u32[]{:S(2)}) collective-permute-start(f32[264,128]{1,0:T(8,128)S(1)} %get-tuple-element.22), channel_id=1, source_target_pairs={{0,16},{8,248},{16,32},{24,8},{32,48},{40,24},{48,64},{56,40},{64,... | collective-permute-start | bytes 405512 | tf_op jit(solution)/shard_map/ppermute | solution.py:351
  57.5 0.0 collective-permute-done.refs_1_.refs_0_
  57.5 0.0 collective-permute-done.1.refs_2_.refs_1_
  57.5 5.4 %collective-permute-done.3.refs_3_ = f32[520,128]{1,0:T(8,128)S(1)} collective-permute-done((f32[520,128]{1,0:T(8,128)S(1)}, f32[520,128]{1,0:T(8,128)S(1)}, u32[]{:S(2)}, u32[]{:S(2)}) %collective-permute-start.3) | collective-permute-done | bytes 266272 | tf_op jit(solution)/shard_map/ppermute | solution.py:351
  62.9 0.0 copy-done.1
  62.9 3.3 %spectra.1 = (f32[256,128]{1,0:T(8,128)S(1)}, f32[256,128]{1,0:T(8,128)S(1)}, f32[8,128]{1,0:T(8,128)S(1)}, bf16[288,768]{1,0:T(8,128)(2,1)S(1)}, bf16[768,256]{1,0:T(8,128)(2,1)S(1)}) custom-call(f32[520,128]{1,0:T(8,128)S(1)} %get-tuple-element.23.refs_0_, f32[520,128]{1,0:T(8,128)S(1)} %collective-permute-done.refs_1_.refs_0_, ...), custom_call_target="tpu_custom_call" | custom-call | flops 4000000000 | bytes 4000000 | tf_op jit(solution)/shard_map/spectra/pallas_call | solution.py:361
  66.1 0.0 collective-permute-done.2.refs_2_
  66.2 0.8 chunks.1
  67.0 2.0 %collective-permute-start.4 = (f32[272,128]{1,0:T(8,128)S(1)}, f32[272,128]{1,0:T(8,128)S(1)}, u32[]{:S(2)}, u32[]{:S(2)}) collective-permute-start(f32[272,128]{1,0:T(8,128)S(1)} %get-tuple-element.31), channel_id=1, source_target_pairs={{0,32},{8,232},{16,48},{24,248},{32,0},{40,72},{48,16},{56,88},{64... | collective-permute-start | bytes 417800 | tf_op jit(solution)/shard_map/ppermute | solution.py:351
  68.9 11.6 %collective-permute-done.4.other_ref = f32[272,128]{1,0:T(8,128)S(1)} collective-permute-done((f32[272,128]{1,0:T(8,128)S(1)}, f32[272,128]{1,0:T(8,128)S(1)}, u32[]{:S(2)}, u32[]{:S(2)}) %collective-permute-start.4) | collective-permute-done | bytes 139296 | tf_op jit(solution)/shard_map/ppermute | solution.py:351
  80.5 0.1 join.1
  80.6 30.0 %all_to_all.10 = f32[16,1,2176]{2,1,0:T(1,128)S(1)} all-to-all(f32[16,1,2176]{2,1,0:T(1,128)S(1)} %bitcast.12), channel_id=1, replica_groups={{0,40,16,56,64,104,80,120,128,168,144,184,192,232,208,248},{32,8,48,24,..., dimensions={0} | all-to-all | bytes 278528 | tf_op jit(solution)/shard_map/all_to_all | solution.py:396
  110.6 0.7 finish.1
  111.3 15.3 %all_to_all.11 = f32[8,1,4224]{2,1,0:T(1,128)S(1)} all-to-all(f32[8,1,4224]{2,1,0:T(1,128)S(1)} %bitcast.14), channel_id=1, replica_groups=mesh['grp'=2,'tm'=32,'chan'=4,'sub'=2] {'chan','sub'}, dimensions={0} | all-to-all | bytes 270336 | tf_op jit(solution)/shard_map/all_to_all | solution.py:412
  126.6 0.7 blocks.1
Async XLA Ops:
  0.6 0.7 copy-start.2
  0.6 0.7 copy-start.3
  1.3 1.2 copy-start
  2.5 60.3 %copy-start.1 = (f32[1632,128]{1,0:T(8,128)S(1)}, f32[1632,128]{1,0:T(8,128)}, u32[]{:S(2)}) copy-start(f32[1632,128]{1,0:T(8,128)} %constant.2.clone.refs_4_.refs_3_) | copy-start | bytes 2506756
  3.4 54.1 %collective-permute-start = (f32[520,128]{1,0:T(8,128)S(1)}, f32[520,128]{1,0:T(8,128)S(1)}, u32[]{:S(2)}, u32[]{:S(2)}) collective-permute-start(f32[520,128]{1,0:T(8,128)S(1)} %get-tuple-element.20), channel_id=1, source_target_pairs={{0,8},{8,16},{16,24},{24,32},{32,40},{40,48},{48,56},{56,64},{64,7... | collective-permute-start | bytes 798728 | tf_op jit(solution)/shard_map/ppermute | solution.py:351
  8.6 48.9 %collective-permute-start.1 = (f32[520,128]{1,0:T(8,128)S(1)}, f32[520,128]{1,0:T(8,128)S(1)}, u32[]{:S(2)}, u32[]{:S(2)}) collective-permute-start(f32[520,128]{1,0:T(8,128)S(1)} %get-tuple-element.21), channel_id=1, source_target_pairs={{0,248},{8,0},{16,8},{24,16},{32,24},{40,32},{48,40},{56,48},{64,5... | collective-permute-start | bytes 798728 | tf_op jit(solution)/shard_map/ppermute | solution.py:351
  51.2 11.7 %collective-permute-start.3 = (f32[520,128]{1,0:T(8,128)S(1)}, f32[520,128]{1,0:T(8,128)S(1)}, u32[]{:S(2)}, u32[]{:S(2)}) collective-permute-start(f32[520,128]{1,0:T(8,128)S(1)} %get-tuple-element.24), channel_id=1, source_target_pairs={{0,240},{8,24},{16,0},{24,40},{32,16},{40,56},{48,32},{56,72},{64,... | collective-permute-start | bytes 798728 | tf_op jit(solution)/shard_map/ppermute | solution.py:351
  54.3 11.8 %collective-permute-start.2 = (f32[264,128]{1,0:T(8,128)S(1)}, f32[264,128]{1,0:T(8,128)S(1)}, u32[]{:S(2)}, u32[]{:S(2)}) collective-permute-start(f32[264,128]{1,0:T(8,128)S(1)} %get-tuple-element.22), channel_id=1, source_target_pairs={{0,16},{8,248},{16,32},{24,8},{32,48},{40,24},{48,64},{56,40},{64,... | collective-permute-start | bytes 405512 | tf_op jit(solution)/shard_map/ppermute | solution.py:351
  67.0 13.5 %collective-permute-start.4 = (f32[272,128]{1,0:T(8,128)S(1)}, f32[272,128]{1,0:T(8,128)S(1)}, u32[]{:S(2)}, u32[]{:S(2)}) collective-permute-start(f32[272,128]{1,0:T(8,128)S(1)} %get-tuple-element.31), channel_id=1, source_target_pairs={{0,32},{8,232},{16,48},{24,248},{32,0},{40,72},{48,16},{56,88},{64... | collective-permute-start | bytes 417800 | tf_op jit(solution)/shard_map/ppermute | solution.py:351

commit v8 on v7

--- a/solution.py
+++ b/solution.py
@@ -246,42 +246,46 @@
     out_ref[...] = jnp.where(line < lines // 2, jnp.maximum(mine, other), mine + other)
 
 
-def finish_kernel(per, ids_ref, z_ref, peak_ref, log_ref, part_ref):
+def joined(z_ref, step, r, at, count, op):
+    total = None
+    for s in range(r, z_ref.shape[0] // step, GROUP):
+        term = z_ref[s * step + at : s * step + at + count, :]
+        total = term if total is None else op(total, term)
+    return total
+
+
+def in_order(per, parts, z_ref, kind, op):
+    own = parts // 2
+    size = parts * per
+    lane = lax.broadcasted_iota(jnp.int32, (GROUP * per, LANES), 1)
+    back = jnp.where(lane == 0, 0, LANES - lane)
+    sets = [joined(z_ref, 2 * size + 1, r, kind * size, size, op) for r in range(GROUP)]
+    pieces = []
+    for e in range(own):
+        for i, mirrored in ((e, False), (own + e, True)):
+            piece = jnp.concatenate([t[i * per : (i + 1) * per] for t in sets], axis=0)
+            if mirrored:
+                piece = jnp.take_along_axis(piece, back, axis=1)
+            pieces.append(piece)
+    return jnp.concatenate(pieces, axis=1)
+
+
+def peaks_kernel(per, z_ref, peak_ref):
+    peak_ref[...] = in_order(per, peak_ref.shape[1] // LANES, z_ref, 0, jnp.maximum)
+
+
+def finish_kernel(per, ids_ref, z_ref, log_ref, part_ref):
     channels, bins = log_ref.shape
     parts = bins // LANES
-    own = parts // 2
     size = parts * per
-    step = 2 * size + 1
-    sources = z_ref.shape[0] // step
     lane = lax.broadcasted_iota(jnp.int32, (channels, LANES), 1)
     line = lax.broadcasted_iota(jnp.int32, (channels, LANES), 0)
-    back = jnp.where(lane == 0, 0, LANES - lane)
-
-    def joined(r, at, count, op):
-        total = None
-        for s in range(r, sources, GROUP):
-            term = z_ref[s * step + at : s * step + at + count, :]
-            total = term if total is None else op(total, term)
-        return total
-
-    def in_order(kind, op):
-        sets = [joined(r, kind * size, size, op) for r in range(GROUP)]
-        pieces = []
-        for e in range(own):
-            for i, mirrored in ((e, False), (own + e, True)):
-                piece = jnp.concatenate([t[i * per : (i + 1) * per] for t in sets], axis=0)
-                if mirrored:
-                    piece = jnp.take_along_axis(piece, back, axis=1)
-                pieces.append(piece)
-        return jnp.concatenate(pieces, axis=1)
-
     kept = jnp.zeros((channels, LANES), jnp.float32)
     for r in range(GROUP):
-        row = joined(r, 2 * size, 1, jnp.add)
+        row = joined(z_ref, 2 * size + 1, r, 2 * size, 1, jnp.add)
         kept = jnp.where((line - per * r == lane) & (lane < per), row, kept)
-    log_mean = in_order(1, jnp.add) / jnp.sum(kept, axis=1, keepdims=True)
+    log_mean = in_order(per, parts, z_ref, 1, jnp.add) / jnp.sum(kept, axis=1, keepdims=True)
     log_ref[...] = log_mean
-    peak_ref[...] = in_order(0, jnp.maximum)
     block = lax.broadcasted_iota(jnp.int32, (BLOCKS, LANES), 0).astype(jnp.float32)
     inside = [block == ids_ref[c : c + 1, :] for c in range(channels)]
     step = parts * BLOCKS + 1
@@ -397,19 +401,28 @@
         sums.reshape(dests, 1, -1), "tm", 0, 0, tiled=True, axis_index_groups=roles
     )
     peers = lax.axis_size(("chan", "sub"))
-    peak_hold, log_mean, part = pl.pallas_call(
+    sums = sums.reshape(-1, LANES)
+    log_mean, part = pl.pallas_call(
         functools.partial(finish_kernel, per),
         out_shape=[
-            f32(channels, bins),
             f32(channels, bins),
             f32(peers * (bins // LANES * BLOCKS + 1), LANES),
         ],
         in_specs=[VMEM] * 2,
-        out_specs=[VMEM] * 3,
+        out_specs=[VMEM] * 2,
         compiler_params=PARAMS,
         name="finish",
-    )(ids, sums.reshape(-1, LANES))
+    )(ids, sums)
     part = lax.all_to_all(part.reshape(peers, 1, -1), ("chan", "sub"), 0, 0, tiled=True)
+    peak_hold = pl.pallas_call(
+        functools.partial(peaks_kernel, per),
+        out_shape=f32(channels, bins),
+        in_specs=[VMEM],
+        out_specs=VMEM,
+        compiler_params=PARAMS,
+        cost_estimate=pl.CostEstimate(flops=20_000_000, bytes_accessed=200_000, transcendentals=0),
+        name="peaks",
+    )(sums)
     block_mean = pl.pallas_call(
         blocks_kernel,
         out_shape=f32(BLOCKS, bins),

time: 129 us -> 129 us (level)
  blocking collectives: 45.3 us -> 30 us
  starting transfers between devices: 56 us -> 66.2 us
  waiting for transfers between devices: 17 us -> 21.6 us
    all_to_all x1 -> x0, blocking collectives: 15.3 us -> none  [on_device(): lax.all_to_all(part.reshape(peers, 1, -1), ('chan', 'sub'), 0, 0, tiled=T...]
    all_to_all x0 -> x1, starting transfers between devices: none -> 10.2 us  [on_device(): lax.all_to_all(part.reshape(peers, 1, -1), ('chan', 'sub'), 0, 0, tiled=T...]
    all_to_all x0 -> x1, waiting for transfers between devices: none -> 4.6 us  [on_device(): lax.all_to_all(part.reshape(peers, 1, -1), ('chan', 'sub'), 0, 0, tiled=T...]
  transfers between devices with their start and end apart: 5 -> 6, of which waited for: 2 -> 3; matrix products, arithmetic and copies ran while one was open for 0% -> 0% of each run, Pallas kernels for 3% -> 3%
where the time goes in v8:
time: 129 us; the launch traced here: 128 us
  starting transfers between devices  66.2 us (51%)
  blocking collectives  30 us (23%)
  waiting for transfers between devices  21.6 us (17%)
  Pallas kernels  7.12 us (6%)
  local copies, waits for them, and re-layouts  1.89 us (1%)
    ppermute x5, starting transfers between devices, moved(): lax.ppermute(x, 'tm', [(i, (i + by(i)) % shards) for i in range(shards)])  56 us
    all_to_all x1, blocking collectives, on_device(): lax.all_to_all(sums.reshape(dests, 1, -1), 'tm', 0, 0, tiled=True, axis_i...  30 us
    ppermute x5, waiting for transfers between devices, moved(): lax.ppermute(x, 'tm', [(i, (i + by(i)) % shards) for i in range(shards)])  17 us
    all_to_all x1, starting transfers between devices, on_device(): lax.all_to_all(part.reshape(peers, 1, -1), ('chan', 'sub'), 0, 0, tiled=T...  10.2 us
    all_to_all x1, waiting for transfers between devices, on_device(): lax.all_to_all(part.reshape(peers, 1, -1), ('chan', 'sub'), 0, 0, tiled=T...  4.6 us
    pallas_call x1, Pallas kernels, on_device(): pl.pallas_call(functools.partial(spectra_kernel, per, shards), out_shape=...  3.27 us
  transfers between devices with their start and end apart: 6, of which 3 were waited for; matrix products, arithmetic and copies ran while one was open for 0% of the time, Pallas kernels for 3%

profile of v8, /device:TPU:33, one launch (start us, length us, event | category | flops | bytes accessed | tf_op | source)
XLA Modules:
  0.0 127.5 jit_solution(60512285616665082)
XLA Ops:
  0.6 0.0 copy-start.2
  0.6 0.0 copy-start.3
  0.7 0.7 copy-done.2
  1.3 0.0 copy-done.3
  1.3 0.0 copy-start
  1.3 1.2 copy-done
  2.5 0.0 copy-start.1
  2.5 0.8 pack.1
  3.4 5.3 %collective-permute-start = (f32[520,128]{1,0:T(8,128)S(1)}, f32[520,128]{1,0:T(8,128)S(1)}, u32[]{:S(2)}, u32[]{:S(2)}) collective-permute-start(f32[520,128]{1,0:T(8,128)S(1)} %get-tuple-element.18), channel_id=1, source_target_pairs={{0,8},{8,16},{16,24},{24,32},{32,40},{40,48},{48,56},{56,64},{64,7... | collective-permute-start | bytes 798728 | tf_op jit(solution)/shard_map/ppermute | solution.py:355
  8.6 42.6 %collective-permute-start.1 = (f32[520,128]{1,0:T(8,128)S(1)}, f32[520,128]{1,0:T(8,128)S(1)}, u32[]{:S(2)}, u32[]{:S(2)}) collective-permute-start(f32[520,128]{1,0:T(8,128)S(1)} %get-tuple-element.19), channel_id=1, source_target_pairs={{0,248},{8,0},{16,8},{24,16},{32,24},{40,32},{48,40},{56,48},{64,5... | collective-permute-start | bytes 798728 | tf_op jit(solution)/shard_map/ppermute | solution.py:355
  51.2 3.1 %collective-permute-start.3 = (f32[520,128]{1,0:T(8,128)S(1)}, f32[520,128]{1,0:T(8,128)S(1)}, u32[]{:S(2)}, u32[]{:S(2)}) collective-permute-start(f32[520,128]{1,0:T(8,128)S(1)} %get-tuple-element.22), channel_id=1, source_target_pairs={{0,240},{8,24},{16,0},{24,40},{32,16},{40,56},{48,32},{56,72},{64,... | collective-permute-start | bytes 798728 | tf_op jit(solution)/shard_map/ppermute | solution.py:355
  54.3 3.1 %collective-permute-start.2 = (f32[264,128]{1,0:T(8,128)S(1)}, f32[264,128]{1,0:T(8,128)S(1)}, u32[]{:S(2)}, u32[]{:S(2)}) collective-permute-start(f32[264,128]{1,0:T(8,128)S(1)} %get-tuple-element.20), channel_id=1, source_target_pairs={{0,16},{8,248},{16,32},{24,8},{32,48},{40,24},{48,64},{56,40},{64,... | collective-permute-start | bytes 405512 | tf_op jit(solution)/shard_map/ppermute | solution.py:355
  57.5 0.0 collective-permute-done.refs_1_.refs_0_
  57.5 0.0 collective-permute-done.1.refs_2_.refs_1_
  57.5 5.4 %collective-permute-done.3.refs_3_ = f32[520,128]{1,0:T(8,128)S(1)} collective-permute-done((f32[520,128]{1,0:T(8,128)S(1)}, f32[520,128]{1,0:T(8,128)S(1)}, u32[]{:S(2)}, u32[]{:S(2)}) %collective-permute-start.3) | collective-permute-done | bytes 266272 | tf_op jit(solution)/shard_map/ppermute | solution.py:355
  62.9 0.0 copy-done.1
  62.9 3.3 %spectra.1 = (f32[256,128]{1,0:T(8,128)S(1)}, f32[256,128]{1,0:T(8,128)S(1)}, f32[8,128]{1,0:T(8,128)S(1)}, bf16[288,768]{1,0:T(8,128)(2,1)S(1)}, bf16[768,256]{1,0:T(8,128)(2,1)S(1)}) custom-call(f32[520,128]{1,0:T(8,128)S(1)} %get-tuple-element.21.refs_0_, f32[520,128]{1,0:T(8,128)S(1)} %collective-permute-done.refs_1_.refs_0_, ...), custom_call_target="tpu_custom_call" | custom-call | flops 4000000000 | bytes 4000000 | tf_op jit(solution)/shard_map/spectra/pallas_call | solution.py:365
  66.1 0.0 collective-permute-done.2.refs_2_
  66.2 0.8 chunks.1
  67.0 2.0 %collective-permute-start.4 = (f32[272,128]{1,0:T(8,128)S(1)}, f32[272,128]{1,0:T(8,128)S(1)}, u32[]{:S(2)}, u32[]{:S(2)}) collective-permute-start(f32[272,128]{1,0:T(8,128)S(1)} %get-tuple-element.29), channel_id=1, source_target_pairs={{0,32},{8,232},{16,48},{24,248},{32,0},{40,72},{48,16},{56,88},{64... | collective-permute-start | bytes 417800 | tf_op jit(solution)/shard_map/ppermute | solution.py:355
  68.9 11.6 %collective-permute-done.4.other_ref = f32[272,128]{1,0:T(8,128)S(1)} collective-permute-done((f32[272,128]{1,0:T(8,128)S(1)}, f32[272,128]{1,0:T(8,128)S(1)}, u32[]{:S(2)}, u32[]{:S(2)}) %collective-permute-start.4) | collective-permute-done | bytes 139296 | tf_op jit(solution)/shard_map/ppermute | solution.py:355
  80.5 0.1 join.1
  80.6 30.0 %all_to_all.10 = f32[16,1,2176]{2,1,0:T(1,128)S(1)} all-to-all(f32[16,1,2176]{2,1,0:T(1,128)S(1)} %bitcast.13), channel_id=1, replica_groups={{0,40,16,56,64,104,80,120,128,168,144,184,192,232,208,248},{32,8,48,24,..., dimensions={0} | all-to-all | bytes 278528 | tf_op jit(solution)/shard_map/all_to_all | solution.py:400
  110.6 0.8 finish.1
  111.4 10.2 %all-to-all-start.1 = ((f32[8,1,4224]{2,1,0:T(1,128)}), f32[8,1,4224]{2,1,0:T(1,128)S(1)}, u32[]{:S(2)}, u32[]{:S(2)}) async-start(f32[8,1,4224]{2,1,0:T(1,128)} %bitcast.6), calls=%async_computation.1 | async-start | bytes 270336 | tf_op jit(solution)/shard_map/all_to_all | solution.py:416
  121.6 0.7 peaks.1
  122.2 4.6 %all-to-all-done.1 = f32[8,1,4224]{2,1,0:T(1,128)S(1)} async-done(((f32[8,1,4224]{2,1,0:T(1,128)}), f32[8,1,4224]{2,1,0:T(1,128)S(1)}, u32[]{:S(2)}, u32[]{:S(2)}) %all-to-all-start.1) | async-done | bytes 135200 | tf_op jit(solution)/shard_map/all_to_all | solution.py:416
  126.8 0.7 blocks.1
Async XLA Ops:
  0.6 0.7 copy-start.2
  0.6 0.7 copy-start.3
  1.3 1.2 copy-start
  2.5 60.3 %copy-start.1 = (f32[1632,128]{1,0:T(8,128)S(1)}, f32[1632,128]{1,0:T(8,128)}, u32[]{:S(2)}) copy-start(f32[1632,128]{1,0:T(8,128)} %constant.2.clone.refs_4_.refs_3_) | copy-start | bytes 2506756
  3.4 54.1 %collective-permute-start = (f32[520,128]{1,0:T(8,128)S(1)}, f32[520,128]{1,0:T(8,128)S(1)}, u32[]{:S(2)}, u32[]{:S(2)}) collective-permute-start(f32[520,128]{1,0:T(8,128)S(1)} %get-tuple-element.18), channel_id=1, source_target_pairs={{0,8},{8,16},{16,24},{24,32},{32,40},{40,48},{48,56},{56,64},{64,7... | collective-permute-start | bytes 798728 | tf_op jit(solution)/shard_map/ppermute | solution.py:355
  8.6 48.9 %collective-permute-start.1 = (f32[520,128]{1,0:T(8,128)S(1)}, f32[520,128]{1,0:T(8,128)S(1)}, u32[]{:S(2)}, u32[]{:S(2)}) collective-permute-start(f32[520,128]{1,0:T(8,128)S(1)} %get-tuple-element.19), channel_id=1, source_target_pairs={{0,248},{8,0},{16,8},{24,16},{32,24},{40,32},{48,40},{56,48},{64,5... | collective-permute-start | bytes 798728 | tf_op jit(solution)/shard_map/ppermute | solution.py:355
  51.2 11.7 %collective-permute-start.3 = (f32[520,128]{1,0:T(8,128)S(1)}, f32[520,128]{1,0:T(8,128)S(1)}, u32[]{:S(2)}, u32[]{:S(2)}) collective-permute-start(f32[520,128]{1,0:T(8,128)S(1)} %get-tuple-element.22), channel_id=1, source_target_pairs={{0,240},{8,24},{16,0},{24,40},{32,16},{40,56},{48,32},{56,72},{64,... | collective-permute-start | bytes 798728 | tf_op jit(solution)/shard_map/ppermute | solution.py:355
  54.3 11.8 %collective-permute-start.2 = (f32[264,128]{1,0:T(8,128)S(1)}, f32[264,128]{1,0:T(8,128)S(1)}, u32[]{:S(2)}, u32[]{:S(2)}) collective-permute-start(f32[264,128]{1,0:T(8,128)S(1)} %get-tuple-element.20), channel_id=1, source_target_pairs={{0,16},{8,248},{16,32},{24,8},{32,48},{40,24},{48,64},{56,40},{64,... | collective-permute-start | bytes 405512 | tf_op jit(solution)/shard_map/ppermute | solution.py:355
  67.0 13.5 %collective-permute-start.4 = (f32[272,128]{1,0:T(8,128)S(1)}, f32[272,128]{1,0:T(8,128)S(1)}, u32[]{:S(2)}, u32[]{:S(2)}) collective-permute-start(f32[272,128]{1,0:T(8,128)S(1)} %get-tuple-element.29), channel_id=1, source_target_pairs={{0,32},{8,232},{16,48},{24,248},{32,0},{40,72},{48,16},{56,88},{64... | collective-permute-start | bytes 417800 | tf_op jit(solution)/shard_map/ppermute | solution.py:355
  111.4 15.5 %all-to-all-start.1 = ((f32[8,1,4224]{2,1,0:T(1,128)}), f32[8,1,4224]{2,1,0:T(1,128)S(1)}, u32[]{:S(2)}, u32[]{:S(2)}) async-start(f32[8,1,4224]{2,1,0:T(1,128)} %bitcast.6), calls=%async_computation.1 | async-start | bytes 270336 | tf_op jit(solution)/shard_map/all_to_all | solution.py:416

commit v9 on v7

--- a/solution.py
+++ b/solution.py
@@ -58,14 +58,15 @@
     return np.concatenate([*twiddle, window, *halves], axis=0).astype(np.float32)
 
 
-def pack_kernel(per, mask_ref, assign_ref, x_ref, *refs):
-    o_ref, a_ref, b_ref, c_ref, h_ref, ids_ref = refs
+def pack_kernel(per, far, mask_ref, assign_ref, x_ref, *refs):
+    c_ref = refs[0] if far else None
+    o_ref, a_ref, b_ref, h_ref, ids_ref = (None,) * 5 if far else refs
     me = lax.axis_index("tm")
     channels = GROUP * per
     rows = x_ref.shape[0] // channels
     half = rows // 2
     even = lax.rem(me, 2) == 0
-    for c in range(channels):
+    for c in range(0 if far else channels):
         ids_ref[c : c + 1, :] = jnp.full((1, LANES), assign_ref[c].astype(jnp.float32))
 
     def masks(ref, at, first):
@@ -76,10 +77,14 @@
                 ref[at + 2 * c + s : at + 2 * c + s + 1, :] = jnp.full((1, LANES), value)
 
     for ref, shift in ((c_ref, 2), (a_ref, 1), (b_ref, GROUP - 1), (o_ref, 0)):
+        if (ref is c_ref) != far:
+            continue
         first = per * lax.rem(me + shift, GROUP)
         for c in range(per):
             ref[c * rows : (c + 1) * rows, :] = x_ref[pl.ds(first + c, rows, stride=channels), :]
         masks(ref, per * rows, first)
+    if far:
+        return
     first = per * lax.rem(me + 2, GROUP)
     start = jnp.where(even, half * channels, 0)
     for c in range(per):
@@ -338,18 +343,24 @@
 
     lined = signal.reshape(channels, rows, LANES).transpose(1, 0, 2).reshape(-1, LANES)
     whole, small = per * rows + 8, per * rows // 2 + 8
-    o, a, b, c, h, ids = pl.pallas_call(
-        functools.partial(pack_kernel, per),
-        out_shape=[f32(whole, LANES)] * 4 + [f32(small, LANES), f32(channels, LANES)],
-        in_specs=[SMEM, SMEM, VMEM],
-        out_specs=[VMEM] * 6,
-        compiler_params=PARAMS,
-        name="pack",
-    )(gap_mask.T, assignment, lined)
+
+    def packed(far, shapes):
+        return pl.pallas_call(
+            functools.partial(pack_kernel, per, far),
+            out_shape=shapes,
+            in_specs=[SMEM, SMEM, VMEM],
+            out_specs=[VMEM] * len(shapes),
+            compiler_params=PARAMS,
+            name="pack",
+        )(gap_mask.T, assignment, lined)
 
     def moved(x, by):
         return lax.ppermute(x, "tm", [(i, (i + by(i)) % shards) for i in range(shards)])
 
+    (c,) = packed(True, [f32(whole, LANES)])
+    o, a, b, h, ids = packed(
+        False, [f32(whole, LANES)] * 3 + [f32(small, LANES), f32(channels, LANES)]
+    )
     a = moved(a, lambda i: 1)
     b = moved(b, lambda i: -1)
     c = moved(c, lambda i: 2 if i % 2 else -2)

time: 129 us -> 126 us (0.977)
  blocking collectives: 45.3 us -> 41.8 us
    all_to_all x1, blocking collectives: 15.3 us -> 12.1 us  [on_device(): lax.all_to_all(part.reshape(peers, 1, -1), ('chan', 'sub'), 0, 0, tiled=T...]
  transfers between devices with their start and end apart: 5 -> 5, of which waited for: 2 -> 4; matrix products, arithmetic and copies ran while one was open for 0% -> 0% of each run, Pallas kernels for 3% -> 3%
where the time goes in v9:
time: 126 us; the launch traced here: 124 us
  starting transfers between devices  56 us (44%)
  blocking collectives  41.8 us (33%)
  waiting for transfers between devices  16.6 us (13%)
  Pallas kernels  6.92 us (5%)
  local copies, waits for them, and re-layouts  1.9 us (2%)
    ppermute x5, starting transfers between devices, moved(): lax.ppermute(x, 'tm', [(i, (i + by(i)) % shards) for i in range(shards)])  56 us
    all_to_all x1, blocking collectives, on_device(): lax.all_to_all(sums.reshape(dests, 1, -1), 'tm', 0, 0, tiled=True, axis_i...  29.7 us
    ppermute x5, waiting for transfers between devices, moved(): lax.ppermute(x, 'tm', [(i, (i + by(i)) % shards) for i in range(shards)])  16.6 us
    all_to_all x1, blocking collectives, on_device(): lax.all_to_all(part.reshape(peers, 1, -1), ('chan', 'sub'), 0, 0, tiled=T...  12.1 us
    pallas_call x1, Pallas kernels, on_device(): pl.pallas_call(functools.partial(spectra_kernel, per, shards), out_shape=...  3.25 us
  transfers between devices with their start and end apart: 5, of which 4 were waited for; matrix products, arithmetic and copies ran while one was open for 0% of the time, Pallas kernels for 3%

profile of v9, /device:TPU:33, one launch (start us, length us, event | category | flops | bytes accessed | tf_op | source)
XLA Modules:
  0.0 124.0 jit_solution(1080439644990288373)
XLA Ops:
  0.6 0.0 copy-start.2
  0.6 0.0 copy-start.3
  0.7 0.7 copy-done.2
  1.3 0.0 copy-done.3
  1.3 0.0 copy-start
  1.3 1.2 copy-done
  2.5 0.6 pack.3
  3.2 0.0 copy-start.1
  3.2 45.6 %collective-permute-start.3 = (f32[520,128]{1,0:T(8,128)S(1)}, f32[520,128]{1,0:T(8,128)S(1)}, u32[]{:S(2)}, u32[]{:S(2)}) collective-permute-start(f32[520,128]{1,0:T(8,128)S(1)} %pack.3), channel_id=1, source_target_pairs={{0,240},{8,24},{16,0},{24,40},{32,16},{40,56},{48,32},{56,72},{64,... | collective-permute-start | bytes 798728 | tf_op jit(solution)/shard_map/ppermute | solution.py:358
  48.8 0.8 pack.2
  49.6 2.0 %collective-permute-start = (f32[520,128]{1,0:T(8,128)S(1)}, f32[520,128]{1,0:T(8,128)S(1)}, u32[]{:S(2)}, u32[]{:S(2)}) collective-permute-start(f32[520,128]{1,0:T(8,128)S(1)} %get-tuple-element.19), channel_id=1, source_target_pairs={{0,8},{8,16},{16,24},{24,32},{32,40},{40,48},{48,56},{56,64},{64,7... | collective-permute-start | bytes 798728 | tf_op jit(solution)/shard_map/ppermute | solution.py:358
  51.5 4.6 %collective-permute-start.1 = (f32[520,128]{1,0:T(8,128)S(1)}, f32[520,128]{1,0:T(8,128)S(1)}, u32[]{:S(2)}, u32[]{:S(2)}) collective-permute-start(f32[520,128]{1,0:T(8,128)S(1)} %get-tuple-element.20), channel_id=1, source_target_pairs={{0,248},{8,0},{16,8},{24,16},{32,24},{40,32},{48,40},{56,48},{64,5... | collective-permute-start | bytes 798728 | tf_op jit(solution)/shard_map/ppermute | solution.py:358
  56.1 2.0 %collective-permute-start.2 = (f32[264,128]{1,0:T(8,128)S(1)}, f32[264,128]{1,0:T(8,128)S(1)}, u32[]{:S(2)}, u32[]{:S(2)}) collective-permute-start(f32[264,128]{1,0:T(8,128)S(1)} %get-tuple-element.21), channel_id=1, source_target_pairs={{0,16},{8,248},{16,32},{24,8},{32,48},{40,24},{48,64},{56,40},{64,... | collective-permute-start | bytes 405512 | tf_op jit(solution)/shard_map/ppermute | solution.py:358
  58.1 0.0 collective-permute-done.3.refs_3_
  58.1 3.0 %collective-permute-done.refs_1_.refs_0_ = f32[520,128]{1,0:T(8,128)S(1)} collective-permute-done((f32[520,128]{1,0:T(8,128)S(1)}, f32[520,128]{1,0:T(8,128)S(1)}, u32[]{:S(2)}, u32[]{:S(2)}) %collective-permute-start) | collective-permute-done | bytes 266272 | tf_op jit(solution)/shard_map/ppermute | solution.py:358
  61.1 0.3 collective-permute-done.1.refs_2_.refs_1_
  61.4 0.0 copy-done.1
  61.4 3.3 %spectra.1 = (f32[256,128]{1,0:T(8,128)S(1)}, f32[256,128]{1,0:T(8,128)S(1)}, f32[8,128]{1,0:T(8,128)S(1)}, bf16[288,768]{1,0:T(8,128)(2,1)S(1)}, bf16[768,256]{1,0:T(8,128)(2,1)S(1)}) custom-call(f32[520,128]{1,0:T(8,128)S(1)} %get-tuple-element.22.refs_0_, f32[520,128]{1,0:T(8,128)S(1)} %collective-permute-done.refs_1_.refs_0_, ...), custom_call_target="tpu_custom_call" | custom-call | flops 4000000000 | bytes 4000000 | tf_op jit(solution)/shard_map/spectra/pallas_call | solution.py:372
  64.6 1.3 %collective-permute-done.2.refs_2_ = f32[264,128]{1,0:T(8,128)S(1)} collective-permute-done((f32[264,128]{1,0:T(8,128)S(1)}, f32[264,128]{1,0:T(8,128)S(1)}, u32[]{:S(2)}, u32[]{:S(2)}) %collective-permute-start.2) | collective-permute-done | bytes 135200 | tf_op jit(solution)/shard_map/ppermute | solution.py:358
  65.9 0.8 chunks.1
  66.8 2.0 %collective-permute-start.4 = (f32[272,128]{1,0:T(8,128)S(1)}, f32[272,128]{1,0:T(8,128)S(1)}, u32[]{:S(2)}, u32[]{:S(2)}) collective-permute-start(f32[272,128]{1,0:T(8,128)S(1)} %get-tuple-element.29), channel_id=1, source_target_pairs={{0,32},{8,232},{16,48},{24,248},{32,0},{40,72},{48,16},{56,88},{64... | collective-permute-start | bytes 417800 | tf_op jit(solution)/shard_map/ppermute | solution.py:358
  68.7 12.0 %collective-permute-done.4.other_ref = f32[272,128]{1,0:T(8,128)S(1)} collective-permute-done((f32[272,128]{1,0:T(8,128)S(1)}, f32[272,128]{1,0:T(8,128)S(1)}, u32[]{:S(2)}, u32[]{:S(2)}) %collective-permute-start.4) | collective-permute-done | bytes 139296 | tf_op jit(solution)/shard_map/ppermute | solution.py:358
  80.7 0.1 join.1
  80.8 29.7 %all_to_all.10 = f32[16,1,2176]{2,1,0:T(1,128)S(1)} all-to-all(f32[16,1,2176]{2,1,0:T(1,128)S(1)} %bitcast.13), channel_id=1, replica_groups={{0,40,16,56,64,104,80,120,128,168,144,184,192,232,208,248},{32,8,48,24,..., dimensions={0} | all-to-all | bytes 278528 | tf_op jit(solution)/shard_map/all_to_all | solution.py:407
  110.4 0.7 finish.1
  111.2 12.1 %all_to_all.11 = f32[8,1,4224]{2,1,0:T(1,128)S(1)} all-to-all(f32[8,1,4224]{2,1,0:T(1,128)S(1)} %bitcast.15), channel_id=1, replica_groups=mesh['grp'=2,'tm'=32,'chan'=4,'sub'=2] {'chan','sub'}, dimensions={0} | all-to-all | bytes 270336 | tf_op jit(solution)/shard_map/all_to_all | solution.py:423
  123.3 0.7 blocks.1
Async XLA Ops:
  0.6 0.7 copy-start.2
  0.6 0.7 copy-start.3
  1.3 1.2 copy-start
  3.2 58.2 %copy-start.1 = (f32[1632,128]{1,0:T(8,128)S(1)}, f32[1632,128]{1,0:T(8,128)}, u32[]{:S(2)}) copy-start(f32[1632,128]{1,0:T(8,128)} %constant.2.clone.refs_4_.refs_3_) | copy-start | bytes 2506756
  3.2 54.9 %collective-permute-start.3 = (f32[520,128]{1,0:T(8,128)S(1)}, f32[520,128]{1,0:T(8,128)S(1)}, u32[]{:S(2)}, u32[]{:S(2)}) collective-permute-start(f32[520,128]{1,0:T(8,128)S(1)} %pack.3), channel_id=1, source_target_pairs={{0,240},{8,24},{16,0},{24,40},{32,16},{40,56},{48,32},{56,72},{64,... | collective-permute-start | bytes 798728 | tf_op jit(solution)/shard_map/ppermute | solution.py:358
  49.6 11.5 %collective-permute-start = (f32[520,128]{1,0:T(8,128)S(1)}, f32[520,128]{1,0:T(8,128)S(1)}, u32[]{:S(2)}, u32[]{:S(2)}) collective-permute-start(f32[520,128]{1,0:T(8,128)S(1)} %get-tuple-element.19), channel_id=1, source_target_pairs={{0,8},{8,16},{16,24},{24,32},{32,40},{40,48},{48,56},{56,64},{64,7... | collective-permute-start | bytes 798728 | tf_op jit(solution)/shard_map/ppermute | solution.py:358
  51.5 9.9 %collective-permute-start.1 = (f32[520,128]{1,0:T(8,128)S(1)}, f32[520,128]{1,0:T(8,128)S(1)}, u32[]{:S(2)}, u32[]{:S(2)}) collective-permute-start(f32[520,128]{1,0:T(8,128)S(1)} %get-tuple-element.20), channel_id=1, source_target_pairs={{0,248},{8,0},{16,8},{24,16},{32,24},{40,32},{48,40},{56,48},{64,5... | collective-permute-start | bytes 798728 | tf_op jit(solution)/shard_map/ppermute | solution.py:358
  56.1 9.8 %collective-permute-start.2 = (f32[264,128]{1,0:T(8,128)S(1)}, f32[264,128]{1,0:T(8,128)S(1)}, u32[]{:S(2)}, u32[]{:S(2)}) collective-permute-start(f32[264,128]{1,0:T(8,128)S(1)} %get-tuple-element.21), channel_id=1, source_target_pairs={{0,16},{8,248},{16,32},{24,8},{32,48},{40,24},{48,64},{56,40},{64,... | collective-permute-start | bytes 405512 | tf_op jit(solution)/shard_map/ppermute | solution.py:358
  66.8 14.0 %collective-permute-start.4 = (f32[272,128]{1,0:T(8,128)S(1)}, f32[272,128]{1,0:T(8,128)S(1)}, u32[]{:S(2)}, u32[]{:S(2)}) collective-permute-start(f32[272,128]{1,0:T(8,128)S(1)} %get-tuple-element.29), channel_id=1, source_target_pairs={{0,32},{8,232},{16,48},{24,248},{32,0},{40,72},{48,16},{56,88},{64... | collective-permute-start | bytes 417800 | tf_op jit(solution)/shard_map/ppermute | solution.py:358
